TPU v7x, 32 devices: a whole 2x2x4 slice. The times are simulated.
32 devices in a mesh: sub: 16 (over z, x, core), row: 2 (over y).
Axes of the slice: x: 2, y: 2, z: 4, core: 2. Of those that a mesh axis runs over, the one named last changes fastest.
Arguments:
- factor_blocks: float32 [16, 8, 3, 256, 256], P('sub', 'row'), may hold values from -0.25 to 0.25
- block_inverses: float32 [16, 8, 256, 256], P('sub', 'row'), as said below
- band_offsets: int32 [16, 8, 3], P('sub', 'row'), may hold values from 1 to 4, as said below
- coupling: float32 [16, 2048, 512], P('sub', 'row'), may hold values from -0.125 to 0.125
- interface_block: float32 [16, 4, 128, 512], P('sub', None, 'row'), may hold values from -6 to 6
- tile_ids: int32 [16, 4], replicated, may hold values from 0 to 127, as said below
Outputs:
- schur_tiles: float32 [16, 4, 128, 512], P('sub', None, 'row')
Inputs may be any that keep to these rules, and one draw needn't show every extreme that they name: `band_offsets`: each entry is one of the numbers 1 .. 4, the 3 entries of a block row are distinct and rising. `tile_ids`: A subdomain's 4 numbers are distinct; a number appears in at most two subdomains, and then in neighbouring ones (s and s + 1); every subdomain but the last shares one or two numbers with the next. `block_inverses`: each block is lower triangular with a diagonal between 0.5 and 1.
All inputs are finite; a program needn't handle non-finite values.
Results may differ from a plain program's by a relative error of at most 0.0003.
Values sent between devices are 32-bit elements; how exact they have to be, the bound alone decides.
No kernel may reach another device: no remote copies, remote signals or barrier semaphores. Data moves between devices by JAX's collectives and lax.ppermute only.
A program may use at most 64 MiB of HBM per device.

v0:
```python
import functools

import jax
import jax.numpy as jnp
from jax import lax
from jax.experimental import pallas as pl
from jax.experimental.pallas import tpu as pltpu
from jax.sharding import PartitionSpec as P


F32 = jnp.float32
BF16 = jnp.bfloat16
VMEM_LIMIT = 24 * 1024 * 1024
ALONE = 63 * 1024 * 1024
SLOTS = 2
LAST = 4


def split(x):
    high = x.astype(BF16)
    return high, (x - high.astype(F32)).astype(BF16)


def nt(a, b):
    return lax.dot_general(a, b, (((1,), (1,)), ((), ())), preferred_element_type=F32)


def nn(a, b):
    return lax.dot_general(a, b, (((1,), (0,)), ((), ())), preferred_element_type=F32)


def three(dot, both, high, low):
    rows = both.shape[0] // 2
    wide = dot(both, high)
    return wide[:rows] + (wide[rows:] + dot(both[:rows], low))


def stacked(x):
    return jnp.concatenate(split(x), axis=0)


def substitute(off_ref, f, inverse, kept, acc, begin, finish):
    brows, kband = f.shape[0], f.shape[1]
    for i in range(brows):
        begin(i)
        for band in range(kband):
            source = i - off_ref[band, 0, i]
            if i > 0:

                @pl.when(source >= 0)
                def _():
                    acc[...] -= three(nt, kept[jnp.maximum(source, 0)], *split(f[i, band]))

        x = three(nt, stacked(acc[...]), *split(inverse[i]))
        if i + 1 < brows:
            kept[i] = stacked(x)
        finish(i, x)


def solve_kernel(off_ref, f_hbm, inv_hbm, b_hbm, *rest, first, chunks):
    outs, (f, inverse, b, kept, acc, sems) = rest[: len(chunks)], rest[len(chunks) :]
    brows, _, size, _ = f.shape
    total = sum(chunks)
    copies = []
    for i in range(brows):
        group = [
            pltpu.make_async_copy(inv_hbm.at[0, i], inverse.at[i], sems.at[0, i]),
            pltpu.make_async_copy(
                b_hbm.at[0, pl.ds(i * size, size), pl.ds(first, total)], b.at[i], sems.at[1, i]
            ),
        ]
        if i > 0:
            group.append(pltpu.make_async_copy(f_hbm.at[0, i], f.at[i], sems.at[2, i]))
        for copy in group:
            copy.start()
        copies.append(group)

    def begin(i):
        for copy in copies[i]:
            copy.wait()
        acc[...] = b[i].T

    def finish(i, x):
        start = 0
        for out, n in zip(outs, chunks):
            out[:, i * size : (i + 1) * size] = x[start : start + n]
            start += n

    substitute(off_ref, f, inverse, kept, acc, begin, finish)


def solve(offsets, blocks, inverses, coupling, first, chunks, limit):
    _, brows, kband, size, _ = blocks.shape
    total = sum(chunks)
    hbm = pl.BlockSpec(memory_space=pltpu.HBM)
    return pl.pallas_call(
        functools.partial(solve_kernel, first=first, chunks=chunks),
        in_specs=[pl.BlockSpec(memory_space=pltpu.SMEM), hbm, hbm, hbm],
        out_shape=[jax.ShapeDtypeStruct((n, brows * size), F32) for n in chunks],
        scratch_shapes=[
            pltpu.VMEM((brows, kband, size, size), F32),
            pltpu.VMEM((brows, size, size), F32),
            pltpu.VMEM((brows, size, total), F32),
            pltpu.VMEM((brows, 2 * total, size), BF16),
            pltpu.VMEM((total, size), F32),
            pltpu.SemaphoreType.DMA((3, brows)),
        ],
        compiler_params=pltpu.CompilerParams(vmem_limit_bytes=limit),
        cost_estimate=pl.CostEstimate(flops=6 * 10 * size * size * total, bytes_accessed=8 << 20, transcendentals=0),
    )(offsets, blocks, inverses, coupling)


def response_kernel(off_ref, f_hbm, inv_hbm, gh_ref, gl_ref, f, inverse, kept, acc, sems):
    brows, kband, size, _ = f.shape

    @pl.when(lax.axis_index("row") > 0)
    def _():
        copies = []
        for i in range(brows):
            group = [
                pltpu.make_async_copy(inv_hbm.at[0, i], inverse.at[i], sems.at[0, i]),
                pltpu.make_async_copy(f_hbm.at[0, i], f.at[i], sems.at[1, i]),
            ]
            for copy in group:
                copy.start()
            copies.append(group)

        def begin(i):
            for copy in copies[i]:
                copy.wait()
            acc[...] = jnp.zeros_like(acc)
            for band in range(kband):
                source = i - off_ref[band, 0, i]

                @pl.when(source < 0)
                def _():
                    at = pl.multiple_of((source + brows) * size, size)
                    acc[pl.ds(at, size), :] += f[i, band].T

        def finish(i, x):
            at = slice(i * size, (i + 1) * size)
            gh_ref[:, at], gl_ref[:, at] = split(x)

        substitute(off_ref, f, inverse, kept, acc, begin, finish)


def response(offsets, blocks, inverses):
    _, brows, kband, size, _ = blocks.shape
    width = brows * size
    hbm = pl.BlockSpec(memory_space=pltpu.HBM)
    return pl.pallas_call(
        response_kernel,
        in_specs=[pl.BlockSpec(memory_space=pltpu.SMEM), hbm, hbm],
        out_shape=[jax.ShapeDtypeStruct((width, width), BF16)] * 2,
        scratch_shapes=[
            pltpu.VMEM((brows, kband, size, size), F32),
            pltpu.VMEM((brows, size, size), F32),
            pltpu.VMEM((brows, 2 * width, size), BF16),
            pltpu.VMEM((width, size), F32),
            pltpu.SemaphoreType.DMA((2, brows)),
        ],
        compiler_params=pltpu.CompilerParams(vmem_limit_bytes=VMEM_LIMIT),
        cost_estimate=pl.CostEstimate(flops=6 * 10 * size * size * width, bytes_accessed=8 << 20, transcendentals=0),
        name="response",
    )(offsets, blocks, inverses)


def update_kernel(recv_ref, y_ref, cur_ref, gh_ref, gl_ref, out_ref, *, stage):
    out_ref[...] = cur_ref[...]

    @pl.when(lax.axis_index("row") == stage)
    def _():
        out_ref[...] = y_ref[...] - three(nn, stacked(recv_ref[...]), gh_ref[...], gl_ref[...])


def update(recv, y, cur, gain, stage):
    return pl.pallas_call(
        functools.partial(update_kernel, stage=stage),
        out_shape=jax.ShapeDtypeStruct(y.shape, F32),
        compiler_params=pltpu.CompilerParams(vmem_limit_bytes=VMEM_LIMIT),
        name="update",
    )(recv, y, cur, *gain)


def gram_kernel(*refs, start, fused, clear, last):
    recv_ref, y_ref = refs[:2]
    refs = refs[2:]
    if fused:
        gh_ref, gl_ref = refs[:2]
        refs = refs[2:]
    if start:
        oldh_ref, oldl_ref = refs[:2]
        refs = refs[2:]
    piece = refs[0]
    n, _ = recv_ref.shape
    here = slice(start, start + n)

    @pl.when(lax.axis_index("row") > 0)
    def _():
        recv = stacked(recv_ref[...])
        x = y_ref[...]
        if fused:
            x = x - three(nn, recv, gh_ref[...], gl_ref[...])
        x = stacked(x)
        high = jnp.concatenate([recv[:n], x[:n]], axis=1)
        low = jnp.concatenate([recv[n:], x[n:]], axis=1)
        both = jnp.concatenate([high, low], axis=0)
        if start:
            piece[:, :start] = three(nn, both, oldh_ref[:, :start], oldl_ref[:, :start])
        piece[:, here] = three(nt, both, high, low)
        if not last:
            refs[1][:, here] = high.T
            refs[2][:, here] = low.T

    if clear:

        @pl.when(lax.axis_index("row") == 0)
        def _():
            piece[...] = jnp.zeros_like(piece)


def gram(recv, y, gain, kept, start, total, clear):
    n, half = y.shape
    last = start + n == total
    fused = bool(gain)
    vmem = pl.BlockSpec(memory_space=pltpu.VMEM)
    inputs = [recv, y, *gain, *kept]
    results = pl.pallas_call(
        functools.partial(gram_kernel, start=start, fused=fused, clear=clear, last=last),
        in_specs=[vmem] * len(inputs),
        out_shape=[jax.ShapeDtypeStruct((n, start + n), F32)]
        + ([] if last else [jax.ShapeDtypeStruct((2 * half, total), BF16)] * 2),
        input_output_aliases={len(inputs) - 2 + i: 1 + i for i in range(2)} if start and not last else {},
        compiler_params=pltpu.CompilerParams(vmem_limit_bytes=VMEM_LIMIT),
        cost_estimate=pl.CostEstimate(
            flops=6 * n * half * (half + 2 * (start + n)), bytes_accessed=4 << 20, transcendentals=0
        ),
    )(*inputs)
    return results[0], list(results[1:])


def shared_slots(ids, mine, other, count):
    total = ids.shape[1]
    inside = jnp.logical_and(
        jnp.logical_and(mine >= 0, mine < total), jnp.logical_and(other >= 0, other < total)
    )
    mine, other = jnp.clip(mine, 0, total - 1), jnp.clip(other, 0, total - 1)
    found = jnp.int32(0)
    slots = [[jnp.int32(0), jnp.int32(0), jnp.bool_(False)] for _ in range(SLOTS)]
    for k in range(count):
        hit, place = jnp.bool_(False), jnp.int32(0)
        for i in range(count):
            same = ids[k, mine] == ids[i, other]
            hit = jnp.logical_or(hit, same)
            place = jnp.where(same, jnp.int32(i), place)
        hit = jnp.logical_and(hit, inside)
        for m, slot in enumerate(slots):
            take = jnp.logical_and(hit, found == m)
            slot[0] = jnp.where(take, jnp.int32(k), slot[0])
            slot[1] = jnp.where(take, place, slot[1])
            slot[2] = jnp.logical_or(slot[2], take)
        found = found + hit.astype(jnp.int32)
    return slots


def collect_kernel(ids_ref, face_ref, *refs, count, chunks, parts, exchanged):
    pieces, (base_ref, left_ref, right_ref, g) = refs[:-4], refs[-4:]
    _, share, cols = g.shape
    tile = cols // count
    row, sub = lax.axis_index("row"), lax.axis_index("sub")

    def fill(part):
        mine = pieces[len(chunks) :] if exchanged and part else pieces[: len(chunks)]
        low, high = part * share, (part + 1) * share
        start = 0
        for n, piece in zip(chunks, mine):
            at, inner = start // tile, start % tile
            first, stop = max(inner, low), min(inner + n, high)
            if first < stop:
                g[at, first - low : stop - low, : start + n] = piece[first - inner : stop - inner]
            turned = piece[:, :start].T if start else None
            for t in range(-(-start // tile)):
                stop = min(t * tile + high, start)
                first = t * tile + low
                if first < stop:
                    g[t, : stop - first, start : start + n] = turned[first:stop]
            start += n

    for part in range(parts):
        pl.when(row == part)(functools.partial(fill, part))
    base_ref[...] = face_ref[0] - g[...]
    for delta, out in ((-1, left_ref), (1, right_ref)):
        slots = shared_slots(ids_ref, sub, sub + delta, count)
        for m in range(SLOTS):
            for n in range(SLOTS):
                at = pl.multiple_of(slots[n][0] * tile, tile)
                out[m, :, n * tile : (n + 1) * tile] = g[slots[m][0], :, pl.ds(at, tile)]


def collect(ids, face, pieces, chunks, parts, exchanged):
    _, count, share, cols = face.shape
    smem = pl.BlockSpec(memory_space=pltpu.SMEM)
    vmem = pl.BlockSpec(memory_space=pltpu.VMEM)
    halo = jax.ShapeDtypeStruct((SLOTS, share, SLOTS * (cols // count)), F32)
    return pl.pallas_call(
        functools.partial(collect_kernel, count=count, chunks=chunks, parts=parts, exchanged=exchanged),
        in_specs=[smem, vmem] + [vmem] * len(pieces),
        out_shape=[jax.ShapeDtypeStruct((count, share, cols), F32), halo, halo],
        scratch_shapes=[pltpu.VMEM((count, share, cols), F32)],
        compiler_params=pltpu.CompilerParams(vmem_limit_bytes=VMEM_LIMIT),
        name="collect",
    )(ids, face, *pieces)


def finish_kernel(ids_ref, base_ref, left_ref, right_ref, out_ref, *, count):
    cols = base_ref.shape[2]
    tile = cols // count
    sub = lax.axis_index("sub")
    out_ref[0] = base_ref[...]
    for delta, halo in ((-1, left_ref), (1, right_ref)):
        slots = shared_slots(ids_ref, sub + delta, sub, count)
        for m in range(SLOTS):
            for n in range(SLOTS):

                @pl.when(jnp.logical_and(slots[m][2], slots[n][2]))
                def _():
                    at = pl.multiple_of(slots[n][1] * tile, tile)
                    out_ref[0, slots[m][1], :, pl.ds(at, tile)] -= halo[m, :, n * tile : (n + 1) * tile]


def finish(ids, base, left, right):
    count, share, cols = base.shape
    smem = pl.BlockSpec(memory_space=pltpu.SMEM)
    vmem = pl.BlockSpec(memory_space=pltpu.VMEM)
    return pl.pallas_call(
        functools.partial(finish_kernel, count=count),
        in_specs=[smem, vmem, vmem, vmem],
        out_shape=jax.ShapeDtypeStruct((1, count, share, cols), F32),
        compiler_params=pltpu.CompilerParams(vmem_limit_bytes=VMEM_LIMIT),
        name="finish",
    )(ids, base, left, right)


def sizes(count, tile):
    short = tile // LAST
    return (tile,) * (count - 1) + (tile - short, short)


def shards(factor_blocks, block_inverses, band_offsets, coupling, interface_block, tile_ids):
    rows = lax.axis_size("row")
    subs = lax.axis_size("sub")
    count = interface_block.shape[1]
    cols = coupling.shape[2]
    chunks = sizes(count, cols // count)
    offsets = jnp.transpose(band_offsets, (2, 0, 1))
    ids = jnp.transpose(tile_ids)
    ys = solve(offsets, factor_blocks, block_inverses, coupling, 0, chunks[:1], ALONE)
    ys += solve(offsets, factor_blocks, block_inverses, coupling, chunks[0], chunks[1:], VMEM_LIMIT)
    gain = response(offsets, factor_blocks, block_inverses)
    xs, first, gain_now = list(ys), None, gain if rows == 2 else ()
    for stage in range(1, rows):
        recv = []
        for x in xs:
            recv.append(lax.ppermute(x, "row", [(stage - 1, stage)]))
        first = first or recv
        if rows > 2:
            xs = [update(r, y, x, gain, stage) for r, y, x in zip(recv, ys, xs)]
    kept, own, got, start = [], [], [], 0
    for c, n in enumerate(chunks):
        piece, kept = gram(first[c], xs[c], gain_now, kept, start, cols, rows > 2)
        start += n
        if rows == 2:
            got.append(lax.ppermute(piece, "row", [(1, 0)]))
            own.append(piece)
        else:
            got.append(lax.psum(piece, "row"))
    base, left, right = collect(ids, interface_block, got + own, chunks, rows, rows == 2)
    from_left = lax.ppermute(right, "sub", [(i, i + 1) for i in range(subs - 1)])
    from_right = lax.ppermute(left, "sub", [(i + 1, i) for i in range(subs - 1)])
    return finish(ids, base, from_left, from_right)


def solution(mesh):
    return jax.shard_map(
        shards,
        mesh=mesh,
        in_specs=(
            P("sub", "row", None, None, None),
            P("sub", "row", None, None),
            P("sub", "row", None),
            P("sub", "row", None),
            P("sub", None, "row", None),
            P(),
        ),
        out_specs=P("sub", None, "row", None),
        check_vma=False,
    )
```

profile of v0, /device:TPU:11, one launch (start us, length us, event | category | flops | bytes accessed | tf_op | source)
XLA Modules:
  0.0 80.8 jit_solution(15793247717903481768)
XLA Ops:
  0.0 5.8 %shard_map.64.refs_1_ = f32[128,1024]{1,0:T(8,128)} custom-call(s32[3,1,4]{2,1,0:T(1,128)} %bitcast.4, f32[1,4,3,256,256]{4,3,2,1,0:T(8,128)} %f_hbm.5, f32[1,4,256,256]{3,2,1,0:T(8,128)} %inv_hbm.5, f32[1,1024,512]{2,1,0:T(8,128)} %b_hbm.3), custom_call_target="tpu_custom_call" | custom-call | flops 503316480 | bytes 8388608 | tf_op jit(solution)/shard_map/pallas_call | solution.py:96
  5.8 2.7 %collective-permute-start = (f32[128,1024]{1,0:T(8,128)}, f32[128,1024]{1,0:T(8,128)S(1)}, u32[]{:S(2)}, u32[]{:S(2)}) collective-permute-start(f32[128,1024]{1,0:T(8,128)} %shard_map.64.refs_1_), channel_id=1, source_target_pairs={{0,1},{2,3},{4,5},{6,7},{8,9},{10,11},{12,13},{14,15},{16,17},{18,... | collective-permute-start | bytes 1572872 | tf_op jit(solution)/shard_map/ppermute | solution.py:364
  8.5 0.0 copy-start
  8.5 1.9 %copy-done = f32[1,4,3,256,256]{4,3,2,1,0:T(8,128)S(1)} copy-done((f32[1,4,3,256,256]{4,3,2,1,0:T(8,128)S(1)}, f32[1,4,3,256,256]{4,3,2,1,0:T(8,128)}, u32[]{:S(2)}) %copy-start) | copy-done | bytes 3145752
  10.4 1.6 %copy-done.1 = f32[1,1024,512]{2,1,0:T(8,128)S(1)} copy-done((f32[1,1024,512]{2,1,0:T(8,128)S(1)}, f32[1,1024,512]{2,1,0:T(8,128)}, u32[]{:S(2)}) %copy-start.1) | copy-done | bytes 2097176
  12.0 1.2 %copy-done.2 = f32[1,4,256,256]{3,2,1,0:T(8,128)S(1)} copy-done((f32[1,4,256,256]{3,2,1,0:T(8,128)S(1)}, f32[1,4,256,256]{3,2,1,0:T(8,128)}, u32[]{:S(2)}) %copy-start.2) | copy-done | bytes 1048600
  13.2 5.2 %shard_map.66 = (f32[128,1024]{1,0:T(8,128)S(1)}, f32[128,1024]{1,0:T(8,128)S(1)}, f32[96,1024]{1,0:T(8,128)S(1)}, f32[32,1024]{1,0:T(8,128)S(1)}) custom-call(s32[3,1,4]{2,1,0:T(1,128)S(1)} %bitcast.5, f32[1,4,3,256,256]{4,3,2,1,0:T(8,128)S(1)} %copy-done, f32[1,4,256,256]{3,2,1,0:T(8,128)S(1)} %copy-done.2, f32[1,1024,512]{2,1,0:T(8,128)S(1)} %copy-done.1), custom_call_target="tpu_custom_call" | custom-call | flops 1509949440 | bytes 8388608 | tf_op jit(solution)/shard_map/pallas_call | solution.py:96
  18.4 1.3 %collective-permute-start.2 = (f32[128,1024]{1,0:T(8,128)S(1)}, f32[128,1024]{1,0:T(8,128)S(1)}, u32[]{:S(2)}, u32[]{:S(2)}) collective-permute-start(f32[128,1024]{1,0:T(8,128)S(1)} %get-tuple-element.29.refs_1_), channel_id=1, source_target_pairs={{0,1},{2,3},{4,5},{6,7},{8,9},{10,11},{12,13},{14,15},{16,17},{18,... | collective-permute-start | bytes 1572872 | tf_op jit(solution)/shard_map/ppermute | solution.py:364
  19.7 1.3 %collective-permute-start.4 = (f32[128,1024]{1,0:T(8,128)S(1)}, f32[128,1024]{1,0:T(8,128)S(1)}, u32[]{:S(2)}, u32[]{:S(2)}) collective-permute-start(f32[128,1024]{1,0:T(8,128)S(1)} %get-tuple-element.33.refs_1_), channel_id=1, source_target_pairs={{0,1},{2,3},{4,5},{6,7},{8,9},{10,11},{12,13},{14,15},{16,17},{18,... | collective-permute-start | bytes 1572872 | tf_op jit(solution)/shard_map/ppermute | solution.py:364
  21.1 1.3 %collective-permute-start.6 = (f32[96,1024]{1,0:T(8,128)S(1)}, f32[96,1024]{1,0:T(8,128)S(1)}, u32[]{:S(2)}, u32[]{:S(2)}) collective-permute-start(f32[96,1024]{1,0:T(8,128)S(1)} %get-tuple-element.37.refs_1_), channel_id=1, source_target_pairs={{0,1},{2,3},{4,5},{6,7},{8,9},{10,11},{12,13},{14,15},{16,17},{18,... | collective-permute-start | bytes 1179656 | tf_op jit(solution)/shard_map/ppermute | solution.py:364
  22.4 0.0 copy-start.3
  22.4 1.4 %collective-permute-start.8 = (f32[32,1024]{1,0:T(8,128)S(1)}, f32[32,1024]{1,0:T(8,128)S(1)}, u32[]{:S(2)}, u32[]{:S(2)}) collective-permute-start(f32[32,1024]{1,0:T(8,128)S(1)} %get-tuple-element.41.refs_1_), channel_id=1, source_target_pairs={{0,1},{2,3},{4,5},{6,7},{8,9},{10,11},{12,13},{14,15},{16,17},{18,... | collective-permute-start | bytes 393224 | tf_op jit(solution)/shard_map/ppermute | solution.py:364
  23.8 0.9 %response.1 = (bf16[1024,1024]{1,0:T(8,128)(2,1)S(1)}, bf16[1024,1024]{1,0:T(8,128)(2,1)S(1)}) custom-call(s32[3,1,4]{2,1,0:T(1,128)S(1)} %bitcast.6, f32[1,4,3,256,256]{4,3,2,1,0:T(8,128)S(1)} %copy-done, f32[1,4,256,256]{3,2,1,0:T(8,128)S(1)} %copy-done.2), custom_call_target="tpu_custom_call" | custom-call | flops 4026531840 | bytes 8388608 | tf_op jit(solution)/shard_map/response/pallas_call | solution.py:151
  24.7 0.0 collective-permute-done.refs_0_
  24.8 6.0 %collective-permute-done.2.refs_0_ = f32[128,1024]{1,0:T(8,128)S(1)} collective-permute-done((f32[128,1024]{1,0:T(8,128)S(1)}, f32[128,1024]{1,0:T(8,128)S(1)}, u32[]{:S(2)}, u32[]{:S(2)}) %collective-permute-start.2) | collective-permute-done | bytes 524320 | tf_op jit(solution)/shard_map/ppermute | solution.py:364
  30.7 11.2 %collective-permute-done.4.refs_0_ = f32[128,1024]{1,0:T(8,128)S(1)} collective-permute-done((f32[128,1024]{1,0:T(8,128)S(1)}, f32[128,1024]{1,0:T(8,128)S(1)}, u32[]{:S(2)}, u32[]{:S(2)}) %collective-permute-start.4) | collective-permute-done | bytes 524320 | tf_op jit(solution)/shard_map/ppermute | solution.py:364
  42.0 1.3 %collective-permute-start.5 = (f32[128,384]{1,0:T(8,128)S(1)}, f32[128,384]{1,0:T(8,128)S(1)}, u32[]{:S(2)}, u32[]{:S(2)}) collective-permute-start(f32[128,384]{1,0:T(8,128)S(1)} %get-tuple-element.36.refs_7_), channel_id=1, source_target_pairs={{1,0},{3,2},{5,4},{7,6},{9,8},{11,10},{13,12},{15,14},{17,16},{19,... | collective-permute-start | bytes 589832 | tf_op jit(solution)/shard_map/ppermute | solution.py:373
  43.3 7.1 %collective-permute-done.6.refs_0_ = f32[96,1024]{1,0:T(8,128)S(1)} collective-permute-done((f32[96,1024]{1,0:T(8,128)S(1)}, f32[96,1024]{1,0:T(8,128)S(1)}, u32[]{:S(2)}, u32[]{:S(2)}) %collective-permute-start.6) | collective-permute-done | bytes 393248 | tf_op jit(solution)/shard_map/ppermute | solution.py:364
  50.4 1.3 %collective-permute-start.7 = (f32[96,480]{1,0:T(8,128)S(1)}, f32[96,480]{1,0:T(8,128)S(1)}, u32[]{:S(2)}, u32[]{:S(2)}) collective-permute-start(f32[96,480]{1,0:T(8,128)S(1)} %get-tuple-element.40.refs_8_), channel_id=1, source_target_pairs={{1,0},{3,2},{5,4},{7,6},{9,8},{11,10},{13,12},{15,14},{17,16},{19,... | collective-permute-start | bytes 552968 | tf_op jit(solution)/shard_map/ppermute | solution.py:373
  51.7 1.3 %collective-permute-start.3 = (f32[128,256]{1,0:T(8,128)S(1)}, f32[128,256]{1,0:T(8,128)S(1)}, u32[]{:S(2)}, u32[]{:S(2)}) collective-permute-start(f32[128,256]{1,0:T(8,128)S(1)} %get-tuple-element.32.refs_6_), channel_id=1, source_target_pairs={{1,0},{3,2},{5,4},{7,6},{9,8},{11,10},{13,12},{15,14},{17,16},{19,... | collective-permute-start | bytes 393224 | tf_op jit(solution)/shard_map/ppermute | solution.py:373
  53.0 0.2 collective-permute-done.8.refs_0_
  53.2 1.4 %collective-permute-start.9 = (f32[32,512]{1,0:T(8,128)S(1)}, f32[32,512]{1,0:T(8,128)S(1)}, u32[]{:S(2)}, u32[]{:S(2)}) collective-permute-start(f32[32,512]{1,0:T(8,128)S(1)} %shard_map.70.refs_9_), channel_id=1, source_target_pairs={{1,0},{3,2},{5,4},{7,6},{9,8},{11,10},{13,12},{15,14},{17,16},{19,... | collective-permute-start | bytes 196616 | tf_op jit(solution)/shard_map/ppermute | solution.py:373
  54.6 1.3 %collective-permute-start.1 = (f32[128,128]{1,0:T(8,128)S(1)}, f32[128,128]{1,0:T(8,128)S(1)}, u32[]{:S(2)}, u32[]{:S(2)}) collective-permute-start(f32[128,128]{1,0:T(8,128)S(1)} %get-tuple-element.28.refs_5_), channel_id=1, source_target_pairs={{1,0},{3,2},{5,4},{7,6},{9,8},{11,10},{13,12},{15,14},{17,16},{19,... | collective-permute-start | bytes 196616 | tf_op jit(solution)/shard_map/ppermute | solution.py:373
  55.9 7.4 %collective-permute-done.9.refs_4_ = f32[32,512]{1,0:T(8,128)S(1)} collective-permute-done((f32[32,512]{1,0:T(8,128)S(1)}, f32[32,512]{1,0:T(8,128)S(1)}, u32[]{:S(2)}, u32[]{:S(2)}) %collective-permute-start.9) | collective-permute-done | bytes 65568 | tf_op jit(solution)/shard_map/ppermute | solution.py:373
  63.4 1.4 %collective-permute-done.1.refs_0_ = f32[128,128]{1,0:T(8,128)S(1)} collective-permute-done((f32[128,128]{1,0:T(8,128)S(1)}, f32[128,128]{1,0:T(8,128)S(1)}, u32[]{:S(2)}, u32[]{:S(2)}) %collective-permute-start.1) | collective-permute-done | bytes 65568 | tf_op jit(solution)/shard_map/ppermute | solution.py:373
  64.8 0.0 collective-permute-done.7.refs_3_
  64.8 0.0 collective-permute-done.5.refs_2_
  64.8 0.9 %collect.1 = (f32[4,64,512]{2,1,0:T(8,128)S(1)}, f32[2,64,256]{2,1,0:T(8,128)S(1)}, f32[2,64,256]{2,1,0:T(8,128)S(1)}) custom-call(s32[4,16]{1,0:T(4,128)S(1)} %bitcast.2, f32[1,4,64,512]{3,2,1,0:T(8,128)S(1)} %copy-done.4, f32[128,128]{1,0:T(8,128)S(1)} %collective-permute-done.1.refs_0_, f32[128,256]{1,0:T(8,128)S(1)} %collective-permute-done.3.refs_1_, ...), custom_call_target="tpu_custom_call" | custom-call | tf_op jit(solution)/shard_map/collect/pallas_call | solution.py:305
  65.7 6.3 %collective-permute-start.10 = (f32[2,64,256]{2,1,0:T(8,128)S(1)}, f32[2,64,256]{2,1,0:T(8,128)S(1)}, u32[]{:S(2)}, u32[]{:S(2)}) collective-permute-start(f32[2,64,256]{2,1,0:T(8,128)S(1)} %get-tuple-element.45), channel_id=1, source_target_pairs={{0,2},{2,4},{4,6},{6,8},{8,10},{10,12},{12,14},{14,16},{16,18},{18... | collective-permute-start | bytes 393224 | tf_op jit(solution)/shard_map/ppermute | solution.py:378
  72.1 1.9 %collective-permute-start.11 = (f32[2,64,256]{2,1,0:T(8,128)S(1)}, f32[2,64,256]{2,1,0:T(8,128)S(1)}, u32[]{:S(2)}, u32[]{:S(2)}) collective-permute-start(f32[2,64,256]{2,1,0:T(8,128)S(1)} %get-tuple-element.46), channel_id=1, source_target_pairs={{2,0},{4,2},{6,4},{8,6},{10,8},{12,10},{14,12},{16,14},{18,16},{20... | collective-permute-start | bytes 393224 | tf_op jit(solution)/shard_map/ppermute | solution.py:379
  74.0 5.2 %collective-permute-done.11.right_ref = f32[2,64,256]{2,1,0:T(8,128)S(1)} collective-permute-done((f32[2,64,256]{2,1,0:T(8,128)S(1)}, f32[2,64,256]{2,1,0:T(8,128)S(1)}, u32[]{:S(2)}, u32[]{:S(2)}) %collective-permute-start.11) | collective-permute-done | bytes 131104 | tf_op jit(solution)/shard_map/ppermute | solution.py:379
  79.3 1.5 %finish.1 = f32[1,4,64,512]{3,2,1,0:T(8,128)} custom-call(s32[4,16]{1,0:T(4,128)S(1)} %bitcast.3, f32[4,64,512]{2,1,0:T(8,128)S(1)} %get-tuple-element.44.base_ref, f32[2,64,256]{2,1,0:T(8,128)S(1)} %collective-permute-done.10.left_ref, f32[2,64,256]{2,1,0:T(8,128)S(1)} %collective-permute-done.11.right_ref), custom_call_target="tpu_custom_call" | custom-call | tf_op jit(solution)/shard_map/finish/pallas_call | solution.py:335
  (16 shorter events, 0.0 us)
Async XLA Ops:
  0.0 8.5 %copy-start.6 = (s32[1,4,3]{1,0,2:T(1,128)S(1)}, s32[1,4,3]{1,0,2:T(1,128)}, u32[]{:S(2)}) copy-start(s32[1,4,3]{1,0,2:T(1,128)} %param.8) | copy-start | bytes 148
  5.8 18.9 %collective-permute-start = (f32[128,1024]{1,0:T(8,128)}, f32[128,1024]{1,0:T(8,128)S(1)}, u32[]{:S(2)}, u32[]{:S(2)}) collective-permute-start(f32[128,1024]{1,0:T(8,128)} %shard_map.64.refs_1_), channel_id=1, source_target_pairs={{0,1},{2,3},{4,5},{6,7},{8,9},{10,11},{12,13},{14,15},{16,17},{18,... | collective-permute-start | bytes 1572872 | tf_op jit(solution)/shard_map/ppermute | solution.py:364
  8.5 1.9 %copy-start = (f32[1,4,3,256,256]{4,3,2,1,0:T(8,128)S(1)}, f32[1,4,3,256,256]{4,3,2,1,0:T(8,128)}, u32[]{:S(2)}) copy-start(f32[1,4,3,256,256]{4,3,2,1,0:T(8,128)} %f_hbm.5) | copy-start | bytes 9437188
  10.4 1.6 %copy-start.1 = (f32[1,1024,512]{2,1,0:T(8,128)S(1)}, f32[1,1024,512]{2,1,0:T(8,128)}, u32[]{:S(2)}) copy-start(f32[1,1024,512]{2,1,0:T(8,128)} %b_hbm.3) | copy-start | bytes 6291460
  12.0 1.2 %copy-start.2 = (f32[1,4,256,256]{3,2,1,0:T(8,128)S(1)}, f32[1,4,256,256]{3,2,1,0:T(8,128)}, u32[]{:S(2)}) copy-start(f32[1,4,256,256]{3,2,1,0:T(8,128)} %inv_hbm.5) | copy-start | bytes 3145732
  18.4 12.3 %collective-permute-start.2 = (f32[128,1024]{1,0:T(8,128)S(1)}, f32[128,1024]{1,0:T(8,128)S(1)}, u32[]{:S(2)}, u32[]{:S(2)}) collective-permute-start(f32[128,1024]{1,0:T(8,128)S(1)} %get-tuple-element.29.refs_1_), channel_id=1, source_target_pairs={{0,1},{2,3},{4,5},{6,7},{8,9},{10,11},{12,13},{14,15},{16,17},{18,... | collective-permute-start | bytes 1572872 | tf_op jit(solution)/shard_map/ppermute | solution.py:364
  19.7 22.2 %collective-permute-start.4 = (f32[128,1024]{1,0:T(8,128)S(1)}, f32[128,1024]{1,0:T(8,128)S(1)}, u32[]{:S(2)}, u32[]{:S(2)}) collective-permute-start(f32[128,1024]{1,0:T(8,128)S(1)} %get-tuple-element.33.refs_1_), channel_id=1, source_target_pairs={{0,1},{2,3},{4,5},{6,7},{8,9},{10,11},{12,13},{14,15},{16,17},{18,... | collective-permute-start | bytes 1572872 | tf_op jit(solution)/shard_map/ppermute | solution.py:364
  21.1 29.3 %collective-permute-start.6 = (f32[96,1024]{1,0:T(8,128)S(1)}, f32[96,1024]{1,0:T(8,128)S(1)}, u32[]{:S(2)}, u32[]{:S(2)}) collective-permute-start(f32[96,1024]{1,0:T(8,128)S(1)} %get-tuple-element.37.refs_1_), channel_id=1, source_target_pairs={{0,1},{2,3},{4,5},{6,7},{8,9},{10,11},{12,13},{14,15},{16,17},{18,... | collective-permute-start | bytes 1179656 | tf_op jit(solution)/shard_map/ppermute | solution.py:364
  22.4 2.3 %copy-start.3 = (f32[128,1024]{1,0:T(8,128)S(1)}, f32[128,1024]{1,0:T(8,128)}, u32[]{:S(2)}) copy-start(f32[128,1024]{1,0:T(8,128)} %shard_map.64.refs_1_) | copy-start | bytes 1572868
  22.4 30.8 %collective-permute-start.8 = (f32[32,1024]{1,0:T(8,128)S(1)}, f32[32,1024]{1,0:T(8,128)S(1)}, u32[]{:S(2)}, u32[]{:S(2)}) collective-permute-start(f32[32,1024]{1,0:T(8,128)S(1)} %get-tuple-element.41.refs_1_), channel_id=1, source_target_pairs={{0,1},{2,3},{4,5},{6,7},{8,9},{10,11},{12,13},{14,15},{16,17},{18,... | collective-permute-start | bytes 393224 | tf_op jit(solution)/shard_map/ppermute | solution.py:364
  42.0 22.8 %collective-permute-start.5 = (f32[128,384]{1,0:T(8,128)S(1)}, f32[128,384]{1,0:T(8,128)S(1)}, u32[]{:S(2)}, u32[]{:S(2)}) collective-permute-start(f32[128,384]{1,0:T(8,128)S(1)} %get-tuple-element.36.refs_7_), channel_id=1, source_target_pairs={{1,0},{3,2},{5,4},{7,6},{9,8},{11,10},{13,12},{15,14},{17,16},{19,... | collective-permute-start | bytes 589832 | tf_op jit(solution)/shard_map/ppermute | solution.py:373
  50.4 14.4 %collective-permute-start.7 = (f32[96,480]{1,0:T(8,128)S(1)}, f32[96,480]{1,0:T(8,128)S(1)}, u32[]{:S(2)}, u32[]{:S(2)}) collective-permute-start(f32[96,480]{1,0:T(8,128)S(1)} %get-tuple-element.40.refs_8_), channel_id=1, source_target_pairs={{1,0},{3,2},{5,4},{7,6},{9,8},{11,10},{13,12},{15,14},{17,16},{19,... | collective-permute-start | bytes 552968 | tf_op jit(solution)/shard_map/ppermute | solution.py:373
  51.7 13.1 %collective-permute-start.3 = (f32[128,256]{1,0:T(8,128)S(1)}, f32[128,256]{1,0:T(8,128)S(1)}, u32[]{:S(2)}, u32[]{:S(2)}) collective-permute-start(f32[128,256]{1,0:T(8,128)S(1)} %get-tuple-element.32.refs_6_), channel_id=1, source_target_pairs={{1,0},{3,2},{5,4},{7,6},{9,8},{11,10},{13,12},{15,14},{17,16},{19,... | collective-permute-start | bytes 393224 | tf_op jit(solution)/shard_map/ppermute | solution.py:373
  53.2 11.6 %copy-start.4 = (f32[1,4,64,512]{3,2,1,0:T(8,128)S(1)}, f32[1,4,64,512]{3,2,1,0:T(8,128)}, u32[]{:S(2)}) copy-start(f32[1,4,64,512]{3,2,1,0:T(8,128)} %face_ref.1) | copy-start | bytes 1572868
  53.2 11.6 %copy-start.5 = (s32[16,4]{0,1:T(4,128)S(1)}, s32[16,4]{0,1:T(4,128)}, u32[]{:S(2)}) copy-start(s32[16,4]{0,1:T(4,128)} %param.11) | copy-start | bytes 772
  53.2 10.1 %collective-permute-start.9 = (f32[32,512]{1,0:T(8,128)S(1)}, f32[32,512]{1,0:T(8,128)S(1)}, u32[]{:S(2)}, u32[]{:S(2)}) collective-permute-start(f32[32,512]{1,0:T(8,128)S(1)} %shard_map.70.refs_9_), channel_id=1, source_target_pairs={{1,0},{3,2},{5,4},{7,6},{9,8},{11,10},{13,12},{15,14},{17,16},{19,... | collective-permute-start | bytes 196616 | tf_op jit(solution)/shard_map/ppermute | solution.py:373
  54.6 10.1 %collective-permute-start.1 = (f32[128,128]{1,0:T(8,128)S(1)}, f32[128,128]{1,0:T(8,128)S(1)}, u32[]{:S(2)}, u32[]{:S(2)}) collective-permute-start(f32[128,128]{1,0:T(8,128)S(1)} %get-tuple-element.28.refs_5_), channel_id=1, source_target_pairs={{1,0},{3,2},{5,4},{7,6},{9,8},{11,10},{13,12},{15,14},{17,16},{19,... | collective-permute-start | bytes 196616 | tf_op jit(solution)/shard_map/ppermute | solution.py:373
  65.7 8.3 %collective-permute-start.10 = (f32[2,64,256]{2,1,0:T(8,128)S(1)}, f32[2,64,256]{2,1,0:T(8,128)S(1)}, u32[]{:S(2)}, u32[]{:S(2)}) collective-permute-start(f32[2,64,256]{2,1,0:T(8,128)S(1)} %get-tuple-element.45), channel_id=1, source_target_pairs={{0,2},{2,4},{4,6},{6,8},{8,10},{10,12},{12,14},{14,16},{16,18},{18... | collective-permute-start | bytes 393224 | tf_op jit(solution)/shard_map/ppermute | solution.py:378
  72.1 7.2 %collective-permute-start.11 = (f32[2,64,256]{2,1,0:T(8,128)S(1)}, f32[2,64,256]{2,1,0:T(8,128)S(1)}, u32[]{:S(2)}, u32[]{:S(2)}) collective-permute-start(f32[2,64,256]{2,1,0:T(8,128)S(1)} %get-tuple-element.46), channel_id=1, source_target_pairs={{2,0},{4,2},{6,4},{8,6},{10,8},{12,10},{14,12},{16,14},{18,16},{20... | collective-permute-start | bytes 393224 | tf_op jit(solution)/shard_map/ppermute | solution.py:379
where the time goes:
time: 81.2 us; the launch traced here: 80.8 us
  waiting for transfers between devices  38.7 us (48%)
  starting transfers between devices  22.9 us (28%)
  Pallas kernels  14.3 us (18%)
  local copies, waits for them, and re-layouts  4.72 us (6%)
    ppermute x5, waiting for transfers between devices, shards(): recv.append(lax.ppermute(x, 'row', [(stage - 1, stage)]))  24.6 us
    pallas_call x2, Pallas kernels, solve(): pl.pallas_call(functools.partial(solve_kernel, first=first, chunks=chunks...  11 us
    ppermute x5, waiting for transfers between devices, shards(): got.append(lax.ppermute(piece, 'row', [(1, 0)]))  8.83 us
    ppermute x5, starting transfers between devices, shards(): recv.append(lax.ppermute(x, 'row', [(stage - 1, stage)]))  8.05 us
    ppermute x5, starting transfers between devices, shards(): got.append(lax.ppermute(piece, 'row', [(1, 0)]))  6.56 us
    ppermute x1, starting transfers between devices, shards(): lax.ppermute(right, 'sub', [(i, i + 1) for i in range(subs - 1)])  6.32 us
    ppermute x1, waiting for transfers between devices, shards(): lax.ppermute(left, 'sub', [(i + 1, i) for i in range(subs - 1)])  5.25 us
    unnamed x14, local copies, waits for them, and re-layouts  4.72 us
  transfers between devices with their start and end apart: 12, of which 7 were waited for; matrix products, arithmetic and copies ran while one was open for 0% of the time, Pallas kernels for 8%

commit v1 on v0

v1 whole, which is shorter than its diff:
```python
import functools

import jax
import jax.numpy as jnp
from jax import lax
from jax.experimental import pallas as pl
from jax.experimental.pallas import tpu as pltpu
from jax.sharding import PartitionSpec as P


F32 = jnp.float32
BF16 = jnp.bfloat16
VMEM_LIMIT = 24 * 1024 * 1024
ALONE = 63 * 1024 * 1024
PAIR = 2
LAST = 4


def split(x):
    high = x.astype(BF16)
    return high, (x - high.astype(F32)).astype(BF16)


def nt(a, b):
    return lax.dot_general(a, b, (((1,), (1,)), ((), ())), preferred_element_type=F32)


def nn(a, b):
    return lax.dot_general(a, b, (((1,), (0,)), ((), ())), preferred_element_type=F32)


def three(dot, both, high, low):
    rows = both.shape[0] // 2
    wide = dot(both, high)
    return wide[:rows] + (wide[rows:] + dot(both[:rows], low))


def stacked(x):
    return jnp.concatenate(split(x), axis=0)


def near_of(sub):
    return sub + 1 - 2 * (sub % 2)


def far_of(sub):
    return sub - 1 + 2 * (sub % 2)


def shares(ids, k, sub, other):
    count, total = ids.shape
    inside = jnp.logical_and(other >= 0, other < total)
    other = jnp.clip(other, 0, total - 1)
    hit = ids[k, sub] == ids[0, other]
    for i in range(1, count):
        hit = jnp.logical_or(hit, ids[k, sub] == ids[i, other])
    return jnp.logical_and(hit, inside)


def ordered(ids, sub):
    count = ids.shape[0]
    keys = []
    for k in range(count):
        far = shares(ids, k, sub, far_of(sub)).astype(jnp.int32)
        near = shares(ids, k, sub, near_of(sub)).astype(jnp.int32)
        keys.append((1 + near - far) * count + k)
    order = [jnp.int32(0)] * count
    for k in range(count):
        place = sum((keys[j] < keys[k]).astype(jnp.int32) for j in range(count) if j != k)
        order = [jnp.where(place == p, jnp.int32(k), order[p]) for p in range(count)]
    return order


def wait_all(copies):
    for copy in copies:
        copy.wait()


def substitute(off_ref, f, inverse, begin, finish):
    brows, kband = f.shape[0], f.shape[1]
    solved = []
    for i in range(brows):
        rest = begin(i)
        for j in range(i):
            at, found = jnp.int32(0), jnp.bool_(False)
            for band in range(kband):
                same = off_ref[band, 0, i] == i - j
                at = jnp.where(same, jnp.int32(band), at)
                found = jnp.logical_or(found, same)
            block = jnp.where(found, f[i, at], 0.0)
            rest = rest - three(nt, solved[j], *split(block))
        x = three(nt, stacked(rest), *split(inverse[i]))
        solved.append(stacked(x))
        finish(i, x)


def solve_kernel(off_ref, ids_ref, f_hbm, inv_hbm, b_hbm, *rest, chunks, tiles, first_only):
    outs, (f, inverse, b, sems) = rest[: len(chunks)], rest[len(chunks) :]
    brows, _, size, _ = f.shape
    tile = b.shape[2] // tiles

    def run():
        order = ordered(ids_ref, lax.axis_index("sub"))
        copies = []
        for i in range(brows):
            group = [pltpu.make_async_copy(inv_hbm.at[0, i], inverse.at[i], sems.at[0, i])]
            for p in range(tiles):
                columns = pl.ds(pl.multiple_of(order[p] * tile, tile), tile)
                group.append(
                    pltpu.make_async_copy(
                        b_hbm.at[0, pl.ds(i * size, size), columns],
                        b.at[i, :, pl.ds(p * tile, tile)],
                        sems.at[2 + p, i],
                    )
                )
            if i > 0:
                group.append(pltpu.make_async_copy(f_hbm.at[0, i], f.at[i], sems.at[1, i]))
            for copy in group:
                copy.start()
            copies.append(group)

        def begin(i):
            wait_all(copies[i])
            return b[i].T

        def finish(i, x):
            start = 0
            for out, n in zip(outs, chunks):
                out[:, i * size : (i + 1) * size] = x[start : start + n]
                start += n

        substitute(off_ref, f, inverse, begin, finish)

    if first_only:
        pl.when(lax.axis_index("row") == 0)(run)
    else:
        run()


def solve(offsets, ids, blocks, inverses, coupling, chunks, tile, first_only, limit):
    _, brows, kband, size, _ = blocks.shape
    total = sum(chunks)
    tiles = total // tile
    hbm = pl.BlockSpec(memory_space=pltpu.HBM)
    smem = pl.BlockSpec(memory_space=pltpu.SMEM)
    return pl.pallas_call(
        functools.partial(solve_kernel, chunks=chunks, tiles=tiles, first_only=first_only),
        in_specs=[smem, smem, hbm, hbm, hbm],
        out_shape=[jax.ShapeDtypeStruct((n, brows * size), F32) for n in chunks],
        scratch_shapes=[
            pltpu.VMEM((brows, kband, size, size), F32),
            pltpu.VMEM((brows, size, size), F32),
            pltpu.VMEM((brows, size, total), F32),
            pltpu.SemaphoreType.DMA((2 + tiles, brows)),
        ],
        compiler_params=pltpu.CompilerParams(vmem_limit_bytes=limit),
        cost_estimate=pl.CostEstimate(flops=6 * 10 * size * size * total, bytes_accessed=8 << 20, transcendentals=0),
    )(offsets, ids, blocks, inverses, coupling)


def response_kernel(off_ref, f_hbm, inv_hbm, gh_ref, gl_ref, f, inverse, acc, sems):
    brows, kband, size, _ = f.shape

    @pl.when(lax.axis_index("row") > 0)
    def _():
        copies = []
        for i in range(brows):
            group = [
                pltpu.make_async_copy(inv_hbm.at[0, i], inverse.at[i], sems.at[0, i]),
                pltpu.make_async_copy(f_hbm.at[0, i], f.at[i], sems.at[1, i]),
            ]
            for copy in group:
                copy.start()
            copies.append(group)

        def begin(i):
            wait_all(copies[i])
            acc[...] = jnp.zeros_like(acc)
            for band in range(kband):
                source = i - off_ref[band, 0, i]

                @pl.when(source < 0)
                def _():
                    at = pl.multiple_of((source + brows) * size, size)
                    acc[pl.ds(at, size), :] += f[i, band].T

            return acc[...]

        def finish(i, x):
            at = slice(i * size, (i + 1) * size)
            gh_ref[:, at], gl_ref[:, at] = split(x)

        substitute(off_ref, f, inverse, begin, finish)


def response(offsets, blocks, inverses):
    _, brows, kband, size, _ = blocks.shape
    width = brows * size
    hbm = pl.BlockSpec(memory_space=pltpu.HBM)
    return pl.pallas_call(
        response_kernel,
        in_specs=[pl.BlockSpec(memory_space=pltpu.SMEM), hbm, hbm],
        out_shape=[jax.ShapeDtypeStruct((width, width), BF16)] * 2,
        scratch_shapes=[
            pltpu.VMEM((brows, kband, size, size), F32),
            pltpu.VMEM((brows, size, size), F32),
            pltpu.VMEM((width, size), F32),
            pltpu.SemaphoreType.DMA((2, brows)),
        ],
        compiler_params=pltpu.CompilerParams(vmem_limit_bytes=VMEM_LIMIT),
        cost_estimate=pl.CostEstimate(flops=6 * 10 * size * size * width, bytes_accessed=8 << 20, transcendentals=0),
        name="response",
    )(offsets, blocks, inverses)


def update_kernel(recv_ref, y_ref, cur_ref, gh_ref, gl_ref, out_ref, *, stage):
    out_ref[...] = cur_ref[...]

    @pl.when(lax.axis_index("row") == stage)
    def _():
        out_ref[...] = y_ref[...] - three(nn, stacked(recv_ref[...]), gh_ref[...], gl_ref[...])


def update(recv, y, cur, gain, stage):
    return pl.pallas_call(
        functools.partial(update_kernel, stage=stage),
        out_shape=jax.ShapeDtypeStruct(y.shape, F32),
        compiler_params=pltpu.CompilerParams(vmem_limit_bytes=VMEM_LIMIT),
        name="update",
    )(recv, y, cur, *gain)


def gram_kernel(*refs, start, fused, clear, last):
    recv_ref, y_ref = refs[:2]
    refs = refs[2:]
    if fused:
        gh_ref, gl_ref = refs[:2]
        refs = refs[2:]
    if start:
        oldh_ref, oldl_ref = refs[:2]
        refs = refs[2:]
    piece = refs[0]
    n, _ = recv_ref.shape
    here = slice(start, start + n)

    @pl.when(lax.axis_index("row") > 0)
    def _():
        recv = stacked(recv_ref[...])
        x = y_ref[...]
        if fused:
            x = x - three(nn, recv, gh_ref[...], gl_ref[...])
        x = stacked(x)
        high = jnp.concatenate([recv[:n], x[:n]], axis=1)
        low = jnp.concatenate([recv[n:], x[n:]], axis=1)
        both = jnp.concatenate([high, low], axis=0)
        if start:
            piece[:, :start] = three(nn, both, oldh_ref[:, :start], oldl_ref[:, :start])
        piece[:, here] = three(nt, both, high, low)
        if not last:
            refs[1][:, here] = high.T
            refs[2][:, here] = low.T

    if clear:

        @pl.when(lax.axis_index("row") == 0)
        def _():
            piece[...] = jnp.zeros_like(piece)


def gram(recv, y, gain, kept, start, total, clear):
    n, half = y.shape
    last = start + n == total
    fused = bool(gain)
    vmem = pl.BlockSpec(memory_space=pltpu.VMEM)
    inputs = [recv, y, *gain, *kept]
    results = pl.pallas_call(
        functools.partial(gram_kernel, start=start, fused=fused, clear=clear, last=last),
        in_specs=[vmem] * len(inputs),
        out_shape=[jax.ShapeDtypeStruct((n, start + n), F32)]
        + ([] if last else [jax.ShapeDtypeStruct((2 * half, total), BF16)] * 2),
        input_output_aliases={len(inputs) - 2 + i: 1 + i for i in range(2)} if start and not last else {},
        compiler_params=pltpu.CompilerParams(vmem_limit_bytes=VMEM_LIMIT),
        cost_estimate=pl.CostEstimate(
            flops=6 * n * half * (half + 2 * (start + n)), bytes_accessed=4 << 20, transcendentals=0
        ),
    )(*inputs)
    return results[0], list(results[1:])


def fill(out, chunks, part, tile, low_tile):
    share = out.shape[1]
    low, high = part * share, (part + 1) * share
    base = low_tile * tile
    for start, piece in chunks:
        n = piece.shape[0]
        at, inner = start // tile, start % tile
        first, stop = max(inner, low), min(inner + n, high)
        if first < stop:
            out[at - low_tile, first - low : stop - low, : start + n - base] = piece[first - inner : stop - inner, base:]
        if start > base:
            turned = piece[:, base:start].T
            for t in range(low_tile, -(-start // tile)):
                first, stop = t * tile + low, min(t * tile + high, start)
                if first < stop:
                    out[t - low_tile, : stop - first, start - base : start - base + n] = turned[
                        first - base : stop - base
                    ]


def fill_mine(out, starts, pieces, parts, tile, low_tile):
    row = lax.axis_index("row")
    both = len(pieces) > len(starts)
    for part in range(parts):
        mine = pieces[len(starts) :] if both and part else pieces[: len(starts)]
        pl.when(row == part)(functools.partial(fill, out, list(zip(starts, mine)), part, tile, low_tile))


def pair_kernel(*refs, starts, parts, tile, low_tile):
    fill_mine(refs[-1], starts, refs[:-1], parts, tile, low_tile)


def pair(pieces, starts, parts, tile, share, low_tile):
    return pl.pallas_call(
        functools.partial(pair_kernel, starts=starts, parts=parts, tile=tile, low_tile=low_tile),
        out_shape=jax.ShapeDtypeStruct((PAIR, share, PAIR * tile), F32),
        compiler_params=pltpu.CompilerParams(vmem_limit_bytes=VMEM_LIMIT),
    )(*pieces)


def subtract_halo(ids, out, halo, other, low_tile):
    count, total = ids.shape
    tile = halo.shape[2] // PAIR
    sub = lax.axis_index("sub")
    inside = jnp.logical_and(other >= 0, other < total)
    other = jnp.clip(other, 0, total - 1)
    order = ordered(ids, other)
    slots = []
    for m in range(PAIR):
        number = ids[order[low_tile + m], other]
        place, hit = jnp.int32(0), jnp.bool_(False)
        for i in range(count):
            same = ids[i, sub] == number
            place = jnp.where(same, jnp.int32(i), place)
            hit = jnp.logical_or(hit, same)
        slots.append((place, jnp.logical_and(hit, inside)))
    for m in range(PAIR):
        for n in range(PAIR):

            @pl.when(jnp.logical_and(slots[m][1], slots[n][1]))
            def _():
                at = pl.multiple_of(slots[n][0] * tile, tile)
                out[slots[m][0], :, pl.ds(at, tile)] -= halo[m, :, n * tile : (n + 1) * tile]


def middle_kernel(ids_ref, face_ref, halo_ref, *refs, starts, parts, tile):
    pieces, (out_ref, g) = refs[:-2], refs[-2:]
    fill_mine(g, starts, pieces, parts, tile, 0)
    out_ref[...] = face_ref[0]
    sub = lax.axis_index("sub")
    order = ordered(ids_ref, sub)
    for p in range(PAIR):
        for q in range(PAIR):
            at = pl.multiple_of(order[q] * tile, tile)
            out_ref[order[p], :, pl.ds(at, tile)] -= g[p, :, q * tile : (q + 1) * tile]
    subtract_halo(ids_ref, out_ref, halo_ref, far_of(sub), 0)


def rest_kernel(ids_ref, base_ref, *refs, starts, parts, tile):
    pieces, (out_ref, g) = refs[:-2], refs[-2:]
    count = base_ref.shape[0]
    fill_mine(g, starts, pieces, parts, tile, 0)
    out_ref[...] = base_ref[...]
    order = ordered(ids_ref, lax.axis_index("sub"))
    for p in range(count):
        for q in range(count):
            if p >= PAIR or q >= PAIR:
                at = pl.multiple_of(order[q] * tile, tile)
                out_ref[order[p], :, pl.ds(at, tile)] -= g[p, :, q * tile : (q + 1) * tile]


def finish_kernel(ids_ref, base_ref, halo_ref, out_ref, *, low_tile):
    out_ref[...] = base_ref[...]
    subtract_halo(ids_ref, out_ref, halo_ref, near_of(lax.axis_index("sub")), low_tile)


def assemble(kernel, ids, arrays, shape, scratch):
    smem = pl.BlockSpec(memory_space=pltpu.SMEM)
    vmem = pl.BlockSpec(memory_space=pltpu.VMEM)
    return pl.pallas_call(
        kernel,
        in_specs=[smem] + [vmem] * len(arrays),
        out_shape=jax.ShapeDtypeStruct(shape, F32),
        scratch_shapes=[pltpu.VMEM(scratch, F32)] if scratch else [],
        compiler_params=pltpu.CompilerParams(vmem_limit_bytes=VMEM_LIMIT),
    )(ids, *arrays)


def sizes(count, tile):
    short = tile // LAST
    return (tile,) * (count - 1) + (tile - short, short)


def shards(factor_blocks, block_inverses, band_offsets, coupling, interface_block, tile_ids):
    rows = lax.axis_size("row")
    subs = lax.axis_size("sub")
    _, count, share, cols = interface_block.shape
    tile = cols // count
    chunks = sizes(count, tile)
    starts = [sum(chunks[:c]) for c in range(len(chunks))]
    offsets = jnp.transpose(band_offsets, (2, 0, 1))
    ids = jnp.transpose(tile_ids)
    given = (offsets, ids, factor_blocks, block_inverses, coupling)
    far = [(s, s - 1 + 2 * (s % 2)) for s in range(subs)]
    near = [(s, s + 1 - 2 * (s % 2)) for s in range(subs)]
    far, near = ([(s, t) for s, t in pairs if 0 <= t < subs] for pairs in (far, near))
    early = solve(*given, chunks[:1], tile, True, ALONE)
    ys = solve(*given, chunks, tile, False, VMEM_LIMIT)
    gain = response(offsets, factor_blocks, block_inverses)
    xs, first, gain_now = early + ys[1:], None, gain if rows == 2 else ()
    for stage in range(1, rows):
        recv = []
        for x in xs:
            recv.append(lax.ppermute(x, "row", [(stage - 1, stage)]))
        first = first or recv
        if rows > 2:
            xs = [update(r, y, x, gain, stage) for r, y, x in zip(recv, ys, xs)]
    kept, own, got = [], [], []
    for c, start in enumerate(starts):
        piece, kept = gram(first[c], (ys if rows == 2 else xs)[c], gain_now, kept, start, cols, rows > 2)
        if rows == 2:
            got.append(lax.ppermute(piece, "row", [(1, 0)]))
            own.append(piece)
        else:
            got.append(lax.psum(piece, "row"))
    shape = (count, share, cols)
    last = count - PAIR

    def pick(low, high):
        return got[low:high] + own[low:high]

    message = pair(pick(0, PAIR), starts[:PAIR], rows, tile, share, 0)
    from_far = lax.ppermute(message, "sub", far)
    kernel = functools.partial(middle_kernel, starts=starts[:PAIR], parts=rows, tile=tile)
    base = assemble(kernel, ids, [interface_block, from_far] + pick(0, PAIR), shape, (PAIR, share, PAIR * tile))
    message = pair(pick(last, None), starts[last:], rows, tile, share, last)
    from_near = lax.ppermute(message, "sub", near)
    kernel = functools.partial(rest_kernel, starts=starts[PAIR:], parts=rows, tile=tile)
    base = assemble(kernel, ids, [base] + pick(PAIR, None), shape, shape)
    kernel = functools.partial(finish_kernel, low_tile=last)
    return assemble(kernel, ids, [base, from_near], shape, None)[None]


def solution(mesh):
    return jax.shard_map(
        shards,
        mesh=mesh,
        in_specs=(
            P("sub", "row", None, None, None),
            P("sub", "row", None, None),
            P("sub", "row", None),
            P("sub", "row", None),
            P("sub", None, "row", None),
            P(),
        ),
        out_specs=P("sub", None, "row", None),
        check_vma=False,
    )
```

time: 81.2 us -> 75.6 us (0.931)
  the two profiles are of different devices: /device:TPU:11 before, /device:TPU:9 now
where the time goes in v1:
time: 75.6 us; the launch traced here: 75.1 us
  waiting for transfers between devices  35.8 us (47%)
  starting transfers between devices  19.6 us (26%)
  Pallas kernels  14.7 us (19%)
  local copies, waits for them, and re-layouts  4.72 us (6%)
    ppermute x5, waiting for transfers between devices, shards(): recv.append(lax.ppermute(x, 'row', [(stage - 1, stage)]))  24.4 us
    pallas_call x2, Pallas kernels, solve(): pl.pallas_call(functools.partial(solve_kernel, chunks=chunks, tiles=tiles...  10.3 us
    ppermute x5, waiting for transfers between devices, shards(): got.append(lax.ppermute(piece, 'row', [(1, 0)]))  7.69 us
    ppermute x5, starting transfers between devices, shards(): recv.append(lax.ppermute(x, 'row', [(stage - 1, stage)]))  6.58 us
    ppermute x5, starting transfers between devices, shards(): got.append(lax.ppermute(piece, 'row', [(1, 0)]))  6.57 us
    ppermute x1, starting transfers between devices, shards(): from_far = lax.ppermute(message, 'sub', far)  6.37 us
    unnamed x14, local copies, waits for them, and re-layouts  4.72 us
    ppermute x1, waiting for transfers between devices, shards(): from_far = lax.ppermute(message, 'sub', far)  3.75 us
  transfers between devices with their start and end apart: 12, of which 5 were waited for; matrix products, arithmetic and copies ran while one was open for 0% of the time, Pallas kernels for 11%

profile of v1, /device:TPU:9, one launch (start us, length us, event | category | flops | bytes accessed | tf_op | source)
XLA Modules:
  0.0 75.1 jit_solution(15509087540649672657)
XLA Ops:
  0.0 4.8 %shard_map.64 = f32[128,1024]{1,0:T(8,128)} custom-call(s32[3,1,4]{2,1,0:T(1,128)} %bitcast.8, s32[4,16]{1,0:T(4,128)} %bitcast.3, f32[1,4,3,256,256]{4,3,2,1,0:T(8,128)} %f_hbm.5, f32[1,4,256,256]{3,2,1,0:T(8,128)} %inv_hbm.5, f32[1,1024,512]{2,1,0:T(8,128)} %b_hbm.3), custom_call_target="tpu_custom_call" | custom-call | flops 503316480 | bytes 8388608 | tf_op jit(solution)/shard_map/pallas_call | solution.py:146
  4.8 1.3 %collective-permute-start = (f32[128,1024]{1,0:T(8,128)}, f32[128,1024]{1,0:T(8,128)S(1)}, u32[]{:S(2)}, u32[]{:S(2)}) collective-permute-start(f32[128,1024]{1,0:T(8,128)} %shard_map.64), channel_id=1, source_target_pairs={{0,1},{2,3},{4,5},{6,7},{8,9},{10,11},{12,13},{14,15},{16,17},{18,... | collective-permute-start | bytes 1572872 | tf_op jit(solution)/shard_map/ppermute | solution.py:423
  6.2 0.0 copy-start
  6.2 1.9 %copy-done = f32[1,4,3,256,256]{4,3,2,1,0:T(8,128)S(1)} copy-done((f32[1,4,3,256,256]{4,3,2,1,0:T(8,128)S(1)}, f32[1,4,3,256,256]{4,3,2,1,0:T(8,128)}, u32[]{:S(2)}) %copy-start) | copy-done | bytes 3145752
  8.1 1.6 %copy-done.2 = f32[1,1024,512]{2,1,0:T(8,128)S(1)} copy-done((f32[1,1024,512]{2,1,0:T(8,128)S(1)}, f32[1,1024,512]{2,1,0:T(8,128)}, u32[]{:S(2)}) %copy-start.2) | copy-done | bytes 2097176
  9.7 1.2 %copy-done.3 = f32[1,4,256,256]{3,2,1,0:T(8,128)S(1)} copy-done((f32[1,4,256,256]{3,2,1,0:T(8,128)S(1)}, f32[1,4,256,256]{3,2,1,0:T(8,128)}, u32[]{:S(2)}) %copy-start.3) | copy-done | bytes 1048600
  10.9 5.5 %shard_map.65 = (f32[128,1024]{1,0:T(8,128)S(1)}, f32[128,1024]{1,0:T(8,128)S(1)}, f32[128,1024]{1,0:T(8,128)S(1)}, f32[96,1024]{1,0:T(8,128)S(1)}, f32[32,1024]{1,0:T(8,128)S(1)}) custom-call(s32[3,1,4]{2,1,0:T(1,128)S(1)} %bitcast.9, s32[4,16]{1,0:T(4,128)S(1)} %bitcast.4, f32[1,4,3,256,256]{4,3,2,1,0:T(8,128)S(1)} %copy-done, ...), custom_call_target="tpu_custom_call" | custom-call | flops 2013265920 | bytes 8388608 | tf_op jit(solution)/shard_map/pallas_call | solution.py:146
  16.4 1.3 %collective-permute-start.2 = (f32[128,1024]{1,0:T(8,128)S(1)}, f32[128,1024]{1,0:T(8,128)S(1)}, u32[]{:S(2)}, u32[]{:S(2)}) collective-permute-start(f32[128,1024]{1,0:T(8,128)S(1)} %get-tuple-element.28.refs_1_), channel_id=1, source_target_pairs={{0,1},{2,3},{4,5},{6,7},{8,9},{10,11},{12,13},{14,15},{16,17},{18,... | collective-permute-start | bytes 1572872 | tf_op jit(solution)/shard_map/ppermute | solution.py:423
  17.7 1.3 %collective-permute-start.5 = (f32[128,1024]{1,0:T(8,128)S(1)}, f32[128,1024]{1,0:T(8,128)S(1)}, u32[]{:S(2)}, u32[]{:S(2)}) collective-permute-start(f32[128,1024]{1,0:T(8,128)S(1)} %get-tuple-element.32.refs_1_), channel_id=1, source_target_pairs={{0,1},{2,3},{4,5},{6,7},{8,9},{10,11},{12,13},{14,15},{16,17},{18,... | collective-permute-start | bytes 1572872 | tf_op jit(solution)/shard_map/ppermute | solution.py:423
  19.1 1.3 %collective-permute-start.7 = (f32[96,1024]{1,0:T(8,128)S(1)}, f32[96,1024]{1,0:T(8,128)S(1)}, u32[]{:S(2)}, u32[]{:S(2)}) collective-permute-start(f32[96,1024]{1,0:T(8,128)S(1)} %get-tuple-element.36.refs_1_), channel_id=1, source_target_pairs={{0,1},{2,3},{4,5},{6,7},{8,9},{10,11},{12,13},{14,15},{16,17},{18,... | collective-permute-start | bytes 1179656 | tf_op jit(solution)/shard_map/ppermute | solution.py:423
  20.4 1.3 %collective-permute-start.9 = (f32[32,1024]{1,0:T(8,128)S(1)}, f32[32,1024]{1,0:T(8,128)S(1)}, u32[]{:S(2)}, u32[]{:S(2)}) collective-permute-start(f32[32,1024]{1,0:T(8,128)S(1)} %get-tuple-element.40.refs_1_), channel_id=1, source_target_pairs={{0,1},{2,3},{4,5},{6,7},{8,9},{10,11},{12,13},{14,15},{16,17},{18,... | collective-permute-start | bytes 393224 | tf_op jit(solution)/shard_map/ppermute | solution.py:423
  21.7 0.6 response.1
  22.4 0.2 shard_map.66
  22.6 6.0 %collective-permute-done.2.refs_0_ = f32[128,1024]{1,0:T(8,128)S(1)} collective-permute-done((f32[128,1024]{1,0:T(8,128)S(1)}, f32[128,1024]{1,0:T(8,128)S(1)}, u32[]{:S(2)}, u32[]{:S(2)}) %collective-permute-start.2) | collective-permute-done | bytes 524320 | tf_op jit(solution)/shard_map/ppermute | solution.py:423
  28.6 11.2 %collective-permute-done.5.refs_0_ = f32[128,1024]{1,0:T(8,128)S(1)} collective-permute-done((f32[128,1024]{1,0:T(8,128)S(1)}, f32[128,1024]{1,0:T(8,128)S(1)}, u32[]{:S(2)}, u32[]{:S(2)}) %collective-permute-start.5) | collective-permute-done | bytes 524320 | tf_op jit(solution)/shard_map/ppermute | solution.py:423
  39.8 1.3 %collective-permute-start.6 = (f32[128,384]{1,0:T(8,128)S(1)}, f32[128,384]{1,0:T(8,128)S(1)}, u32[]{:S(2)}, u32[]{:S(2)}) collective-permute-start(f32[128,384]{1,0:T(8,128)S(1)} %get-tuple-element.35.refs_3_), channel_id=1, source_target_pairs={{1,0},{3,2},{5,4},{7,6},{9,8},{11,10},{13,12},{15,14},{17,16},{19,... | collective-permute-start | bytes 589832 | tf_op jit(solution)/shard_map/ppermute | solution.py:431
  41.1 7.1 %collective-permute-done.7.refs_0_ = f32[96,1024]{1,0:T(8,128)S(1)} collective-permute-done((f32[96,1024]{1,0:T(8,128)S(1)}, f32[96,1024]{1,0:T(8,128)S(1)}, u32[]{:S(2)}, u32[]{:S(2)}) %collective-permute-start.7) | collective-permute-done | bytes 393248 | tf_op jit(solution)/shard_map/ppermute | solution.py:423
  48.2 1.3 %collective-permute-start.8 = (f32[96,480]{1,0:T(8,128)S(1)}, f32[96,480]{1,0:T(8,128)S(1)}, u32[]{:S(2)}, u32[]{:S(2)}) collective-permute-start(f32[96,480]{1,0:T(8,128)S(1)} %get-tuple-element.39.refs_4_), channel_id=1, source_target_pairs={{1,0},{3,2},{5,4},{7,6},{9,8},{11,10},{13,12},{15,14},{17,16},{19,... | collective-permute-start | bytes 552968 | tf_op jit(solution)/shard_map/ppermute | solution.py:431
  49.5 1.3 %collective-permute-start.3 = (f32[128,256]{1,0:T(8,128)S(1)}, f32[128,256]{1,0:T(8,128)S(1)}, u32[]{:S(2)}, u32[]{:S(2)}) collective-permute-start(f32[128,256]{1,0:T(8,128)S(1)} %get-tuple-element.31.refs_3_), channel_id=1, source_target_pairs={{1,0},{3,2},{5,4},{7,6},{9,8},{11,10},{13,12},{15,14},{17,16},{19,... | collective-permute-start | bytes 393224 | tf_op jit(solution)/shard_map/ppermute | solution.py:431
  50.8 1.3 %collective-permute-start.1 = (f32[128,128]{1,0:T(8,128)S(1)}, f32[128,128]{1,0:T(8,128)S(1)}, u32[]{:S(2)}, u32[]{:S(2)}) collective-permute-start(f32[128,128]{1,0:T(8,128)S(1)} %get-tuple-element.27.refs_2_), channel_id=1, source_target_pairs={{1,0},{3,2},{5,4},{7,6},{9,8},{11,10},{13,12},{15,14},{17,16},{19,... | collective-permute-start | bytes 196616 | tf_op jit(solution)/shard_map/ppermute | solution.py:431
  52.1 0.0 collective-permute-done.9.refs_0_
  52.1 0.0 copy-start.4
  52.2 1.4 %collective-permute-start.10 = (f32[32,512]{1,0:T(8,128)S(1)}, f32[32,512]{1,0:T(8,128)S(1)}, u32[]{:S(2)}, u32[]{:S(2)}) collective-permute-start(f32[32,512]{1,0:T(8,128)S(1)} %shard_map.72.refs_5_), channel_id=1, source_target_pairs={{1,0},{3,2},{5,4},{7,6},{9,8},{11,10},{13,12},{15,14},{17,16},{19,... | collective-permute-start | bytes 196616 | tf_op jit(solution)/shard_map/ppermute | solution.py:431
  53.6 7.7 %collective-permute-done.1.refs_0_ = f32[128,128]{1,0:T(8,128)S(1)} collective-permute-done((f32[128,128]{1,0:T(8,128)S(1)}, f32[128,128]{1,0:T(8,128)S(1)}, u32[]{:S(2)}, u32[]{:S(2)}) %collective-permute-start.1) | collective-permute-done | bytes 65568 | tf_op jit(solution)/shard_map/ppermute | solution.py:431
  61.3 0.1 shard_map.68
  61.3 6.4 %collective-permute-start.4 = (f32[2,64,256]{2,1,0:T(8,128)S(1)}, f32[2,64,256]{2,1,0:T(8,128)S(1)}, u32[]{:S(2)}, u32[]{:S(2)}) collective-permute-start(f32[2,64,256]{2,1,0:T(8,128)S(1)} %shard_map.68), channel_id=1, source_target_pairs={{2,4},{4,2},{6,8},{8,6},{10,12},{12,10},{14,16},{16,14},{18,20},{2... | collective-permute-start | bytes 393224 | tf_op jit(solution)/shard_map/ppermute | solution.py:442
  67.8 0.2 shard_map.74
  67.9 0.1 collective-permute-start.11
  68.0 3.8 %collective-permute-done.4.halo_ref = f32[2,64,256]{2,1,0:T(8,128)S(1)} collective-permute-done((f32[2,64,256]{2,1,0:T(8,128)S(1)}, f32[2,64,256]{2,1,0:T(8,128)S(1)}, u32[]{:S(2)}, u32[]{:S(2)}) %collective-permute-start.4) | collective-permute-done | bytes 131104 | tf_op jit(solution)/shard_map/ppermute | solution.py:442
  71.8 0.8 %shard_map.69.base_ref = f32[4,64,512]{2,1,0:T(8,128)S(1)} custom-call(s32[4,16]{1,0:T(4,128)S(1)} %bitcast.5, f32[1,4,64,512]{3,2,1,0:T(8,128)S(1)} %copy-done.4, f32[2,64,256]{2,1,0:T(8,128)S(1)} %collective-permute-done.4.halo_ref, f32[128,128]{1,0:T(8,128)S(1)} %collective-permute-done.1.refs_0_, f32[128,256]{1,0:T(8,128)S(1)} %collective-permute-done.3.refs_1_, ...), custom_call_target="tpu_custom_call" | custom-call | tf_op jit(solution)/shard_map/pallas_call | solution.py:389
  72.6 1.0 %shard_map.73.base_ref = f32[4,64,512]{2,1,0:T(8,128)S(1)} custom-call(s32[4,16]{1,0:T(4,128)S(1)} %bitcast.6, f32[4,64,512]{2,1,0:T(8,128)S(1)} %shard_map.69.base_ref, f32[128,384]{1,0:T(8,128)S(1)} %collective-permute-done.6.refs_0_, f32[96,480]{1,0:T(8,128)S(1)} %collective-permute-done.8.refs_1_, f32[32,512]{1,0:T(8,128)S(1)} %collective-permute-done.10.refs_2_, ...), custom_call_target="tpu_custom_call" | custom-call | tf_op jit(solution)/shard_map/pallas_call | solution.py:389
  73.6 1.5 %shard_map.75 = f32[4,64,512]{2,1,0:T(8,128)} custom-call(s32[4,16]{1,0:T(4,128)S(1)} %bitcast.7, f32[4,64,512]{2,1,0:T(8,128)S(1)} %shard_map.73.base_ref, f32[2,64,256]{2,1,0:T(8,128)S(1)} %collective-permute-done.11.halo_ref), custom_call_target="tpu_custom_call" | custom-call | tf_op jit(solution)/shard_map/pallas_call | solution.py:389
  (19 shorter events, 0.0 us)
Async XLA Ops:
  0.0 6.2 %copy-start.5 = (s32[16,4]{0,1:T(4,128)S(1)}, s32[16,4]{0,1:T(4,128)}, u32[]{:S(2)}) copy-start(s32[16,4]{0,1:T(4,128)} %param.11) | copy-start | bytes 772
  0.0 6.2 %copy-start.6 = (s32[1,4,3]{1,0,2:T(1,128)S(1)}, s32[1,4,3]{1,0,2:T(1,128)}, u32[]{:S(2)}) copy-start(s32[1,4,3]{1,0,2:T(1,128)} %param.8) | copy-start | bytes 148
  4.8 17.5 %collective-permute-start = (f32[128,1024]{1,0:T(8,128)}, f32[128,1024]{1,0:T(8,128)S(1)}, u32[]{:S(2)}, u32[]{:S(2)}) collective-permute-start(f32[128,1024]{1,0:T(8,128)} %shard_map.64), channel_id=1, source_target_pairs={{0,1},{2,3},{4,5},{6,7},{8,9},{10,11},{12,13},{14,15},{16,17},{18,... | collective-permute-start | bytes 1572872 | tf_op jit(solution)/shard_map/ppermute | solution.py:423
  6.2 1.9 %copy-start = (f32[1,4,3,256,256]{4,3,2,1,0:T(8,128)S(1)}, f32[1,4,3,256,256]{4,3,2,1,0:T(8,128)}, u32[]{:S(2)}) copy-start(f32[1,4,3,256,256]{4,3,2,1,0:T(8,128)} %f_hbm.5) | copy-start | bytes 9437188
  8.1 1.6 %copy-start.2 = (f32[1,1024,512]{2,1,0:T(8,128)S(1)}, f32[1,1024,512]{2,1,0:T(8,128)}, u32[]{:S(2)}) copy-start(f32[1,1024,512]{2,1,0:T(8,128)} %b_hbm.3) | copy-start | bytes 6291460
  9.7 1.2 %copy-start.3 = (f32[1,4,256,256]{3,2,1,0:T(8,128)S(1)}, f32[1,4,256,256]{3,2,1,0:T(8,128)}, u32[]{:S(2)}) copy-start(f32[1,4,256,256]{3,2,1,0:T(8,128)} %inv_hbm.5) | copy-start | bytes 3145732
  10.9 10.8 %copy-start.1 = (f32[1,4,3,256,256]{4,3,2,1,0:T(8,128)S(1)}, f32[1,4,3,256,256]{4,3,2,1,0:T(8,128)}, u32[]{:S(2)}) copy-start(f32[1,4,3,256,256]{4,3,2,1,0:T(8,128)} %f_hbm.5) | copy-start | bytes 9437188
  16.4 12.2 %collective-permute-start.2 = (f32[128,1024]{1,0:T(8,128)S(1)}, f32[128,1024]{1,0:T(8,128)S(1)}, u32[]{:S(2)}, u32[]{:S(2)}) collective-permute-start(f32[128,1024]{1,0:T(8,128)S(1)} %get-tuple-element.28.refs_1_), channel_id=1, source_target_pairs={{0,1},{2,3},{4,5},{6,7},{8,9},{10,11},{12,13},{14,15},{16,17},{18,... | collective-permute-start | bytes 1572872 | tf_op jit(solution)/shard_map/ppermute | solution.py:423
  17.7 22.1 %collective-permute-start.5 = (f32[128,1024]{1,0:T(8,128)S(1)}, f32[128,1024]{1,0:T(8,128)S(1)}, u32[]{:S(2)}, u32[]{:S(2)}) collective-permute-start(f32[128,1024]{1,0:T(8,128)S(1)} %get-tuple-element.32.refs_1_), channel_id=1, source_target_pairs={{0,1},{2,3},{4,5},{6,7},{8,9},{10,11},{12,13},{14,15},{16,17},{18,... | collective-permute-start | bytes 1572872 | tf_op jit(solution)/shard_map/ppermute | solution.py:423
  19.1 29.2 %collective-permute-start.7 = (f32[96,1024]{1,0:T(8,128)S(1)}, f32[96,1024]{1,0:T(8,128)S(1)}, u32[]{:S(2)}, u32[]{:S(2)}) collective-permute-start(f32[96,1024]{1,0:T(8,128)S(1)} %get-tuple-element.36.refs_1_), channel_id=1, source_target_pairs={{0,1},{2,3},{4,5},{6,7},{8,9},{10,11},{12,13},{14,15},{16,17},{18,... | collective-permute-start | bytes 1179656 | tf_op jit(solution)/shard_map/ppermute | solution.py:423
  20.4 31.7 %collective-permute-start.9 = (f32[32,1024]{1,0:T(8,128)S(1)}, f32[32,1024]{1,0:T(8,128)S(1)}, u32[]{:S(2)}, u32[]{:S(2)}) collective-permute-start(f32[32,1024]{1,0:T(8,128)S(1)} %get-tuple-element.40.refs_1_), channel_id=1, source_target_pairs={{0,1},{2,3},{4,5},{6,7},{8,9},{10,11},{12,13},{14,15},{16,17},{18,... | collective-permute-start | bytes 393224 | tf_op jit(solution)/shard_map/ppermute | solution.py:423
  39.8 27.9 %collective-permute-start.6 = (f32[128,384]{1,0:T(8,128)S(1)}, f32[128,384]{1,0:T(8,128)S(1)}, u32[]{:S(2)}, u32[]{:S(2)}) collective-permute-start(f32[128,384]{1,0:T(8,128)S(1)} %get-tuple-element.35.refs_3_), channel_id=1, source_target_pairs={{1,0},{3,2},{5,4},{7,6},{9,8},{11,10},{13,12},{15,14},{17,16},{19,... | collective-permute-start | bytes 589832 | tf_op jit(solution)/shard_map/ppermute | solution.py:431
  48.2 19.5 %collective-permute-start.8 = (f32[96,480]{1,0:T(8,128)S(1)}, f32[96,480]{1,0:T(8,128)S(1)}, u32[]{:S(2)}, u32[]{:S(2)}) collective-permute-start(f32[96,480]{1,0:T(8,128)S(1)} %get-tuple-element.39.refs_4_), channel_id=1, source_target_pairs={{1,0},{3,2},{5,4},{7,6},{9,8},{11,10},{13,12},{15,14},{17,16},{19,... | collective-permute-start | bytes 552968 | tf_op jit(solution)/shard_map/ppermute | solution.py:431
  49.5 11.8 %collective-permute-start.3 = (f32[128,256]{1,0:T(8,128)S(1)}, f32[128,256]{1,0:T(8,128)S(1)}, u32[]{:S(2)}, u32[]{:S(2)}) collective-permute-start(f32[128,256]{1,0:T(8,128)S(1)} %get-tuple-element.31.refs_3_), channel_id=1, source_target_pairs={{1,0},{3,2},{5,4},{7,6},{9,8},{11,10},{13,12},{15,14},{17,16},{19,... | collective-permute-start | bytes 393224 | tf_op jit(solution)/shard_map/ppermute | solution.py:431
  50.8 10.5 %collective-permute-start.1 = (f32[128,128]{1,0:T(8,128)S(1)}, f32[128,128]{1,0:T(8,128)S(1)}, u32[]{:S(2)}, u32[]{:S(2)}) collective-permute-start(f32[128,128]{1,0:T(8,128)S(1)} %get-tuple-element.27.refs_2_), channel_id=1, source_target_pairs={{1,0},{3,2},{5,4},{7,6},{9,8},{11,10},{13,12},{15,14},{17,16},{19,... | collective-permute-start | bytes 196616 | tf_op jit(solution)/shard_map/ppermute | solution.py:431
  52.1 19.6 %copy-start.4 = (f32[1,4,64,512]{3,2,1,0:T(8,128)S(1)}, f32[1,4,64,512]{3,2,1,0:T(8,128)}, u32[]{:S(2)}) copy-start(f32[1,4,64,512]{3,2,1,0:T(8,128)} %face_ref.1) | copy-start | bytes 1572868
  52.2 15.6 %collective-permute-start.10 = (f32[32,512]{1,0:T(8,128)S(1)}, f32[32,512]{1,0:T(8,128)S(1)}, u32[]{:S(2)}, u32[]{:S(2)}) collective-permute-start(f32[32,512]{1,0:T(8,128)S(1)} %shard_map.72.refs_5_), channel_id=1, source_target_pairs={{1,0},{3,2},{5,4},{7,6},{9,8},{11,10},{13,12},{15,14},{17,16},{19,... | collective-permute-start | bytes 196616 | tf_op jit(solution)/shard_map/ppermute | solution.py:431
  61.3 10.4 %collective-permute-start.4 = (f32[2,64,256]{2,1,0:T(8,128)S(1)}, f32[2,64,256]{2,1,0:T(8,128)S(1)}, u32[]{:S(2)}, u32[]{:S(2)}) collective-permute-start(f32[2,64,256]{2,1,0:T(8,128)S(1)} %shard_map.68), channel_id=1, source_target_pairs={{2,4},{4,2},{6,8},{8,6},{10,12},{12,10},{14,16},{16,14},{18,20},{2... | collective-permute-start | bytes 393224 | tf_op jit(solution)/shard_map/ppermute | solution.py:442
  67.9 5.7 %collective-permute-start.11 = (f32[2,64,256]{2,1,0:T(8,128)S(1)}, f32[2,64,256]{2,1,0:T(8,128)S(1)}, u32[]{:S(2)}, u32[]{:S(2)}) collective-permute-start(f32[2,64,256]{2,1,0:T(8,128)S(1)} %shard_map.74), channel_id=1, source_target_pairs={{0,2},{2,0},{4,6},{6,4},{8,10},{10,8},{12,14},{14,12},{16,18},{18,... | collective-permute-start | bytes 393224 | tf_op jit(solution)/shard_map/ppermute | solution.py:446

commit v2 on v1

--- a/solution.py
+++ b/solution.py
@@ -11,9 +11,10 @@
 F32 = jnp.float32
 BF16 = jnp.bfloat16
 VMEM_LIMIT = 24 * 1024 * 1024
+OTHERS = 24 * 1024 * 1024
 ALONE = 63 * 1024 * 1024
 PAIR = 2
-LAST = 4
+LAST = (3, 8)
 
 
 def split(x):
@@ -94,67 +95,108 @@
         finish(i, x)
 
 
-def solve_kernel(off_ref, ids_ref, f_hbm, inv_hbm, b_hbm, *rest, chunks, tiles, first_only):
+def early_kernel(ids_hbm, inv_hbm, b_hbm, out, ids_ref, inverse, b, x_ref, sems):
+    @pl.when(lax.axis_index("row") == 0)
+    def _():
+        size = inverse.shape[0]
+        copies = [
+            pltpu.make_async_copy(inv_hbm.at[0, 0], inverse, sems.at[0]),
+            pltpu.make_async_copy(b_hbm.at[0, pl.ds(0, size)], b, sems.at[1]),
+            pltpu.make_async_copy(ids_hbm, ids_ref, sems.at[2]),
+        ]
+        for copy in copies:
+            copy.start()
+        copies[1].wait()
+        right = stacked(b[...].T)
+        copies[0].wait()
+        x_ref[...] = three(nt, right, *split(inverse[...]))
+        copies[2].wait()
+        order = ordered(ids_ref, lax.axis_index("sub"))
+        tile = x_ref.shape[0] // len(order)
+        for p, k in enumerate(order):
+            out[p * tile : (p + 1) * tile] = x_ref[pl.ds(pl.multiple_of(k * tile, tile), tile)]
+
+
+def early_solve(ids, inverses, coupling):
+    size, cols = inverses.shape[2], coupling.shape[2]
+    hbm = pl.BlockSpec(memory_space=pltpu.HBM)
+    return pl.pallas_call(
+        early_kernel,
+        in_specs=[hbm] * 3,
+        out_shape=jax.ShapeDtypeStruct((cols, size), F32),
+        scratch_shapes=[
+            pltpu.SMEM(ids.shape, jnp.int32),
+            pltpu.VMEM((size, size), F32),
+            pltpu.VMEM((size, cols), F32),
+            pltpu.VMEM((cols, size), F32),
+            pltpu.SemaphoreType.DMA((3,)),
+        ],
+        compiler_params=pltpu.CompilerParams(vmem_limit_bytes=ALONE),
+        cost_estimate=pl.CostEstimate(flops=6 * size * size * cols, bytes_accessed=1 << 20, transcendentals=0),
+        name="early",
+    )(ids, inverses, coupling)
+
+
+def solve_kernel(off_ref, ids_ref, f_hbm, inv_hbm, b_hbm, top, *rest, chunks, tiles):
     outs, (f, inverse, b, sems) = rest[: len(chunks)], rest[len(chunks) :]
     brows, _, size, _ = f.shape
     tile = b.shape[2] // tiles
 
-    def run():
-        order = ordered(ids_ref, lax.axis_index("sub"))
-        copies = []
-        for i in range(brows):
-            group = [pltpu.make_async_copy(inv_hbm.at[0, i], inverse.at[i], sems.at[0, i])]
-            for p in range(tiles):
-                columns = pl.ds(pl.multiple_of(order[p] * tile, tile), tile)
-                group.append(
-                    pltpu.make_async_copy(
-                        b_hbm.at[0, pl.ds(i * size, size), columns],
-                        b.at[i, :, pl.ds(p * tile, tile)],
-                        sems.at[2 + p, i],
-                    )
+    order = ordered(ids_ref, lax.axis_index("sub"))
+    copies = []
+    for i in range(brows):
+        group = [pltpu.make_async_copy(inv_hbm.at[0, i], inverse.at[i], sems.at[0, i])]
+        for p in range(tiles):
+            columns = pl.ds(pl.multiple_of(order[p] * tile, tile), tile)
+            group.append(
+                pltpu.make_async_copy(
+                    b_hbm.at[0, pl.ds(i * size, size), columns],
+                    b.at[i, :, pl.ds(p * tile, tile)],
+                    sems.at[2 + p, i],
                 )
-            if i > 0:
-                group.append(pltpu.make_async_copy(f_hbm.at[0, i], f.at[i], sems.at[1, i]))
-            for copy in group:
-                copy.start()
-            copies.append(group)
-
-        def begin(i):
-            wait_all(copies[i])
-            return b[i].T
-
-        def finish(i, x):
-            start = 0
-            for out, n in zip(outs, chunks):
-                out[:, i * size : (i + 1) * size] = x[start : start + n]
-                start += n
-
-        substitute(off_ref, f, inverse, begin, finish)
-
-    if first_only:
-        pl.when(lax.axis_index("row") == 0)(run)
-    else:
-        run()
-
-
-def solve(offsets, ids, blocks, inverses, coupling, chunks, tile, first_only, limit):
+            )
+        if i > 0:
+            group.append(pltpu.make_async_copy(f_hbm.at[0, i], f.at[i], sems.at[1, i]))
+        for copy in group:
+            copy.start()
+        copies.append(group)
+
+    def begin(i):
+        wait_all(copies[i])
+        return b[i].T
+
+    def finish(i, x):
+        if i == 0:
+            top[...] = x
+            return
+        start = 0
+        for out, n in zip(outs, chunks):
+            out[:, (i - 1) * size : i * size] = x[start : start + n]
+            start += n
+
+    substitute(off_ref, f, inverse, begin, finish)
+
+
+def solve(offsets, ids, blocks, inverses, coupling, chunks, tile):
     _, brows, kband, size, _ = blocks.shape
     total = sum(chunks)
     tiles = total // tile
     hbm = pl.BlockSpec(memory_space=pltpu.HBM)
     smem = pl.BlockSpec(memory_space=pltpu.SMEM)
     return pl.pallas_call(
-        functools.partial(solve_kernel, chunks=chunks, tiles=tiles, first_only=first_only),
+        functools.partial(solve_kernel, chunks=chunks, tiles=tiles),
         in_specs=[smem, smem, hbm, hbm, hbm],
-        out_shape=[jax.ShapeDtypeStruct((n, brows * size), F32) for n in chunks],
+        out_shape=[jax.ShapeDtypeStruct((total, size), F32)]
+        + [jax.ShapeDtypeStruct((n, (brows - 1) * size), F32) for n in chunks],
         scratch_shapes=[
             pltpu.VMEM((brows, kband, size, size), F32),
             pltpu.VMEM((brows, size, size), F32),
             pltpu.VMEM((brows, size, total), F32),
             pltpu.SemaphoreType.DMA((2 + tiles, brows)),
         ],
-        compiler_params=pltpu.CompilerParams(vmem_limit_bytes=limit),
+        compiler_params=pltpu.CompilerParams(vmem_limit_bytes=OTHERS),
         cost_estimate=pl.CostEstimate(flops=6 * 10 * size * size * total, bytes_accessed=8 << 20, transcendentals=0),
+        name="others",
     )(offsets, ids, blocks, inverses, coupling)
 
 
@@ -213,40 +255,52 @@
     )(offsets, blocks, inverses)
 
 
-def update_kernel(recv_ref, y_ref, cur_ref, gh_ref, gl_ref, out_ref, *, stage):
-    out_ref[...] = cur_ref[...]
+def update_kernel(*refs, chunks, stage):
+    gh_ref, gl_ref = refs[:2]
+    width = 1 + len(chunks)
+    recv, y, cur, out = (refs[2 + k * width : 2 + (k + 1) * width] for k in range(4))
+    for source, target in zip(cur, out):
+        target[...] = source[...]
 
     @pl.when(lax.axis_index("row") == stage)
     def _():
-        out_ref[...] = y_ref[...] - three(nn, stacked(recv_ref[...]), gh_ref[...], gl_ref[...])
-
-
-def update(recv, y, cur, gain, stage):
+        size = recv[0].shape[1]
+        start = 0
+        for c, n in enumerate(chunks):
+            rows = slice(start, start + n)
+            given = jnp.concatenate([recv[0][rows], recv[1 + c][...]], axis=1)
+            change = three(nn, stacked(given), gh_ref[...], gl_ref[...])
+            out[0][rows] = y[0][rows] - change[:, :size]
+            out[1 + c][...] = y[1 + c][...] - change[:, size:]
+            start += n
+
+
+def update(recv, y, cur, gain, chunks, stage):
     return pl.pallas_call(
-        functools.partial(update_kernel, stage=stage),
-        out_shape=jax.ShapeDtypeStruct(y.shape, F32),
+        functools.partial(update_kernel, chunks=chunks, stage=stage),
+        out_shape=[jax.ShapeDtypeStruct(x.shape, F32) for x in y],
         compiler_params=pltpu.CompilerParams(vmem_limit_bytes=VMEM_LIMIT),
         name="update",
-    )(recv, y, cur, *gain)
-
-
-def gram_kernel(*refs, start, fused, clear, last):
-    recv_ref, y_ref = refs[:2]
-    refs = refs[2:]
+    )(*gain, *recv, *y, *cur)
+
+
+def gram_kernel(*refs, start, fused, clear, last, share, tile):
+    recv0_ref, recv_ref, y0_ref, y_ref = refs[:4]
+    refs = refs[4:]
     if fused:
         gh_ref, gl_ref = refs[:2]
         refs = refs[2:]
     if start:
         oldh_ref, oldl_ref = refs[:2]
         refs = refs[2:]
-    piece = refs[0]
-    n, _ = recv_ref.shape
+    piece, rest = refs[0], refs[1:]
+    n = recv_ref.shape[0]
     here = slice(start, start + n)
 
     @pl.when(lax.axis_index("row") > 0)
     def _():
-        recv = stacked(recv_ref[...])
-        x = y_ref[...]
+        recv = stacked(jnp.concatenate([recv0_ref[here], recv_ref[...]], axis=1))
+        x = jnp.concatenate([y0_ref[here], y_ref[...]], axis=1)
         if fused:
             x = x - three(nn, recv, gh_ref[...], gl_ref[...])
         x = stacked(x)
@@ -257,8 +311,12 @@
             piece[:, :start] = three(nn, both, oldh_ref[:, :start], oldl_ref[:, :start])
         piece[:, here] = three(nt, both, high, low)
         if not last:
-            refs[1][:, here] = high.T
-            refs[2][:, here] = low.T
+            rest[0][:, here] = high.T
+            rest[1][:, here] = low.T
+        elif share:
+            rest[0][...] = jnp.concatenate(
+                [piece[:, t * tile : t * tile + share] for t in range((start + n) // tile)], axis=1
+            )
 
     if clear:
 
@@ -267,17 +325,21 @@
             piece[...] = jnp.zeros_like(piece)
 
 
-def gram(recv, y, gain, kept, start, total, clear):
-    n, half = y.shape
+def gram(recv, y, gain, kept, start, total, tile, share, clear):
+    n = recv[1].shape[0]
+    half = recv[0].shape[1] + recv[1].shape[1]
     last = start + n == total
-    fused = bool(gain)
-    vmem = pl.BlockSpec(memory_space=pltpu.VMEM)
-    inputs = [recv, y, *gain, *kept]
+    inputs = [*recv, *y, *gain, *kept]
+    if not last:
+        more = [jax.ShapeDtypeStruct((2 * half, total), BF16)] * 2
+    else:
+        more = [jax.ShapeDtypeStruct((n, total // tile * share), F32)] if share else []
     results = pl.pallas_call(
-        functools.partial(gram_kernel, start=start, fused=fused, clear=clear, last=last),
-        in_specs=[vmem] * len(inputs),
-        out_shape=[jax.ShapeDtypeStruct((n, start + n), F32)]
-        + ([] if last else [jax.ShapeDtypeStruct((2 * half, total), BF16)] * 2),
+        functools.partial(
+            gram_kernel, start=start, fused=bool(gain), clear=clear, last=last, share=share, tile=tile
+        ),
+        in_specs=[pl.BlockSpec(memory_space=pltpu.VMEM)] * len(inputs),
+        out_shape=[jax.ShapeDtypeStruct((n, start + n), F32)] + more,
         input_output_aliases={len(inputs) - 2 + i: 1 + i for i in range(2)} if start and not last else {},
         compiler_params=pltpu.CompilerParams(vmem_limit_bytes=VMEM_LIMIT),
         cost_estimate=pl.CostEstimate(
@@ -294,6 +356,12 @@
     for start, piece in chunks:
         n = piece.shape[0]
         at, inner = start // tile, start % tile
+        if piece.shape[1] < start + n:
+            turned = piece[:, low_tile * share :].T
+            for t in range(low_tile, at + 1):
+                first = (t - low_tile) * share
+                out[t - low_tile, :, start - base : start - base + n] = turned[first : first + share]
+            continue
         first, stop = max(inner, low), min(inner + n, high)
         if first < stop:
             out[at - low_tile, first - low : stop - low, : start + n - base] = piece[first - inner : stop - inner, base:]
@@ -396,7 +464,7 @@
 
 
 def sizes(count, tile):
-    short = tile // LAST
+    short = tile * LAST[0] // LAST[1]
     return (tile,) * (count - 1) + (tile - short, short)
 
 
@@ -409,26 +477,30 @@
     starts = [sum(chunks[:c]) for c in range(len(chunks))]
     offsets = jnp.transpose(band_offsets, (2, 0, 1))
     ids = jnp.transpose(tile_ids)
-    given = (offsets, ids, factor_blocks, block_inverses, coupling)
     far = [(s, s - 1 + 2 * (s % 2)) for s in range(subs)]
     near = [(s, s + 1 - 2 * (s % 2)) for s in range(subs)]
     far, near = ([(s, t) for s, t in pairs if 0 <= t < subs] for pairs in (far, near))
-    early = solve(*given, chunks[:1], tile, True, ALONE)
-    ys = solve(*given, chunks, tile, False, VMEM_LIMIT)
+    early = early_solve(ids, block_inverses, coupling) if rows == 2 else None
+    ys = list(solve(offsets, ids, factor_blocks, block_inverses, coupling, chunks, tile))
     gain = response(offsets, factor_blocks, block_inverses)
-    xs, first, gain_now = early + ys[1:], None, gain if rows == 2 else ()
+    xs = [early] + ys[1:] if rows == 2 else ys
+    first = None
     for stage in range(1, rows):
         recv = []
         for x in xs:
             recv.append(lax.ppermute(x, "row", [(stage - 1, stage)]))
         first = first or recv
         if rows > 2:
-            xs = [update(r, y, x, gain, stage) for r, y, x in zip(recv, ys, xs)]
+            xs = list(update(recv, ys, xs, gain, chunks, stage))
+    mine, gain_now = (ys, gain) if rows == 2 else (xs, ())
     kept, own, got = [], [], []
     for c, start in enumerate(starts):
-        piece, kept = gram(first[c], (ys if rows == 2 else xs)[c], gain_now, kept, start, cols, rows > 2)
+        narrow = share if rows == 2 and start % tile >= share else 0
+        piece, kept = gram(
+            (first[0], first[1 + c]), (mine[0], mine[1 + c]), gain_now, kept, start, cols, tile, narrow, rows > 2
+        )
         if rows == 2:
-            got.append(lax.ppermute(piece, "row", [(1, 0)]))
+            got.append(lax.ppermute(kept[0] if narrow else piece, "row", [(1, 0)]))
             own.append(piece)
         else:
             got.append(lax.psum(piece, "row"))

time: 75.6 us -> 71.7 us (0.948)
  waiting for transfers between devices: 35.8 us -> 27.1 us
  starting transfers between devices: 19.6 us -> 26.5 us
  Pallas kernels: 14.7 us -> 12.5 us
    ppermute x5 -> x6, waiting for transfers between devices: 24.4 us -> 17.2 us  [shards(): recv.append(lax.ppermute(x, 'row', [(stage - 1, stage)]))]
    ppermute x5 -> x6, starting transfers between devices: 6.58 us -> 13.1 us  [shards(): recv.append(lax.ppermute(x, 'row', [(stage - 1, stage)]))]
    pallas_call x2 -> x1, Pallas kernels: 10.3 us -> 5.46 us  [solve(): pl.pallas_call(functools.partial(solve_kernel, chunks=chunks, tiles=tiles...]
    pallas_call x5 -> x6, Pallas kernels: 0.21 us -> 2.9 us  [the longest x1 2.68 us: early_solve(): pl.pallas_call(early_kernel, in_specs=[hbm] * 3, out_shape=jax.ShapeDtype...]
    ppermute x5, waiting for transfers between devices: 7.69 us -> 6.15 us  [shards(): got.append(lax.ppermute(kept[0] if narrow else piece, 'row', [(1, 0)]))]
  transfers between devices with their start and end apart: 12 -> 13, of which waited for: 5 -> 6; matrix products, arithmetic and copies ran while one was open for 0% -> 0% of each run, Pallas kernels for 11% -> 12%
where the time goes in v2:
time: 71.7 us; the launch traced here: 71.2 us
  waiting for transfers between devices  27.1 us (38%)
  starting transfers between devices  26.5 us (37%)
  Pallas kernels  12.5 us (17%)
  local copies, waits for them, and re-layouts  4.72 us (7%)
    ppermute x6, waiting for transfers between devices, shards(): recv.append(lax.ppermute(x, 'row', [(stage - 1, stage)]))  17.2 us
    ppermute x6, starting transfers between devices, shards(): recv.append(lax.ppermute(x, 'row', [(stage - 1, stage)]))  13.1 us
    ppermute x1, starting transfers between devices, shards(): from_far = lax.ppermute(message, 'sub', far)  6.78 us
    ppermute x5, starting transfers between devices, shards(): got.append(lax.ppermute(kept[0] if narrow else piece, 'row', [(1, 0)]))  6.57 us
    ppermute x5, waiting for transfers between devices, shards(): got.append(lax.ppermute(kept[0] if narrow else piece, 'row', [(1, 0)]))  6.15 us
    pallas_call x1, Pallas kernels, solve(): pl.pallas_call(functools.partial(solve_kernel, chunks=chunks, tiles=tiles...  5.46 us
    unnamed x14, local copies, waits for them, and re-layouts  4.72 us
    ppermute x1, waiting for transfers between devices, shards(): from_far = lax.ppermute(message, 'sub', far)  3.75 us
  transfers between devices with their start and end apart: 13, of which 6 were waited for; matrix products, arithmetic and copies ran while one was open for 0% of the time, Pallas kernels for 12%

profile of v2, /device:TPU:9, one launch (start us, length us, event | category | flops | bytes accessed | tf_op | source)
XLA Modules:
  0.0 71.2 jit_solution(8370482765702071395)
XLA Ops:
  0.0 2.7 %early.1 = f32[512,256]{1,0:T(8,128)} custom-call(s32[4,16]{1,0:T(4,128)} %bitcast.3, f32[1,4,256,256]{3,2,1,0:T(8,128)} %inv_hbm.5, f32[1,1024,512]{2,1,0:T(8,128)} %b_hbm.3), custom_call_target="tpu_custom_call" | custom-call | flops 201326592 | bytes 1048576 | tf_op jit(solution)/shard_map/early/pallas_call | solution.py:123
  2.7 1.3 %collective-permute-start = (f32[512,256]{1,0:T(8,128)}, f32[512,256]{1,0:T(8,128)S(1)}, u32[]{:S(2)}, u32[]{:S(2)}) collective-permute-start(f32[512,256]{1,0:T(8,128)} %early.1), channel_id=1, source_target_pairs={{0,1},{2,3},{4,5},{6,7},{8,9},{10,11},{12,13},{14,15},{16,17},{18,... | collective-permute-start | bytes 1572872 | tf_op jit(solution)/shard_map/ppermute | solution.py:491
  4.0 0.0 copy-start
  4.1 1.6 %copy-done = f32[1,1024,512]{2,1,0:T(8,128)S(1)} copy-done((f32[1,1024,512]{2,1,0:T(8,128)S(1)}, f32[1,1024,512]{2,1,0:T(8,128)}, u32[]{:S(2)}) %copy-start) | copy-done | bytes 2097176
  5.6 1.2 %copy-done.1 = f32[1,4,256,256]{3,2,1,0:T(8,128)S(1)} copy-done((f32[1,4,256,256]{3,2,1,0:T(8,128)S(1)}, f32[1,4,256,256]{3,2,1,0:T(8,128)}, u32[]{:S(2)}) %copy-start.1) | copy-done | bytes 1048600
  6.9 1.9 %copy-done.5 = f32[1,4,3,256,256]{4,3,2,1,0:T(8,128)S(1)} copy-done((f32[1,4,3,256,256]{4,3,2,1,0:T(8,128)S(1)}, f32[1,4,3,256,256]{4,3,2,1,0:T(8,128)}, u32[]{:S(2)}) %copy-start.5) | copy-done | bytes 3145752
  8.8 5.5 %others.1 = (f32[512,256]{1,0:T(8,128)S(1)}, f32[128,768]{1,0:T(8,128)S(1)}, f32[128,768]{1,0:T(8,128)S(1)}, f32[128,768]{1,0:T(8,128)S(1)}, f32[80,768]{1,0:T(8,128)S(1)}, /*index=5*/f32[48,768]{1,0:T(8,128)S(1)}) custom-call(s32[3,1,4]{2,1,0:T(1,128)S(1)} %bitcast.8, s32[4,16]{1,0:T(4,128)S(1)} %bitcast.4, f32[1,4,3,256,256]{4,3,2,1,0:T(8,128)S(1)} %copy-done.5, ...), custom_call_target="tpu_custom_call" | custom-call | flops 2013265920 | bytes 8388608 | tf_op jit(solution)/shard_map/others/pallas_call | solution.py:186
  14.2 1.3 %collective-permute-start.1 = (f32[128,768]{1,0:T(8,128)S(1)}, f32[128,768]{1,0:T(8,128)S(1)}, u32[]{:S(2)}, u32[]{:S(2)}) collective-permute-start(f32[128,768]{1,0:T(8,128)S(1)} %get-tuple-element.27.refs_3_), channel_id=1, source_target_pairs={{0,1},{2,3},{4,5},{6,7},{8,9},{10,11},{12,13},{14,15},{16,17},{18,... | collective-permute-start | bytes 1179656 | tf_op jit(solution)/shard_map/ppermute | solution.py:491
  15.5 1.3 %collective-permute-start.3 = (f32[128,768]{1,0:T(8,128)S(1)}, f32[128,768]{1,0:T(8,128)S(1)}, u32[]{:S(2)}, u32[]{:S(2)}) collective-permute-start(f32[128,768]{1,0:T(8,128)S(1)} %get-tuple-element.32.refs_3_), channel_id=1, source_target_pairs={{0,1},{2,3},{4,5},{6,7},{8,9},{10,11},{12,13},{14,15},{16,17},{18,... | collective-permute-start | bytes 1179656 | tf_op jit(solution)/shard_map/ppermute | solution.py:491
  16.9 1.3 %collective-permute-start.6 = (f32[128,768]{1,0:T(8,128)S(1)}, f32[128,768]{1,0:T(8,128)S(1)}, u32[]{:S(2)}, u32[]{:S(2)}) collective-permute-start(f32[128,768]{1,0:T(8,128)S(1)} %get-tuple-element.36.refs_3_), channel_id=1, source_target_pairs={{0,1},{2,3},{4,5},{6,7},{8,9},{10,11},{12,13},{14,15},{16,17},{18,... | collective-permute-start | bytes 1179656 | tf_op jit(solution)/shard_map/ppermute | solution.py:491
  18.2 1.3 %collective-permute-start.8 = (f32[80,768]{1,0:T(8,128)S(1)}, f32[80,768]{1,0:T(8,128)S(1)}, u32[]{:S(2)}, u32[]{:S(2)}) collective-permute-start(f32[80,768]{1,0:T(8,128)S(1)} %get-tuple-element.40.refs_3_), channel_id=1, source_target_pairs={{0,1},{2,3},{4,5},{6,7},{8,9},{10,11},{12,13},{14,15},{16,17},{18,... | collective-permute-start | bytes 737288 | tf_op jit(solution)/shard_map/ppermute | solution.py:491
  19.5 0.6 response.1
  20.2 3.2 %collective-permute-done.1.refs_1_ = f32[128,768]{1,0:T(8,128)S(1)} collective-permute-done((f32[128,768]{1,0:T(8,128)S(1)}, f32[128,768]{1,0:T(8,128)S(1)}, u32[]{:S(2)}, u32[]{:S(2)}) %collective-permute-start.1) | collective-permute-done | bytes 393248 | tf_op jit(solution)/shard_map/ppermute | solution.py:491
  23.3 6.5 %collective-permute-start.10 = (f32[48,768]{1,0:T(8,128)S(1)}, f32[48,768]{1,0:T(8,128)S(1)}, u32[]{:S(2)}, u32[]{:S(2)}) collective-permute-start(f32[48,768]{1,0:T(8,128)S(1)} %get-tuple-element.44.refs_3_), channel_id=1, source_target_pairs={{0,1},{2,3},{4,5},{6,7},{8,9},{10,11},{12,13},{14,15},{16,17},{18,... | collective-permute-start | bytes 442376 | tf_op jit(solution)/shard_map/ppermute | solution.py:491
  29.9 0.2 shard_map.64
  30.1 1.7 %collective-permute-done.3.refs_1_ = f32[128,768]{1,0:T(8,128)S(1)} collective-permute-done((f32[128,768]{1,0:T(8,128)S(1)}, f32[128,768]{1,0:T(8,128)S(1)}, u32[]{:S(2)}, u32[]{:S(2)}) %collective-permute-start.3) | collective-permute-done | bytes 393248 | tf_op jit(solution)/shard_map/ppermute | solution.py:491
  31.7 8.4 %collective-permute-done.6.refs_1_ = f32[128,768]{1,0:T(8,128)S(1)} collective-permute-done((f32[128,768]{1,0:T(8,128)S(1)}, f32[128,768]{1,0:T(8,128)S(1)}, u32[]{:S(2)}, u32[]{:S(2)}) %collective-permute-start.6) | collective-permute-done | bytes 393248 | tf_op jit(solution)/shard_map/ppermute | solution.py:491
  40.2 1.3 %collective-permute-start.7 = (f32[128,384]{1,0:T(8,128)S(1)}, f32[128,384]{1,0:T(8,128)S(1)}, u32[]{:S(2)}, u32[]{:S(2)}) collective-permute-start(f32[128,384]{1,0:T(8,128)S(1)} %get-tuple-element.39.refs_3_), channel_id=1, source_target_pairs={{1,0},{3,2},{5,4},{7,6},{9,8},{11,10},{13,12},{15,14},{17,16},{19,... | collective-permute-start | bytes 589832 | tf_op jit(solution)/shard_map/ppermute | solution.py:503
  41.5 4.0 %collective-permute-done.8.refs_1_ = f32[80,768]{1,0:T(8,128)S(1)} collective-permute-done((f32[80,768]{1,0:T(8,128)S(1)}, f32[80,768]{1,0:T(8,128)S(1)}, u32[]{:S(2)}, u32[]{:S(2)}) %collective-permute-start.8) | collective-permute-done | bytes 245792 | tf_op jit(solution)/shard_map/ppermute | solution.py:491
  45.4 1.3 %collective-permute-start.9 = (f32[80,464]{1,0:T(8,128)S(1)}, f32[80,464]{1,0:T(8,128)S(1)}, u32[]{:S(2)}, u32[]{:S(2)}) collective-permute-start(f32[80,464]{1,0:T(8,128)S(1)} %get-tuple-element.43.refs_4_), channel_id=1, source_target_pairs={{1,0},{3,2},{5,4},{7,6},{9,8},{11,10},{13,12},{15,14},{17,16},{19,... | collective-permute-start | bytes 445448 | tf_op jit(solution)/shard_map/ppermute | solution.py:503
  46.7 1.3 %collective-permute-start.4 = (f32[128,256]{1,0:T(8,128)S(1)}, f32[128,256]{1,0:T(8,128)S(1)}, u32[]{:S(2)}, u32[]{:S(2)}) collective-permute-start(f32[128,256]{1,0:T(8,128)S(1)} %get-tuple-element.35.refs_3_), channel_id=1, source_target_pairs={{1,0},{3,2},{5,4},{7,6},{9,8},{11,10},{13,12},{15,14},{17,16},{19,... | collective-permute-start | bytes 393224 | tf_op jit(solution)/shard_map/ppermute | solution.py:503
  48.0 1.3 %collective-permute-start.2 = (f32[128,128]{1,0:T(8,128)S(1)}, f32[128,128]{1,0:T(8,128)S(1)}, u32[]{:S(2)}, u32[]{:S(2)}) collective-permute-start(f32[128,128]{1,0:T(8,128)S(1)} %get-tuple-element.31.refs_2_), channel_id=1, source_target_pairs={{1,0},{3,2},{5,4},{7,6},{9,8},{11,10},{13,12},{15,14},{17,16},{19,... | collective-permute-start | bytes 196616 | tf_op jit(solution)/shard_map/ppermute | solution.py:503
  49.4 1.4 %collective-permute-start.11 = (f32[48,256]{1,0:T(8,128)S(1)}, f32[48,256]{1,0:T(8,128)S(1)}, u32[]{:S(2)}, u32[]{:S(2)}) collective-permute-start(f32[48,256]{1,0:T(8,128)S(1)} %get-tuple-element.47), channel_id=1, source_target_pairs={{1,0},{3,2},{5,4},{7,6},{9,8},{11,10},{13,12},{15,14},{17,16},{19,... | collective-permute-start | bytes 147464 | tf_op jit(solution)/shard_map/ppermute | solution.py:503
  50.8 6.1 %collective-permute-done.2.refs_0_ = f32[128,128]{1,0:T(8,128)S(1)} collective-permute-done((f32[128,128]{1,0:T(8,128)S(1)}, f32[128,128]{1,0:T(8,128)S(1)}, u32[]{:S(2)}, u32[]{:S(2)}) %collective-permute-start.2) | collective-permute-done | bytes 65568 | tf_op jit(solution)/shard_map/ppermute | solution.py:503
  56.9 0.1 shard_map.66
  57.0 6.8 %collective-permute-start.5 = (f32[2,64,256]{2,1,0:T(8,128)S(1)}, f32[2,64,256]{2,1,0:T(8,128)S(1)}, u32[]{:S(2)}, u32[]{:S(2)}) collective-permute-start(f32[2,64,256]{2,1,0:T(8,128)S(1)} %shard_map.66), channel_id=1, source_target_pairs={{2,4},{4,2},{6,8},{8,6},{10,12},{12,10},{14,16},{16,14},{18,20},{2... | collective-permute-start | bytes 393224 | tf_op jit(solution)/shard_map/ppermute | solution.py:514
  63.8 0.2 shard_map.72
  64.0 0.1 collective-permute-start.12
  64.1 3.8 %collective-permute-done.5.halo_ref = f32[2,64,256]{2,1,0:T(8,128)S(1)} collective-permute-done((f32[2,64,256]{2,1,0:T(8,128)S(1)}, f32[2,64,256]{2,1,0:T(8,128)S(1)}, u32[]{:S(2)}, u32[]{:S(2)}) %collective-permute-start.5) | collective-permute-done | bytes 131104 | tf_op jit(solution)/shard_map/ppermute | solution.py:514
  67.8 0.8 %shard_map.67.base_ref = f32[4,64,512]{2,1,0:T(8,128)S(1)} custom-call(s32[4,16]{1,0:T(4,128)S(1)} %bitcast.5, f32[1,4,64,512]{3,2,1,0:T(8,128)S(1)} %copy-done.3, f32[2,64,256]{2,1,0:T(8,128)S(1)} %collective-permute-done.5.halo_ref, f32[128,128]{1,0:T(8,128)S(1)} %collective-permute-done.2.refs_0_, f32[128,256]{1,0:T(8,128)S(1)} %collective-permute-done.4.refs_1_, ...), custom_call_target="tpu_custom_call" | custom-call | tf_op jit(solution)/shard_map/pallas_call | solution.py:457
  68.7 1.0 %shard_map.71.base_ref = f32[4,64,512]{2,1,0:T(8,128)S(1)} custom-call(s32[4,16]{1,0:T(4,128)S(1)} %bitcast.6, f32[4,64,512]{2,1,0:T(8,128)S(1)} %shard_map.67.base_ref, f32[128,384]{1,0:T(8,128)S(1)} %collective-permute-done.7.refs_0_, f32[80,464]{1,0:T(8,128)S(1)} %collective-permute-done.9.refs_1_, f32[48,256]{1,0:T(8,128)S(1)} %collective-permute-done.11.refs_2_, ...), custom_call_target="tpu_custom_call" | custom-call | tf_op jit(solution)/shard_map/pallas_call | solution.py:457
  69.7 1.5 %shard_map.73 = f32[4,64,512]{2,1,0:T(8,128)} custom-call(s32[4,16]{1,0:T(4,128)S(1)} %bitcast.7, f32[4,64,512]{2,1,0:T(8,128)S(1)} %shard_map.71.base_ref, f32[2,64,256]{2,1,0:T(8,128)S(1)} %collective-permute-done.12.halo_ref), custom_call_target="tpu_custom_call" | custom-call | tf_op jit(solution)/shard_map/pallas_call | solution.py:457
  (21 shorter events, 0.1 us)
Async XLA Ops:
  0.0 4.0 %copy-start.4 = (s32[16,4]{0,1:T(4,128)S(1)}, s32[16,4]{0,1:T(4,128)}, u32[]{:S(2)}) copy-start(s32[16,4]{0,1:T(4,128)} %param.11) | copy-start | bytes 772
  0.0 4.0 %copy-start.6 = (s32[1,4,3]{1,0,2:T(1,128)S(1)}, s32[1,4,3]{1,0,2:T(1,128)}, u32[]{:S(2)}) copy-start(s32[1,4,3]{1,0,2:T(1,128)} %param.8) | copy-start | bytes 148
  2.7 27.1 %collective-permute-start = (f32[512,256]{1,0:T(8,128)}, f32[512,256]{1,0:T(8,128)S(1)}, u32[]{:S(2)}, u32[]{:S(2)}) collective-permute-start(f32[512,256]{1,0:T(8,128)} %early.1), channel_id=1, source_target_pairs={{0,1},{2,3},{4,5},{6,7},{8,9},{10,11},{12,13},{14,15},{16,17},{18,... | collective-permute-start | bytes 1572872 | tf_op jit(solution)/shard_map/ppermute | solution.py:491
  4.0 1.6 %copy-start = (f32[1,1024,512]{2,1,0:T(8,128)S(1)}, f32[1,1024,512]{2,1,0:T(8,128)}, u32[]{:S(2)}) copy-start(f32[1,1024,512]{2,1,0:T(8,128)} %b_hbm.3) | copy-start | bytes 6291460
  5.6 1.2 %copy-start.1 = (f32[1,4,256,256]{3,2,1,0:T(8,128)S(1)}, f32[1,4,256,256]{3,2,1,0:T(8,128)}, u32[]{:S(2)}) copy-start(f32[1,4,256,256]{3,2,1,0:T(8,128)} %inv_hbm.5) | copy-start | bytes 3145732
  6.9 1.9 %copy-start.5 = (f32[1,4,3,256,256]{4,3,2,1,0:T(8,128)S(1)}, f32[1,4,3,256,256]{4,3,2,1,0:T(8,128)}, u32[]{:S(2)}) copy-start(f32[1,4,3,256,256]{4,3,2,1,0:T(8,128)} %f_hbm.3) | copy-start | bytes 9437188
  8.8 10.7 %copy-start.2 = (f32[1,4,256,256]{3,2,1,0:T(8,128)S(1)}, f32[1,4,256,256]{3,2,1,0:T(8,128)}, u32[]{:S(2)}) copy-start(f32[1,4,256,256]{3,2,1,0:T(8,128)} %inv_hbm.5) | copy-start | bytes 3145732
  14.2 9.1 %collective-permute-start.1 = (f32[128,768]{1,0:T(8,128)S(1)}, f32[128,768]{1,0:T(8,128)S(1)}, u32[]{:S(2)}, u32[]{:S(2)}) collective-permute-start(f32[128,768]{1,0:T(8,128)S(1)} %get-tuple-element.27.refs_3_), channel_id=1, source_target_pairs={{0,1},{2,3},{4,5},{6,7},{8,9},{10,11},{12,13},{14,15},{16,17},{18,... | collective-permute-start | bytes 1179656 | tf_op jit(solution)/shard_map/ppermute | solution.py:491
  15.5 16.2 %collective-permute-start.3 = (f32[128,768]{1,0:T(8,128)S(1)}, f32[128,768]{1,0:T(8,128)S(1)}, u32[]{:S(2)}, u32[]{:S(2)}) collective-permute-start(f32[128,768]{1,0:T(8,128)S(1)} %get-tuple-element.32.refs_3_), channel_id=1, source_target_pairs={{0,1},{2,3},{4,5},{6,7},{8,9},{10,11},{12,13},{14,15},{16,17},{18,... | collective-permute-start | bytes 1179656 | tf_op jit(solution)/shard_map/ppermute | solution.py:491
  16.9 23.3 %collective-permute-start.6 = (f32[128,768]{1,0:T(8,128)S(1)}, f32[128,768]{1,0:T(8,128)S(1)}, u32[]{:S(2)}, u32[]{:S(2)}) collective-permute-start(f32[128,768]{1,0:T(8,128)S(1)} %get-tuple-element.36.refs_3_), channel_id=1, source_target_pairs={{0,1},{2,3},{4,5},{6,7},{8,9},{10,11},{12,13},{14,15},{16,17},{18,... | collective-permute-start | bytes 1179656 | tf_op jit(solution)/shard_map/ppermute | solution.py:491
  18.2 27.2 %collective-permute-start.8 = (f32[80,768]{1,0:T(8,128)S(1)}, f32[80,768]{1,0:T(8,128)S(1)}, u32[]{:S(2)}, u32[]{:S(2)}) collective-permute-start(f32[80,768]{1,0:T(8,128)S(1)} %get-tuple-element.40.refs_3_), channel_id=1, source_target_pairs={{0,1},{2,3},{4,5},{6,7},{8,9},{10,11},{12,13},{14,15},{16,17},{18,... | collective-permute-start | bytes 737288 | tf_op jit(solution)/shard_map/ppermute | solution.py:491
  23.3 26.0 %collective-permute-start.10 = (f32[48,768]{1,0:T(8,128)S(1)}, f32[48,768]{1,0:T(8,128)S(1)}, u32[]{:S(2)}, u32[]{:S(2)}) collective-permute-start(f32[48,768]{1,0:T(8,128)S(1)} %get-tuple-element.44.refs_3_), channel_id=1, source_target_pairs={{0,1},{2,3},{4,5},{6,7},{8,9},{10,11},{12,13},{14,15},{16,17},{18,... | collective-permute-start | bytes 442376 | tf_op jit(solution)/shard_map/ppermute | solution.py:491
  40.2 23.7 %collective-permute-start.7 = (f32[128,384]{1,0:T(8,128)S(1)}, f32[128,384]{1,0:T(8,128)S(1)}, u32[]{:S(2)}, u32[]{:S(2)}) collective-permute-start(f32[128,384]{1,0:T(8,128)S(1)} %get-tuple-element.39.refs_3_), channel_id=1, source_target_pairs={{1,0},{3,2},{5,4},{7,6},{9,8},{11,10},{13,12},{15,14},{17,16},{19,... | collective-permute-start | bytes 589832 | tf_op jit(solution)/shard_map/ppermute | solution.py:503
  45.4 18.4 %collective-permute-start.9 = (f32[80,464]{1,0:T(8,128)S(1)}, f32[80,464]{1,0:T(8,128)S(1)}, u32[]{:S(2)}, u32[]{:S(2)}) collective-permute-start(f32[80,464]{1,0:T(8,128)S(1)} %get-tuple-element.43.refs_4_), channel_id=1, source_target_pairs={{1,0},{3,2},{5,4},{7,6},{9,8},{11,10},{13,12},{15,14},{17,16},{19,... | collective-permute-start | bytes 445448 | tf_op jit(solution)/shard_map/ppermute | solution.py:503
  46.7 10.2 %collective-permute-start.4 = (f32[128,256]{1,0:T(8,128)S(1)}, f32[128,256]{1,0:T(8,128)S(1)}, u32[]{:S(2)}, u32[]{:S(2)}) collective-permute-start(f32[128,256]{1,0:T(8,128)S(1)} %get-tuple-element.35.refs_3_), channel_id=1, source_target_pairs={{1,0},{3,2},{5,4},{7,6},{9,8},{11,10},{13,12},{15,14},{17,16},{19,... | collective-permute-start | bytes 393224 | tf_op jit(solution)/shard_map/ppermute | solution.py:503
  48.0 8.9 %collective-permute-start.2 = (f32[128,128]{1,0:T(8,128)S(1)}, f32[128,128]{1,0:T(8,128)S(1)}, u32[]{:S(2)}, u32[]{:S(2)}) collective-permute-start(f32[128,128]{1,0:T(8,128)S(1)} %get-tuple-element.31.refs_2_), channel_id=1, source_target_pairs={{1,0},{3,2},{5,4},{7,6},{9,8},{11,10},{13,12},{15,14},{17,16},{19,... | collective-permute-start | bytes 196616 | tf_op jit(solution)/shard_map/ppermute | solution.py:503
  49.3 18.5 %copy-start.3 = (f32[1,4,64,512]{3,2,1,0:T(8,128)S(1)}, f32[1,4,64,512]{3,2,1,0:T(8,128)}, u32[]{:S(2)}) copy-start(f32[1,4,64,512]{3,2,1,0:T(8,128)} %face_ref.1) | copy-start | bytes 1572868
  49.4 14.4 %collective-permute-start.11 = (f32[48,256]{1,0:T(8,128)S(1)}, f32[48,256]{1,0:T(8,128)S(1)}, u32[]{:S(2)}, u32[]{:S(2)}) collective-permute-start(f32[48,256]{1,0:T(8,128)S(1)} %get-tuple-element.47), channel_id=1, source_target_pairs={{1,0},{3,2},{5,4},{7,6},{9,8},{11,10},{13,12},{15,14},{17,16},{19,... | collective-permute-start | bytes 147464 | tf_op jit(solution)/shard_map/ppermute | solution.py:503
  57.0 10.8 %collective-permute-start.5 = (f32[2,64,256]{2,1,0:T(8,128)S(1)}, f32[2,64,256]{2,1,0:T(8,128)S(1)}, u32[]{:S(2)}, u32[]{:S(2)}) collective-permute-start(f32[2,64,256]{2,1,0:T(8,128)S(1)} %shard_map.66), channel_id=1, source_target_pairs={{2,4},{4,2},{6,8},{8,6},{10,12},{12,10},{14,16},{16,14},{18,20},{2... | collective-permute-start | bytes 393224 | tf_op jit(solution)/shard_map/ppermute | solution.py:514
  64.0 5.7 %collective-permute-start.12 = (f32[2,64,256]{2,1,0:T(8,128)S(1)}, f32[2,64,256]{2,1,0:T(8,128)S(1)}, u32[]{:S(2)}, u32[]{:S(2)}) collective-permute-start(f32[2,64,256]{2,1,0:T(8,128)S(1)} %shard_map.72), channel_id=1, source_target_pairs={{0,2},{2,0},{4,6},{6,4},{8,10},{10,8},{12,14},{14,12},{16,18},{18,... | collective-permute-start | bytes 393224 | tf_op jit(solution)/shard_map/ppermute | solution.py:518

commit v3 on v2

--- a/solution.py
+++ b/solution.py
@@ -11,7 +11,7 @@
 F32 = jnp.float32
 BF16 = jnp.bfloat16
 VMEM_LIMIT = 24 * 1024 * 1024
-OTHERS = 24 * 1024 * 1024
+OTHERS = 52 * 1024 * 1024
 ALONE = 63 * 1024 * 1024
 PAIR = 2
 LAST = (3, 8)
@@ -113,8 +113,12 @@
         copies[2].wait()
         order = ordered(ids_ref, lax.axis_index("sub"))
         tile = x_ref.shape[0] // len(order)
+        writes = []
         for p, k in enumerate(order):
-            out[p * tile : (p + 1) * tile] = x_ref[pl.ds(pl.multiple_of(k * tile, tile), tile)]
+            rows = pl.ds(pl.multiple_of(k * tile, tile), tile)
+            writes.append(pltpu.make_async_copy(x_ref.at[rows], out.at[pl.ds(p * tile, tile)], sems.at[3 + p]))
+            writes[-1].start()
+        wait_all(writes)
 
 
 def early_solve(ids, inverses, coupling):
@@ -123,13 +127,14 @@
     return pl.pallas_call(
         early_kernel,
         in_specs=[hbm] * 3,
+        out_specs=hbm,
         out_shape=jax.ShapeDtypeStruct((cols, size), F32),
         scratch_shapes=[
             pltpu.SMEM(ids.shape, jnp.int32),
             pltpu.VMEM((size, size), F32),
             pltpu.VMEM((size, cols), F32),
             pltpu.VMEM((cols, size), F32),
-            pltpu.SemaphoreType.DMA((3,)),
+            pltpu.SemaphoreType.DMA((3 + ids.shape[0],)),
         ],
         compiler_params=pltpu.CompilerParams(vmem_limit_bytes=ALONE),
         cost_estimate=pl.CostEstimate(flops=6 * size * size * cols, bytes_accessed=1 << 20, transcendentals=0),
@@ -420,34 +425,33 @@
                 out[slots[m][0], :, pl.ds(at, tile)] -= halo[m, :, n * tile : (n + 1) * tile]
 
 
+def subtract_gram(ids_ref, out, g, chunks, parts, tile, blocks):
+    starts, pieces = chunks
+    for p, q in blocks:
+        g[p, :, q * tile : (q + 1) * tile] = jnp.zeros((g.shape[1], tile), F32)
+    fill_mine(g, starts, pieces, parts, tile, 0)
+    order = ordered(ids_ref, lax.axis_index("sub"))
+    for p, q in blocks:
+        at = pl.multiple_of(order[q] * tile, tile)
+        out[order[p], :, pl.ds(at, tile)] -= g[p, :, q * tile : (q + 1) * tile]
+
+
 def middle_kernel(ids_ref, face_ref, halo_ref, *refs, starts, parts, tile):
     pieces, (out_ref, g) = refs[:-2], refs[-2:]
-    fill_mine(g, starts, pieces, parts, tile, 0)
+    count = out_ref.shape[0]
     out_ref[...] = face_ref[0]
-    sub = lax.axis_index("sub")
-    order = ordered(ids_ref, sub)
-    for p in range(PAIR):
-        for q in range(PAIR):
-            at = pl.multiple_of(order[q] * tile, tile)
-            out_ref[order[p], :, pl.ds(at, tile)] -= g[p, :, q * tile : (q + 1) * tile]
-    subtract_halo(ids_ref, out_ref, halo_ref, far_of(sub), 0)
-
-
-def rest_kernel(ids_ref, base_ref, *refs, starts, parts, tile):
+    blocks = [(p, q) for p in range(count) for q in range(count)]
+    subtract_gram(ids_ref, out_ref, g, (starts, pieces), parts, tile, blocks)
+    subtract_halo(ids_ref, out_ref, halo_ref, far_of(lax.axis_index("sub")), 0)
+
+
+def finish_kernel(ids_ref, base_ref, halo_ref, *refs, starts, parts, tile, low_tile):
     pieces, (out_ref, g) = refs[:-2], refs[-2:]
-    count = base_ref.shape[0]
-    fill_mine(g, starts, pieces, parts, tile, 0)
+    count = out_ref.shape[0]
+    last = count - 1
     out_ref[...] = base_ref[...]
-    order = ordered(ids_ref, lax.axis_index("sub"))
-    for p in range(count):
-        for q in range(count):
-            if p >= PAIR or q >= PAIR:
-                at = pl.multiple_of(order[q] * tile, tile)
-                out_ref[order[p], :, pl.ds(at, tile)] -= g[p, :, q * tile : (q + 1) * tile]
-
-
-def finish_kernel(ids_ref, base_ref, halo_ref, out_ref, *, low_tile):
-    out_ref[...] = base_ref[...]
+    blocks = [(p, q) for p in range(count) for q in range(count) if last in (p, q)]
+    subtract_gram(ids_ref, out_ref, g, (starts, pieces), parts, tile, blocks)
     subtract_halo(ids_ref, out_ref, halo_ref, near_of(lax.axis_index("sub")), low_tile)
 
 
@@ -512,14 +516,13 @@
 
     message = pair(pick(0, PAIR), starts[:PAIR], rows, tile, share, 0)
     from_far = lax.ppermute(message, "sub", far)
-    kernel = functools.partial(middle_kernel, starts=starts[:PAIR], parts=rows, tile=tile)
-    base = assemble(kernel, ids, [interface_block, from_far] + pick(0, PAIR), shape, (PAIR, share, PAIR * tile))
+    kernel = functools.partial(middle_kernel, starts=starts[:-1], parts=rows, tile=tile)
+    arrays = [interface_block, from_far] + got[:-1] + own[:-1]
+    base = assemble(kernel, ids, arrays, shape, shape)
     message = pair(pick(last, None), starts[last:], rows, tile, share, last)
     from_near = lax.ppermute(message, "sub", near)
-    kernel = functools.partial(rest_kernel, starts=starts[PAIR:], parts=rows, tile=tile)
-    base = assemble(kernel, ids, [base] + pick(PAIR, None), shape, shape)
-    kernel = functools.partial(finish_kernel, low_tile=last)
-    return assemble(kernel, ids, [base, from_near], shape, None)[None]
+    kernel = functools.partial(finish_kernel, starts=starts[-1:], parts=rows, tile=tile, low_tile=last)
+    return assemble(kernel, ids, [base, from_near] + pick(-1, None), shape, shape)[None]
 
 
 def solution(mesh):

time: 71.7 us -> 71.3 us (level)
  waiting for transfers between devices: 27.1 us -> 34.1 us
  local copies, waits for them, and re-layouts: 4.72 us -> 0.03 us
  starting transfers between devices: 26.5 us -> 23.7 us
    ppermute x6, waiting for transfers between devices: 17.2 us -> 23.6 us  [shards(): recv.append(lax.ppermute(x, 'row', [(stage - 1, stage)]))]
    unnamed x14 -> x12, local copies, waits for them, and re-layouts: 4.72 us -> 0.03 us
    ppermute x6, starting transfers between devices: 13.1 us -> 10.8 us  [shards(): recv.append(lax.ppermute(x, 'row', [(stage - 1, stage)]))]
    pallas_call x1, Pallas kernels: 5.46 us -> 6.39 us  [solve(): pl.pallas_call(functools.partial(solve_kernel, chunks=chunks, tiles=tiles...]
    pallas_call x3 -> x2, Pallas kernels: 3.32 us -> 2.76 us  [assemble(): pl.pallas_call(kernel, in_specs=[smem] + [vmem] * len(arrays), out_shape=...]
where the time goes in v3:
time: 71.3 us; the launch traced here: 70.9 us
  waiting for transfers between devices  34.1 us (48%)
  starting transfers between devices  23.7 us (33%)
  Pallas kernels  12.7 us (18%)
    ppermute x6, waiting for transfers between devices, shards(): recv.append(lax.ppermute(x, 'row', [(stage - 1, stage)]))  23.6 us
    ppermute x6, starting transfers between devices, shards(): recv.append(lax.ppermute(x, 'row', [(stage - 1, stage)]))  10.8 us
    ppermute x5, waiting for transfers between devices, shards(): got.append(lax.ppermute(kept[0] if narrow else piece, 'row', [(1, 0)]))  6.76 us
    ppermute x5, starting transfers between devices, shards(): got.append(lax.ppermute(kept[0] if narrow else piece, 'row', [(1, 0)]))  6.57 us
    pallas_call x1, Pallas kernels, solve(): pl.pallas_call(functools.partial(solve_kernel, chunks=chunks, tiles=tiles...  6.39 us
    ppermute x1, starting transfers between devices, shards(): from_far = lax.ppermute(message, 'sub', far)  6.26 us
    ppermute x1, waiting for transfers between devices, shards(): from_far = lax.ppermute(message, 'sub', far)  3.75 us
    pallas_call x2, Pallas kernels, assemble(): pl.pallas_call(kernel, in_specs=[smem] + [vmem] * len(arrays), out_shape=...  2.76 us
  transfers between devices with their start and end apart: 13, of which 6 were waited for; matrix products, arithmetic and copies ran while one was open for 0% of the time, Pallas kernels for 12%

profile of v3, /device:TPU:9, one launch (start us, length us, event | category | flops | bytes accessed | tf_op | source)
XLA Modules:
  0.0 70.9 jit_solution(14484793636143109180)
XLA Ops:
  0.0 2.7 %early.1 = f32[512,256]{1,0:T(8,128)} custom-call(s32[4,16]{1,0:T(4,128)} %bitcast.3, f32[1,4,256,256]{3,2,1,0:T(8,128)} %inv_hbm.5, f32[1,1024,512]{2,1,0:T(8,128)} %b_hbm.3), custom_call_target="tpu_custom_call" | custom-call | flops 201326592 | bytes 1048576 | tf_op jit(solution)/shard_map/early/pallas_call | solution.py:127
  2.7 1.3 %collective-permute-start = (f32[512,256]{1,0:T(8,128)}, f32[512,256]{1,0:T(8,128)S(1)}, u32[]{:S(2)}, u32[]{:S(2)}) collective-permute-start(f32[512,256]{1,0:T(8,128)} %early.1), channel_id=1, source_target_pairs={{0,1},{2,3},{4,5},{6,7},{8,9},{10,11},{12,13},{14,15},{16,17},{18,... | collective-permute-start | bytes 1572872 | tf_op jit(solution)/shard_map/ppermute | solution.py:495
  4.0 0.0 copy-start.1
  4.0 0.0 copy-start.4
  4.1 6.4 %others.1 = (f32[512,256]{1,0:T(8,128)}, f32[128,768]{1,0:T(8,128)S(1)}, f32[128,768]{1,0:T(8,128)S(1)}, f32[128,768]{1,0:T(8,128)S(1)}, f32[80,768]{1,0:T(8,128)S(1)}, /*index=5*/f32[48,768]{1,0:T(8,128)S(1)}) custom-call(s32[3,1,4]{2,1,0:T(1,128)S(1)} %bitcast.7, s32[4,16]{1,0:T(4,128)S(1)} %bitcast.4, f32[1,4,3,256,256]{4,3,2,1,0:T(8,128)} %f_hbm.3, ...), custom_call_target="tpu_custom_call" | custom-call | flops 2013265920 | bytes 8388608 | tf_op jit(solution)/shard_map/others/pallas_call | solution.py:191
  10.5 1.3 %collective-permute-start.1 = (f32[128,768]{1,0:T(8,128)S(1)}, f32[128,768]{1,0:T(8,128)S(1)}, u32[]{:S(2)}, u32[]{:S(2)}) collective-permute-start(f32[128,768]{1,0:T(8,128)S(1)} %get-tuple-element.27.refs_3_), channel_id=1, source_target_pairs={{0,1},{2,3},{4,5},{6,7},{8,9},{10,11},{12,13},{14,15},{16,17},{18,... | collective-permute-start | bytes 1179656 | tf_op jit(solution)/shard_map/ppermute | solution.py:495
  11.8 1.3 %collective-permute-start.3 = (f32[128,768]{1,0:T(8,128)S(1)}, f32[128,768]{1,0:T(8,128)S(1)}, u32[]{:S(2)}, u32[]{:S(2)}) collective-permute-start(f32[128,768]{1,0:T(8,128)S(1)} %get-tuple-element.32.refs_3_), channel_id=1, source_target_pairs={{0,1},{2,3},{4,5},{6,7},{8,9},{10,11},{12,13},{14,15},{16,17},{18,... | collective-permute-start | bytes 1179656 | tf_op jit(solution)/shard_map/ppermute | solution.py:495
  13.1 1.3 %collective-permute-start.6 = (f32[128,768]{1,0:T(8,128)S(1)}, f32[128,768]{1,0:T(8,128)S(1)}, u32[]{:S(2)}, u32[]{:S(2)}) collective-permute-start(f32[128,768]{1,0:T(8,128)S(1)} %get-tuple-element.36.refs_3_), channel_id=1, source_target_pairs={{0,1},{2,3},{4,5},{6,7},{8,9},{10,11},{12,13},{14,15},{16,17},{18,... | collective-permute-start | bytes 1179656 | tf_op jit(solution)/shard_map/ppermute | solution.py:495
  14.4 1.4 %collective-permute-start.8 = (f32[80,768]{1,0:T(8,128)S(1)}, f32[80,768]{1,0:T(8,128)S(1)}, u32[]{:S(2)}, u32[]{:S(2)}) collective-permute-start(f32[80,768]{1,0:T(8,128)S(1)} %get-tuple-element.40.refs_3_), channel_id=1, source_target_pairs={{0,1},{2,3},{4,5},{6,7},{8,9},{10,11},{12,13},{14,15},{16,17},{18,... | collective-permute-start | bytes 737288 | tf_op jit(solution)/shard_map/ppermute | solution.py:495
  15.9 0.6 response.1
  16.6 6.9 %collective-permute-done.1.refs_1_ = f32[128,768]{1,0:T(8,128)S(1)} collective-permute-done((f32[128,768]{1,0:T(8,128)S(1)}, f32[128,768]{1,0:T(8,128)S(1)}, u32[]{:S(2)}, u32[]{:S(2)}) %collective-permute-start.1) | collective-permute-done | bytes 393248 | tf_op jit(solution)/shard_map/ppermute | solution.py:495
  23.5 4.1 %collective-permute-start.10 = (f32[48,768]{1,0:T(8,128)S(1)}, f32[48,768]{1,0:T(8,128)S(1)}, u32[]{:S(2)}, u32[]{:S(2)}) collective-permute-start(f32[48,768]{1,0:T(8,128)S(1)} %get-tuple-element.44.refs_3_), channel_id=1, source_target_pairs={{0,1},{2,3},{4,5},{6,7},{8,9},{10,11},{12,13},{14,15},{16,17},{18,... | collective-permute-start | bytes 442376 | tf_op jit(solution)/shard_map/ppermute | solution.py:495
  27.6 0.0 collective-permute-done.refs_0_
  27.6 4.3 %collective-permute-done.3.refs_1_ = f32[128,768]{1,0:T(8,128)S(1)} collective-permute-done((f32[128,768]{1,0:T(8,128)S(1)}, f32[128,768]{1,0:T(8,128)S(1)}, u32[]{:S(2)}, u32[]{:S(2)}) %collective-permute-start.3) | collective-permute-done | bytes 393248 | tf_op jit(solution)/shard_map/ppermute | solution.py:495
  31.9 8.4 %collective-permute-done.6.refs_1_ = f32[128,768]{1,0:T(8,128)S(1)} collective-permute-done((f32[128,768]{1,0:T(8,128)S(1)}, f32[128,768]{1,0:T(8,128)S(1)}, u32[]{:S(2)}, u32[]{:S(2)}) %collective-permute-start.6) | collective-permute-done | bytes 393248 | tf_op jit(solution)/shard_map/ppermute | solution.py:495
  40.3 1.3 %collective-permute-start.7 = (f32[128,384]{1,0:T(8,128)S(1)}, f32[128,384]{1,0:T(8,128)S(1)}, u32[]{:S(2)}, u32[]{:S(2)}) collective-permute-start(f32[128,384]{1,0:T(8,128)S(1)} %get-tuple-element.39.refs_6_.refs_3_), channel_id=1, source_target_pairs={{1,0},{3,2},{5,4},{7,6},{9,8},{11,10},{13,12},{15,14},{17,16},{19,... | collective-permute-start | bytes 589832 | tf_op jit(solution)/shard_map/ppermute | solution.py:507
  41.6 4.0 %collective-permute-done.8.refs_1_ = f32[80,768]{1,0:T(8,128)S(1)} collective-permute-done((f32[80,768]{1,0:T(8,128)S(1)}, f32[80,768]{1,0:T(8,128)S(1)}, u32[]{:S(2)}, u32[]{:S(2)}) %collective-permute-start.8) | collective-permute-done | bytes 245792 | tf_op jit(solution)/shard_map/ppermute | solution.py:495
  45.6 1.3 %collective-permute-start.9 = (f32[80,464]{1,0:T(8,128)S(1)}, f32[80,464]{1,0:T(8,128)S(1)}, u32[]{:S(2)}, u32[]{:S(2)}) collective-permute-start(f32[80,464]{1,0:T(8,128)S(1)} %get-tuple-element.43.refs_7_.refs_4_), channel_id=1, source_target_pairs={{1,0},{3,2},{5,4},{7,6},{9,8},{11,10},{13,12},{15,14},{17,16},{19,... | collective-permute-start | bytes 445448 | tf_op jit(solution)/shard_map/ppermute | solution.py:507
  46.9 1.3 %collective-permute-start.4 = (f32[128,256]{1,0:T(8,128)S(1)}, f32[128,256]{1,0:T(8,128)S(1)}, u32[]{:S(2)}, u32[]{:S(2)}) collective-permute-start(f32[128,256]{1,0:T(8,128)S(1)} %get-tuple-element.35.refs_3_.refs_5_), channel_id=1, source_target_pairs={{1,0},{3,2},{5,4},{7,6},{9,8},{11,10},{13,12},{15,14},{17,16},{19,... | collective-permute-start | bytes 393224 | tf_op jit(solution)/shard_map/ppermute | solution.py:507
  48.2 1.3 %collective-permute-start.2 = (f32[128,128]{1,0:T(8,128)S(1)}, f32[128,128]{1,0:T(8,128)S(1)}, u32[]{:S(2)}, u32[]{:S(2)}) collective-permute-start(f32[128,128]{1,0:T(8,128)S(1)} %get-tuple-element.31.refs_2_.refs_4_), channel_id=1, source_target_pairs={{1,0},{3,2},{5,4},{7,6},{9,8},{11,10},{13,12},{15,14},{17,16},{19,... | collective-permute-start | bytes 196616 | tf_op jit(solution)/shard_map/ppermute | solution.py:507
  49.5 0.0 collective-permute-done.10.refs_1_
  49.5 0.0 copy-start.2
  49.5 1.4 %collective-permute-start.11 = (f32[48,256]{1,0:T(8,128)S(1)}, f32[48,256]{1,0:T(8,128)S(1)}, u32[]{:S(2)}, u32[]{:S(2)}) collective-permute-start(f32[48,256]{1,0:T(8,128)S(1)} %get-tuple-element.47), channel_id=1, source_target_pairs={{1,0},{3,2},{5,4},{7,6},{9,8},{11,10},{13,12},{15,14},{17,16},{19,... | collective-permute-start | bytes 147464 | tf_op jit(solution)/shard_map/ppermute | solution.py:507
  51.0 6.8 %collective-permute-done.2.refs_0_ = f32[128,128]{1,0:T(8,128)S(1)} collective-permute-done((f32[128,128]{1,0:T(8,128)S(1)}, f32[128,128]{1,0:T(8,128)S(1)}, u32[]{:S(2)}, u32[]{:S(2)}) %collective-permute-start.2) | collective-permute-done | bytes 65568 | tf_op jit(solution)/shard_map/ppermute | solution.py:507
  57.7 0.0 collective-permute-done.4.refs_1_
  57.7 0.1 shard_map.66
  57.8 6.3 %collective-permute-start.5 = (f32[2,64,256]{2,1,0:T(8,128)S(1)}, f32[2,64,256]{2,1,0:T(8,128)S(1)}, u32[]{:S(2)}, u32[]{:S(2)}) collective-permute-start(f32[2,64,256]{2,1,0:T(8,128)S(1)} %shard_map.66), channel_id=1, source_target_pairs={{2,4},{4,2},{6,8},{8,6},{10,12},{12,10},{14,16},{16,14},{18,20},{2... | collective-permute-start | bytes 393224 | tf_op jit(solution)/shard_map/ppermute | solution.py:518
  64.1 0.2 shard_map.71
  64.3 0.1 collective-permute-start.12
  64.4 3.8 %collective-permute-done.5.halo_ref = f32[2,64,256]{2,1,0:T(8,128)S(1)} collective-permute-done((f32[2,64,256]{2,1,0:T(8,128)S(1)}, f32[2,64,256]{2,1,0:T(8,128)S(1)}, u32[]{:S(2)}, u32[]{:S(2)}) %collective-permute-start.5) | collective-permute-done | bytes 131104 | tf_op jit(solution)/shard_map/ppermute | solution.py:518
  68.1 1.0 %shard_map.69.base_ref = f32[4,64,512]{2,1,0:T(8,128)S(1)} custom-call(s32[4,16]{1,0:T(4,128)S(1)} %bitcast.5, f32[1,4,64,512]{3,2,1,0:T(8,128)S(1)} %copy-done.2, f32[2,64,256]{2,1,0:T(8,128)S(1)} %collective-permute-done.5.halo_ref, f32[128,128]{1,0:T(8,128)S(1)} %collective-permute-done.2.refs_0_, f32[128,256]{1,0:T(8,128)S(1)} %collective-permute-done.4.refs_1_, ...), custom_call_target="tpu_custom_call" | custom-call | tf_op jit(solution)/shard_map/pallas_call | solution.py:461
  69.1 1.7 %shard_map.72 = f32[4,64,512]{2,1,0:T(8,128)} custom-call(s32[4,16]{1,0:T(4,128)S(1)} %bitcast.6, f32[4,64,512]{2,1,0:T(8,128)S(1)} %shard_map.69.base_ref, f32[2,64,256]{2,1,0:T(8,128)S(1)} %collective-permute-done.12.halo_ref, f32[48,256]{1,0:T(8,128)S(1)} %collective-permute-done.11.refs_2_.refs_0_, f32[48,512]{1,0:T(8,128)S(1)} %get-tuple-element.48.refs_5_.refs_1_), custom_call_target="tpu_custom_call" | custom-call | tf_op jit(solution)/shard_map/pallas_call | solution.py:461
  (18 shorter events, 0.1 us)
Async XLA Ops:
  0.0 4.0 %copy-start.3 = (s32[16,4]{0,1:T(4,128)S(1)}, s32[16,4]{0,1:T(4,128)}, u32[]{:S(2)}) copy-start(s32[16,4]{0,1:T(4,128)} %param.11) | copy-start | bytes 772
  0.0 4.0 %copy-start.5 = (s32[1,4,3]{1,0,2:T(1,128)S(1)}, s32[1,4,3]{1,0,2:T(1,128)}, u32[]{:S(2)}) copy-start(s32[1,4,3]{1,0,2:T(1,128)} %param.8) | copy-start | bytes 148
  2.7 24.9 %collective-permute-start = (f32[512,256]{1,0:T(8,128)}, f32[512,256]{1,0:T(8,128)S(1)}, u32[]{:S(2)}, u32[]{:S(2)}) collective-permute-start(f32[512,256]{1,0:T(8,128)} %early.1), channel_id=1, source_target_pairs={{0,1},{2,3},{4,5},{6,7},{8,9},{10,11},{12,13},{14,15},{16,17},{18,... | collective-permute-start | bytes 1572872 | tf_op jit(solution)/shard_map/ppermute | solution.py:495
  4.0 11.8 %copy-start.1 = (f32[1,4,256,256]{3,2,1,0:T(8,128)S(1)}, f32[1,4,256,256]{3,2,1,0:T(8,128)}, u32[]{:S(2)}) copy-start(f32[1,4,256,256]{3,2,1,0:T(8,128)} %inv_hbm.5) | copy-start | bytes 3145732
  4.0 11.8 %copy-start.4 = (f32[1,4,3,256,256]{4,3,2,1,0:T(8,128)S(1)}, f32[1,4,3,256,256]{4,3,2,1,0:T(8,128)}, u32[]{:S(2)}) copy-start(f32[1,4,3,256,256]{4,3,2,1,0:T(8,128)} %f_hbm.3) | copy-start | bytes 9437188
  10.5 13.0 %collective-permute-start.1 = (f32[128,768]{1,0:T(8,128)S(1)}, f32[128,768]{1,0:T(8,128)S(1)}, u32[]{:S(2)}, u32[]{:S(2)}) collective-permute-start(f32[128,768]{1,0:T(8,128)S(1)} %get-tuple-element.27.refs_3_), channel_id=1, source_target_pairs={{0,1},{2,3},{4,5},{6,7},{8,9},{10,11},{12,13},{14,15},{16,17},{18,... | collective-permute-start | bytes 1179656 | tf_op jit(solution)/shard_map/ppermute | solution.py:495
  11.8 20.1 %collective-permute-start.3 = (f32[128,768]{1,0:T(8,128)S(1)}, f32[128,768]{1,0:T(8,128)S(1)}, u32[]{:S(2)}, u32[]{:S(2)}) collective-permute-start(f32[128,768]{1,0:T(8,128)S(1)} %get-tuple-element.32.refs_3_), channel_id=1, source_target_pairs={{0,1},{2,3},{4,5},{6,7},{8,9},{10,11},{12,13},{14,15},{16,17},{18,... | collective-permute-start | bytes 1179656 | tf_op jit(solution)/shard_map/ppermute | solution.py:495
  13.1 27.2 %collective-permute-start.6 = (f32[128,768]{1,0:T(8,128)S(1)}, f32[128,768]{1,0:T(8,128)S(1)}, u32[]{:S(2)}, u32[]{:S(2)}) collective-permute-start(f32[128,768]{1,0:T(8,128)S(1)} %get-tuple-element.36.refs_3_), channel_id=1, source_target_pairs={{0,1},{2,3},{4,5},{6,7},{8,9},{10,11},{12,13},{14,15},{16,17},{18,... | collective-permute-start | bytes 1179656 | tf_op jit(solution)/shard_map/ppermute | solution.py:495
  14.4 13.2 %copy-start = (f32[512,256]{1,0:T(8,128)S(1)}, f32[512,256]{1,0:T(8,128)}, u32[]{:S(2)}) copy-start(f32[512,256]{1,0:T(8,128)} %get-tuple-element.28.refs_2_) | copy-start | bytes 1572868
  14.4 31.2 %collective-permute-start.8 = (f32[80,768]{1,0:T(8,128)S(1)}, f32[80,768]{1,0:T(8,128)S(1)}, u32[]{:S(2)}, u32[]{:S(2)}) collective-permute-start(f32[80,768]{1,0:T(8,128)S(1)} %get-tuple-element.40.refs_3_), channel_id=1, source_target_pairs={{0,1},{2,3},{4,5},{6,7},{8,9},{10,11},{12,13},{14,15},{16,17},{18,... | collective-permute-start | bytes 737288 | tf_op jit(solution)/shard_map/ppermute | solution.py:495
  23.5 26.0 %collective-permute-start.10 = (f32[48,768]{1,0:T(8,128)S(1)}, f32[48,768]{1,0:T(8,128)S(1)}, u32[]{:S(2)}, u32[]{:S(2)}) collective-permute-start(f32[48,768]{1,0:T(8,128)S(1)} %get-tuple-element.44.refs_3_), channel_id=1, source_target_pairs={{0,1},{2,3},{4,5},{6,7},{8,9},{10,11},{12,13},{14,15},{16,17},{18,... | collective-permute-start | bytes 442376 | tf_op jit(solution)/shard_map/ppermute | solution.py:495
  40.3 23.7 %collective-permute-start.7 = (f32[128,384]{1,0:T(8,128)S(1)}, f32[128,384]{1,0:T(8,128)S(1)}, u32[]{:S(2)}, u32[]{:S(2)}) collective-permute-start(f32[128,384]{1,0:T(8,128)S(1)} %get-tuple-element.39.refs_6_.refs_3_), channel_id=1, source_target_pairs={{1,0},{3,2},{5,4},{7,6},{9,8},{11,10},{13,12},{15,14},{17,16},{19,... | collective-permute-start | bytes 589832 | tf_op jit(solution)/shard_map/ppermute | solution.py:507
  45.6 18.5 %collective-permute-start.9 = (f32[80,464]{1,0:T(8,128)S(1)}, f32[80,464]{1,0:T(8,128)S(1)}, u32[]{:S(2)}, u32[]{:S(2)}) collective-permute-start(f32[80,464]{1,0:T(8,128)S(1)} %get-tuple-element.43.refs_7_.refs_4_), channel_id=1, source_target_pairs={{1,0},{3,2},{5,4},{7,6},{9,8},{11,10},{13,12},{15,14},{17,16},{19,... | collective-permute-start | bytes 445448 | tf_op jit(solution)/shard_map/ppermute | solution.py:507
  46.9 10.8 %collective-permute-start.4 = (f32[128,256]{1,0:T(8,128)S(1)}, f32[128,256]{1,0:T(8,128)S(1)}, u32[]{:S(2)}, u32[]{:S(2)}) collective-permute-start(f32[128,256]{1,0:T(8,128)S(1)} %get-tuple-element.35.refs_3_.refs_5_), channel_id=1, source_target_pairs={{1,0},{3,2},{5,4},{7,6},{9,8},{11,10},{13,12},{15,14},{17,16},{19,... | collective-permute-start | bytes 393224 | tf_op jit(solution)/shard_map/ppermute | solution.py:507
  48.2 9.5 %collective-permute-start.2 = (f32[128,128]{1,0:T(8,128)S(1)}, f32[128,128]{1,0:T(8,128)S(1)}, u32[]{:S(2)}, u32[]{:S(2)}) collective-permute-start(f32[128,128]{1,0:T(8,128)S(1)} %get-tuple-element.31.refs_2_.refs_4_), channel_id=1, source_target_pairs={{1,0},{3,2},{5,4},{7,6},{9,8},{11,10},{13,12},{15,14},{17,16},{19,... | collective-permute-start | bytes 196616 | tf_op jit(solution)/shard_map/ppermute | solution.py:507
  49.5 18.6 %copy-start.2 = (f32[1,4,64,512]{3,2,1,0:T(8,128)S(1)}, f32[1,4,64,512]{3,2,1,0:T(8,128)}, u32[]{:S(2)}) copy-start(f32[1,4,64,512]{3,2,1,0:T(8,128)} %face_ref.1) | copy-start | bytes 1572868
  49.5 14.5 %collective-permute-start.11 = (f32[48,256]{1,0:T(8,128)S(1)}, f32[48,256]{1,0:T(8,128)S(1)}, u32[]{:S(2)}, u32[]{:S(2)}) collective-permute-start(f32[48,256]{1,0:T(8,128)S(1)} %get-tuple-element.47), channel_id=1, source_target_pairs={{1,0},{3,2},{5,4},{7,6},{9,8},{11,10},{13,12},{15,14},{17,16},{19,... | collective-permute-start | bytes 147464 | tf_op jit(solution)/shard_map/ppermute | solution.py:507
  57.8 10.3 %collective-permute-start.5 = (f32[2,64,256]{2,1,0:T(8,128)S(1)}, f32[2,64,256]{2,1,0:T(8,128)S(1)}, u32[]{:S(2)}, u32[]{:S(2)}) collective-permute-start(f32[2,64,256]{2,1,0:T(8,128)S(1)} %shard_map.66), channel_id=1, source_target_pairs={{2,4},{4,2},{6,8},{8,6},{10,12},{12,10},{14,16},{16,14},{18,20},{2... | collective-permute-start | bytes 393224 | tf_op jit(solution)/shard_map/ppermute | solution.py:518
  64.3 4.9 %collective-permute-start.12 = (f32[2,64,256]{2,1,0:T(8,128)S(1)}, f32[2,64,256]{2,1,0:T(8,128)S(1)}, u32[]{:S(2)}, u32[]{:S(2)}) collective-permute-start(f32[2,64,256]{2,1,0:T(8,128)S(1)} %shard_map.71), channel_id=1, source_target_pairs={{0,2},{2,0},{4,6},{6,4},{8,10},{10,8},{12,14},{14,12},{16,18},{18,... | collective-permute-start | bytes 393224 | tf_op jit(solution)/shard_map/ppermute | solution.py:523

commit v4 on v3

--- a/solution.py
+++ b/solution.py
@@ -14,7 +14,7 @@
 OTHERS = 52 * 1024 * 1024
 ALONE = 63 * 1024 * 1024
 PAIR = 2
-LAST = (3, 8)
+LAST = (1, 2)
 
 
 def split(x):
@@ -400,9 +400,8 @@
     )(*pieces)
 
 
-def subtract_halo(ids, out, halo, other, low_tile):
+def matches(ids, other, low_tile):
     count, total = ids.shape
-    tile = halo.shape[2] // PAIR
     sub = lax.axis_index("sub")
     inside = jnp.logical_and(other >= 0, other < total)
     other = jnp.clip(other, 0, total - 1)
@@ -416,6 +415,12 @@
             place = jnp.where(same, jnp.int32(i), place)
             hit = jnp.logical_or(hit, same)
         slots.append((place, jnp.logical_and(hit, inside)))
+    return slots
+
+
+def subtract_halo(ids, out, halo, other, low_tile):
+    tile = halo.shape[2] // PAIR
+    slots = matches(ids, other, low_tile)
     for m in range(PAIR):
         for n in range(PAIR):
 
@@ -445,26 +450,44 @@
     subtract_halo(ids_ref, out_ref, halo_ref, far_of(lax.axis_index("sub")), 0)
 
 
-def finish_kernel(ids_ref, base_ref, halo_ref, *refs, starts, parts, tile, low_tile):
-    pieces, (out_ref, g) = refs[:-2], refs[-2:]
+def rest_kernel(ids_ref, base_ref, *refs, starts, parts, tile, low_tile):
+    pieces, (out_ref, weight_ref, g) = refs[:-3], refs[-3:]
     count = out_ref.shape[0]
     last = count - 1
     out_ref[...] = base_ref[...]
     blocks = [(p, q) for p in range(count) for q in range(count) if last in (p, q)]
     subtract_gram(ids_ref, out_ref, g, (starts, pieces), parts, tile, blocks)
-    subtract_halo(ids_ref, out_ref, halo_ref, near_of(lax.axis_index("sub")), low_tile)
-
-
-def assemble(kernel, ids, arrays, shape, scratch):
+    slots = matches(ids_ref, near_of(lax.axis_index("sub")), low_tile)
+    for m, (place, hit) in enumerate(slots):
+        for i in range(count):
+            weight = jnp.logical_and(hit, place == i).astype(F32)
+            weight_ref[m, i] = jnp.full(weight_ref.shape[2:], weight, F32)
+
+
+def finish_kernel(base_ref, halo_ref, weight_ref, out_ref):
+    count, _, cols = base_ref.shape
+    tile = cols // count
+    for i in range(count):
+        left = [weight_ref[m, i, 0:1] for m in range(PAIR)]
+        for j in range(count):
+            right = [weight_ref[n, j, 0:1] for n in range(PAIR)]
+            block = base_ref[i, :, j * tile : (j + 1) * tile]
+            for m in range(PAIR):
+                for n in range(PAIR):
+                    block = block - (left[m] * right[n]) * halo_ref[m, :, n * tile : (n + 1) * tile]
+            out_ref[i, :, j * tile : (j + 1) * tile] = block
+
+
+def assemble(kernel, ids, arrays, shapes, scratch):
     smem = pl.BlockSpec(memory_space=pltpu.SMEM)
     vmem = pl.BlockSpec(memory_space=pltpu.VMEM)
     return pl.pallas_call(
         kernel,
-        in_specs=[smem] + [vmem] * len(arrays),
-        out_shape=jax.ShapeDtypeStruct(shape, F32),
+        in_specs=[smem] * len(ids) + [vmem] * len(arrays),
+        out_shape=[jax.ShapeDtypeStruct(shape, F32) for shape in shapes],
         scratch_shapes=[pltpu.VMEM(scratch, F32)] if scratch else [],
         compiler_params=pltpu.CompilerParams(vmem_limit_bytes=VMEM_LIMIT),
-    )(ids, *arrays)
+    )(*ids, *arrays)
 
 
 def sizes(count, tile):
@@ -518,11 +541,14 @@
     from_far = lax.ppermute(message, "sub", far)
     kernel = functools.partial(middle_kernel, starts=starts[:-1], parts=rows, tile=tile)
     arrays = [interface_block, from_far] + got[:-1] + own[:-1]
-    base = assemble(kernel, ids, arrays, shape, shape)
+    (base,) = assemble(kernel, [ids], arrays, [shape], shape)
     message = pair(pick(last, None), starts[last:], rows, tile, share, last)
     from_near = lax.ppermute(message, "sub", near)
-    kernel = functools.partial(finish_kernel, starts=starts[-1:], parts=rows, tile=tile, low_tile=last)
-    return assemble(kernel, ids, [base, from_near] + pick(-1, None), shape, shape)[None]
+    kernel = functools.partial(rest_kernel, starts=starts[-1:], parts=rows, tile=tile, low_tile=last)
+    arrays = [base] + pick(-1, None)
+    base, weights = assemble(kernel, [ids], arrays, [shape, (PAIR, count, 8, tile)], shape)
+    (out,) = assemble(finish_kernel, [], [base, from_near, weights], [shape], None)
+    return out[None]
 
 
 def solution(mesh):

time: 71.3 us -> 70 us (0.982)
  waiting for transfers between devices: 34.1 us -> 33 us
    ppermute x6, waiting for transfers between devices: 23.6 us -> 22.9 us  [shards(): recv.append(lax.ppermute(x, 'row', [(stage - 1, stage)]))]
    pallas_call x2 -> x3, Pallas kernels: 2.76 us -> 2.91 us  [assemble(): pl.pallas_call(kernel, in_specs=[smem] * len(ids) + [vmem] * len(arrays),...]
  transfers between devices with their start and end apart: 13 -> 13, of which waited for: 6 -> 7; matrix products, arithmetic and copies ran while one was open for 0% -> 0% of each run, Pallas kernels for 12% -> 13%
where the time goes in v4:
time: 70 us; the launch traced here: 69.6 us
  waiting for transfers between devices  33 us (47%)
  starting transfers between devices  23.4 us (33%)
  Pallas kernels  12.9 us (18%)
    ppermute x6, waiting for transfers between devices, shards(): recv.append(lax.ppermute(x, 'row', [(stage - 1, stage)]))  22.9 us
    ppermute x6, starting transfers between devices, shards(): recv.append(lax.ppermute(x, 'row', [(stage - 1, stage)]))  10.8 us
    ppermute x5, starting transfers between devices, shards(): got.append(lax.ppermute(kept[0] if narrow else piece, 'row', [(1, 0)]))  6.56 us
    pallas_call x1, Pallas kernels, solve(): pl.pallas_call(functools.partial(solve_kernel, chunks=chunks, tiles=tiles...  6.38 us
    ppermute x5, waiting for transfers between devices, shards(): got.append(lax.ppermute(kept[0] if narrow else piece, 'row', [(1, 0)]))  6.35 us
    ppermute x1, starting transfers between devices, shards(): from_far = lax.ppermute(message, 'sub', far)  6 us
    ppermute x1, waiting for transfers between devices, shards(): from_far = lax.ppermute(message, 'sub', far)  3.75 us
    pallas_call x3, Pallas kernels, assemble(): pl.pallas_call(kernel, in_specs=[smem] * len(ids) + [vmem] * len(arrays),...  2.91 us
  transfers between devices with their start and end apart: 13, of which 7 were waited for; matrix products, arithmetic and copies ran while one was open for 0% of the time, Pallas kernels for 13%

profile of v4, /device:TPU:9, one launch (start us, length us, event | category | flops | bytes accessed | tf_op | source)
XLA Modules:
  0.0 69.6 jit_solution(6761701836848612149)
XLA Ops:
  0.0 2.7 %early.1 = f32[512,256]{1,0:T(8,128)} custom-call(s32[4,16]{1,0:T(4,128)} %bitcast.3, f32[1,4,256,256]{3,2,1,0:T(8,128)} %inv_hbm.5, f32[1,1024,512]{2,1,0:T(8,128)} %b_hbm.3), custom_call_target="tpu_custom_call" | custom-call | flops 201326592 | bytes 1048576 | tf_op jit(solution)/shard_map/early/pallas_call | solution.py:127
  2.7 1.3 %collective-permute-start = (f32[512,256]{1,0:T(8,128)}, f32[512,256]{1,0:T(8,128)S(1)}, u32[]{:S(2)}, u32[]{:S(2)}) collective-permute-start(f32[512,256]{1,0:T(8,128)} %early.1), channel_id=1, source_target_pairs={{0,1},{2,3},{4,5},{6,7},{8,9},{10,11},{12,13},{14,15},{16,17},{18,... | collective-permute-start | bytes 1572872 | tf_op jit(solution)/shard_map/ppermute | solution.py:518
  4.0 0.0 copy-start.1
  4.0 0.0 copy-start.4
  4.1 6.4 %others.1 = (f32[512,256]{1,0:T(8,128)}, f32[128,768]{1,0:T(8,128)S(1)}, f32[128,768]{1,0:T(8,128)S(1)}, f32[128,768]{1,0:T(8,128)S(1)}, f32[64,768]{1,0:T(8,128)S(1)}, /*index=5*/f32[64,768]{1,0:T(8,128)S(1)}) custom-call(s32[3,1,4]{2,1,0:T(1,128)S(1)} %bitcast.7, s32[4,16]{1,0:T(4,128)S(1)} %bitcast.4, f32[1,4,3,256,256]{4,3,2,1,0:T(8,128)} %f_hbm.3, ...), custom_call_target="tpu_custom_call" | custom-call | flops 2013265920 | bytes 8388608 | tf_op jit(solution)/shard_map/others/pallas_call | solution.py:191
  10.5 1.3 %collective-permute-start.1 = (f32[128,768]{1,0:T(8,128)S(1)}, f32[128,768]{1,0:T(8,128)S(1)}, u32[]{:S(2)}, u32[]{:S(2)}) collective-permute-start(f32[128,768]{1,0:T(8,128)S(1)} %get-tuple-element.29.refs_3_), channel_id=1, source_target_pairs={{0,1},{2,3},{4,5},{6,7},{8,9},{10,11},{12,13},{14,15},{16,17},{18,... | collective-permute-start | bytes 1179656 | tf_op jit(solution)/shard_map/ppermute | solution.py:518
  11.8 1.3 %collective-permute-start.3 = (f32[128,768]{1,0:T(8,128)S(1)}, f32[128,768]{1,0:T(8,128)S(1)}, u32[]{:S(2)}, u32[]{:S(2)}) collective-permute-start(f32[128,768]{1,0:T(8,128)S(1)} %get-tuple-element.34.refs_3_), channel_id=1, source_target_pairs={{0,1},{2,3},{4,5},{6,7},{8,9},{10,11},{12,13},{14,15},{16,17},{18,... | collective-permute-start | bytes 1179656 | tf_op jit(solution)/shard_map/ppermute | solution.py:518
  13.1 1.3 %collective-permute-start.6 = (f32[128,768]{1,0:T(8,128)S(1)}, f32[128,768]{1,0:T(8,128)S(1)}, u32[]{:S(2)}, u32[]{:S(2)}) collective-permute-start(f32[128,768]{1,0:T(8,128)S(1)} %get-tuple-element.38.refs_3_), channel_id=1, source_target_pairs={{0,1},{2,3},{4,5},{6,7},{8,9},{10,11},{12,13},{14,15},{16,17},{18,... | collective-permute-start | bytes 1179656 | tf_op jit(solution)/shard_map/ppermute | solution.py:518
  14.4 1.4 %collective-permute-start.8 = (f32[64,768]{1,0:T(8,128)S(1)}, f32[64,768]{1,0:T(8,128)S(1)}, u32[]{:S(2)}, u32[]{:S(2)}) collective-permute-start(f32[64,768]{1,0:T(8,128)S(1)} %get-tuple-element.42.refs_3_), channel_id=1, source_target_pairs={{0,1},{2,3},{4,5},{6,7},{8,9},{10,11},{12,13},{14,15},{16,17},{18,... | collective-permute-start | bytes 589832 | tf_op jit(solution)/shard_map/ppermute | solution.py:518
  15.9 0.6 response.1
  16.5 6.9 %collective-permute-done.1.refs_1_ = f32[128,768]{1,0:T(8,128)S(1)} collective-permute-done((f32[128,768]{1,0:T(8,128)S(1)}, f32[128,768]{1,0:T(8,128)S(1)}, u32[]{:S(2)}, u32[]{:S(2)}) %collective-permute-start.1) | collective-permute-done | bytes 393248 | tf_op jit(solution)/shard_map/ppermute | solution.py:518
  23.5 4.1 %collective-permute-start.10 = (f32[64,768]{1,0:T(8,128)S(1)}, f32[64,768]{1,0:T(8,128)S(1)}, u32[]{:S(2)}, u32[]{:S(2)}) collective-permute-start(f32[64,768]{1,0:T(8,128)S(1)} %get-tuple-element.46.refs_3_), channel_id=1, source_target_pairs={{0,1},{2,3},{4,5},{6,7},{8,9},{10,11},{12,13},{14,15},{16,17},{18,... | collective-permute-start | bytes 589832 | tf_op jit(solution)/shard_map/ppermute | solution.py:518
  27.6 0.0 collective-permute-done.refs_0_
  27.6 4.3 %collective-permute-done.3.refs_1_ = f32[128,768]{1,0:T(8,128)S(1)} collective-permute-done((f32[128,768]{1,0:T(8,128)S(1)}, f32[128,768]{1,0:T(8,128)S(1)}, u32[]{:S(2)}, u32[]{:S(2)}) %collective-permute-start.3) | collective-permute-done | bytes 393248 | tf_op jit(solution)/shard_map/ppermute | solution.py:518
  31.9 8.4 %collective-permute-done.6.refs_1_ = f32[128,768]{1,0:T(8,128)S(1)} collective-permute-done((f32[128,768]{1,0:T(8,128)S(1)}, f32[128,768]{1,0:T(8,128)S(1)}, u32[]{:S(2)}, u32[]{:S(2)}) %collective-permute-start.6) | collective-permute-done | bytes 393248 | tf_op jit(solution)/shard_map/ppermute | solution.py:518
  40.3 1.3 %collective-permute-start.7 = (f32[128,384]{1,0:T(8,128)S(1)}, f32[128,384]{1,0:T(8,128)S(1)}, u32[]{:S(2)}, u32[]{:S(2)}) collective-permute-start(f32[128,384]{1,0:T(8,128)S(1)} %get-tuple-element.41.refs_6_.refs_3_), channel_id=1, source_target_pairs={{1,0},{3,2},{5,4},{7,6},{9,8},{11,10},{13,12},{15,14},{17,16},{19,... | collective-permute-start | bytes 589832 | tf_op jit(solution)/shard_map/ppermute | solution.py:530
  41.6 2.9 %collective-permute-done.8.refs_1_ = f32[64,768]{1,0:T(8,128)S(1)} collective-permute-done((f32[64,768]{1,0:T(8,128)S(1)}, f32[64,768]{1,0:T(8,128)S(1)}, u32[]{:S(2)}, u32[]{:S(2)}) %collective-permute-start.8) | collective-permute-done | bytes 196640 | tf_op jit(solution)/shard_map/ppermute | solution.py:518
  44.5 1.3 %collective-permute-start.9 = (f32[64,448]{1,0:T(8,128)S(1)}, f32[64,448]{1,0:T(8,128)S(1)}, u32[]{:S(2)}, u32[]{:S(2)}) collective-permute-start(f32[64,448]{1,0:T(8,128)S(1)} %get-tuple-element.45.refs_7_.refs_4_), channel_id=1, source_target_pairs={{1,0},{3,2},{5,4},{7,6},{9,8},{11,10},{13,12},{15,14},{17,16},{19,... | collective-permute-start | bytes 344072 | tf_op jit(solution)/shard_map/ppermute | solution.py:530
  45.8 1.3 %collective-permute-start.4 = (f32[128,256]{1,0:T(8,128)S(1)}, f32[128,256]{1,0:T(8,128)S(1)}, u32[]{:S(2)}, u32[]{:S(2)}) collective-permute-start(f32[128,256]{1,0:T(8,128)S(1)} %get-tuple-element.37.refs_3_.refs_5_), channel_id=1, source_target_pairs={{1,0},{3,2},{5,4},{7,6},{9,8},{11,10},{13,12},{15,14},{17,16},{19,... | collective-permute-start | bytes 393224 | tf_op jit(solution)/shard_map/ppermute | solution.py:530
  47.1 1.3 %collective-permute-start.2 = (f32[128,128]{1,0:T(8,128)S(1)}, f32[128,128]{1,0:T(8,128)S(1)}, u32[]{:S(2)}, u32[]{:S(2)}) collective-permute-start(f32[128,128]{1,0:T(8,128)S(1)} %get-tuple-element.33.refs_2_.refs_4_), channel_id=1, source_target_pairs={{1,0},{3,2},{5,4},{7,6},{9,8},{11,10},{13,12},{15,14},{17,16},{19,... | collective-permute-start | bytes 196616 | tf_op jit(solution)/shard_map/ppermute | solution.py:530
  48.4 0.3 collective-permute-done.10.refs_1_
  48.8 1.4 %collective-permute-start.11 = (f32[64,256]{1,0:T(8,128)S(1)}, f32[64,256]{1,0:T(8,128)S(1)}, u32[]{:S(2)}, u32[]{:S(2)}) collective-permute-start(f32[64,256]{1,0:T(8,128)S(1)} %get-tuple-element.49), channel_id=1, source_target_pairs={{1,0},{3,2},{5,4},{7,6},{9,8},{11,10},{13,12},{15,14},{17,16},{19,... | collective-permute-start | bytes 196616 | tf_op jit(solution)/shard_map/ppermute | solution.py:530
  50.2 6.3 %collective-permute-done.2.refs_0_ = f32[128,128]{1,0:T(8,128)S(1)} collective-permute-done((f32[128,128]{1,0:T(8,128)S(1)}, f32[128,128]{1,0:T(8,128)S(1)}, u32[]{:S(2)}, u32[]{:S(2)}) %collective-permute-start.2) | collective-permute-done | bytes 65568 | tf_op jit(solution)/shard_map/ppermute | solution.py:530
  56.5 0.1 shard_map.66
  56.6 6.0 %collective-permute-start.5 = (f32[2,64,256]{2,1,0:T(8,128)S(1)}, f32[2,64,256]{2,1,0:T(8,128)S(1)}, u32[]{:S(2)}, u32[]{:S(2)}) collective-permute-start(f32[2,64,256]{2,1,0:T(8,128)S(1)} %shard_map.66), channel_id=1, source_target_pairs={{2,4},{4,2},{6,8},{8,6},{10,12},{12,10},{14,16},{16,14},{18,20},{2... | collective-permute-start | bytes 393224 | tf_op jit(solution)/shard_map/ppermute | solution.py:541
  62.6 0.0 collective-permute-done.9.refs_3_.refs_1_
  62.6 0.2 shard_map.72
  62.8 0.1 collective-permute-start.12
  62.9 3.8 %collective-permute-done.5.halo_ref = f32[2,64,256]{2,1,0:T(8,128)S(1)} collective-permute-done((f32[2,64,256]{2,1,0:T(8,128)S(1)}, f32[2,64,256]{2,1,0:T(8,128)S(1)}, u32[]{:S(2)}, u32[]{:S(2)}) %collective-permute-start.5) | collective-permute-done | bytes 131104 | tf_op jit(solution)/shard_map/ppermute | solution.py:541
  66.7 1.0 %shard_map.69.base_ref = f32[4,64,512]{2,1,0:T(8,128)S(1)} custom-call(s32[4,16]{1,0:T(4,128)S(1)} %bitcast.5, f32[1,4,64,512]{3,2,1,0:T(8,128)S(1)} %copy-done.2, f32[2,64,256]{2,1,0:T(8,128)S(1)} %collective-permute-done.5.halo_ref, f32[128,128]{1,0:T(8,128)S(1)} %collective-permute-done.2.refs_0_, f32[128,256]{1,0:T(8,128)S(1)} %collective-permute-done.4.refs_1_, ...), custom_call_target="tpu_custom_call" | custom-call | tf_op jit(solution)/shard_map/pallas_call | solution.py:484
  67.7 0.9 %shard_map.71 = (f32[4,64,512]{2,1,0:T(8,128)S(1)}, f32[2,4,8,128]{3,2,1,0:T(8,128)S(1)}) custom-call(s32[4,16]{1,0:T(4,128)S(1)} %bitcast.6, f32[4,64,512]{2,1,0:T(8,128)S(1)} %shard_map.69.base_ref, f32[64,256]{1,0:T(8,128)S(1)} %collective-permute-done.11.refs_0_.refs_2_, f32[64,512]{1,0:T(8,128)S(1)} %get-tuple-element.50.refs_1_.refs_5_), custom_call_target="tpu_custom_call" | custom-call | tf_op jit(solution)/shard_map/pallas_call | solution.py:484
  68.6 1.0 %shard_map.73 = f32[4,64,512]{2,1,0:T(8,128)} custom-call(f32[4,64,512]{2,1,0:T(8,128)S(1)} %get-tuple-element.51.base_ref, f32[2,64,256]{2,1,0:T(8,128)S(1)} %collective-permute-done.12.halo_ref, f32[2,4,8,128]{3,2,1,0:T(8,128)S(1)} %get-tuple-element.52.weight_ref), custom_call_target="tpu_custom_call" | custom-call | tf_op jit(solution)/shard_map/pallas_call | solution.py:484
  (19 shorter events, 0.0 us)
Async XLA Ops:
  0.0 4.0 %copy-start.3 = (s32[16,4]{0,1:T(4,128)S(1)}, s32[16,4]{0,1:T(4,128)}, u32[]{:S(2)}) copy-start(s32[16,4]{0,1:T(4,128)} %param.11) | copy-start | bytes 772
  0.0 4.0 %copy-start.5 = (s32[1,4,3]{1,0,2:T(1,128)S(1)}, s32[1,4,3]{1,0,2:T(1,128)}, u32[]{:S(2)}) copy-start(s32[1,4,3]{1,0,2:T(1,128)} %param.8) | copy-start | bytes 148
  2.7 24.9 %collective-permute-start = (f32[512,256]{1,0:T(8,128)}, f32[512,256]{1,0:T(8,128)S(1)}, u32[]{:S(2)}, u32[]{:S(2)}) collective-permute-start(f32[512,256]{1,0:T(8,128)} %early.1), channel_id=1, source_target_pairs={{0,1},{2,3},{4,5},{6,7},{8,9},{10,11},{12,13},{14,15},{16,17},{18,... | collective-permute-start | bytes 1572872 | tf_op jit(solution)/shard_map/ppermute | solution.py:518
  4.0 11.8 %copy-start.1 = (f32[1,4,256,256]{3,2,1,0:T(8,128)S(1)}, f32[1,4,256,256]{3,2,1,0:T(8,128)}, u32[]{:S(2)}) copy-start(f32[1,4,256,256]{3,2,1,0:T(8,128)} %inv_hbm.5) | copy-start | bytes 3145732
  4.0 11.8 %copy-start.4 = (f32[1,4,3,256,256]{4,3,2,1,0:T(8,128)S(1)}, f32[1,4,3,256,256]{4,3,2,1,0:T(8,128)}, u32[]{:S(2)}) copy-start(f32[1,4,3,256,256]{4,3,2,1,0:T(8,128)} %f_hbm.3) | copy-start | bytes 9437188
  10.5 13.0 %collective-permute-start.1 = (f32[128,768]{1,0:T(8,128)S(1)}, f32[128,768]{1,0:T(8,128)S(1)}, u32[]{:S(2)}, u32[]{:S(2)}) collective-permute-start(f32[128,768]{1,0:T(8,128)S(1)} %get-tuple-element.29.refs_3_), channel_id=1, source_target_pairs={{0,1},{2,3},{4,5},{6,7},{8,9},{10,11},{12,13},{14,15},{16,17},{18,... | collective-permute-start | bytes 1179656 | tf_op jit(solution)/shard_map/ppermute | solution.py:518
  11.8 20.1 %collective-permute-start.3 = (f32[128,768]{1,0:T(8,128)S(1)}, f32[128,768]{1,0:T(8,128)S(1)}, u32[]{:S(2)}, u32[]{:S(2)}) collective-permute-start(f32[128,768]{1,0:T(8,128)S(1)} %get-tuple-element.34.refs_3_), channel_id=1, source_target_pairs={{0,1},{2,3},{4,5},{6,7},{8,9},{10,11},{12,13},{14,15},{16,17},{18,... | collective-permute-start | bytes 1179656 | tf_op jit(solution)/shard_map/ppermute | solution.py:518
  13.1 27.2 %collective-permute-start.6 = (f32[128,768]{1,0:T(8,128)S(1)}, f32[128,768]{1,0:T(8,128)S(1)}, u32[]{:S(2)}, u32[]{:S(2)}) collective-permute-start(f32[128,768]{1,0:T(8,128)S(1)} %get-tuple-element.38.refs_3_), channel_id=1, source_target_pairs={{0,1},{2,3},{4,5},{6,7},{8,9},{10,11},{12,13},{14,15},{16,17},{18,... | collective-permute-start | bytes 1179656 | tf_op jit(solution)/shard_map/ppermute | solution.py:518
  14.4 13.2 %copy-start = (f32[512,256]{1,0:T(8,128)S(1)}, f32[512,256]{1,0:T(8,128)}, u32[]{:S(2)}) copy-start(f32[512,256]{1,0:T(8,128)} %get-tuple-element.30.refs_2_) | copy-start | bytes 1572868
  14.4 30.1 %collective-permute-start.8 = (f32[64,768]{1,0:T(8,128)S(1)}, f32[64,768]{1,0:T(8,128)S(1)}, u32[]{:S(2)}, u32[]{:S(2)}) collective-permute-start(f32[64,768]{1,0:T(8,128)S(1)} %get-tuple-element.42.refs_3_), channel_id=1, source_target_pairs={{0,1},{2,3},{4,5},{6,7},{8,9},{10,11},{12,13},{14,15},{16,17},{18,... | collective-permute-start | bytes 589832 | tf_op jit(solution)/shard_map/ppermute | solution.py:518
  23.5 25.3 %collective-permute-start.10 = (f32[64,768]{1,0:T(8,128)S(1)}, f32[64,768]{1,0:T(8,128)S(1)}, u32[]{:S(2)}, u32[]{:S(2)}) collective-permute-start(f32[64,768]{1,0:T(8,128)S(1)} %get-tuple-element.46.refs_3_), channel_id=1, source_target_pairs={{0,1},{2,3},{4,5},{6,7},{8,9},{10,11},{12,13},{14,15},{16,17},{18,... | collective-permute-start | bytes 589832 | tf_op jit(solution)/shard_map/ppermute | solution.py:518
  40.3 22.3 %collective-permute-start.7 = (f32[128,384]{1,0:T(8,128)S(1)}, f32[128,384]{1,0:T(8,128)S(1)}, u32[]{:S(2)}, u32[]{:S(2)}) collective-permute-start(f32[128,384]{1,0:T(8,128)S(1)} %get-tuple-element.41.refs_6_.refs_3_), channel_id=1, source_target_pairs={{1,0},{3,2},{5,4},{7,6},{9,8},{11,10},{13,12},{15,14},{17,16},{19,... | collective-permute-start | bytes 589832 | tf_op jit(solution)/shard_map/ppermute | solution.py:530
  44.5 18.1 %collective-permute-start.9 = (f32[64,448]{1,0:T(8,128)S(1)}, f32[64,448]{1,0:T(8,128)S(1)}, u32[]{:S(2)}, u32[]{:S(2)}) collective-permute-start(f32[64,448]{1,0:T(8,128)S(1)} %get-tuple-element.45.refs_7_.refs_4_), channel_id=1, source_target_pairs={{1,0},{3,2},{5,4},{7,6},{9,8},{11,10},{13,12},{15,14},{17,16},{19,... | collective-permute-start | bytes 344072 | tf_op jit(solution)/shard_map/ppermute | solution.py:530
  45.8 10.7 %collective-permute-start.4 = (f32[128,256]{1,0:T(8,128)S(1)}, f32[128,256]{1,0:T(8,128)S(1)}, u32[]{:S(2)}, u32[]{:S(2)}) collective-permute-start(f32[128,256]{1,0:T(8,128)S(1)} %get-tuple-element.37.refs_3_.refs_5_), channel_id=1, source_target_pairs={{1,0},{3,2},{5,4},{7,6},{9,8},{11,10},{13,12},{15,14},{17,16},{19,... | collective-permute-start | bytes 393224 | tf_op jit(solution)/shard_map/ppermute | solution.py:530
  47.1 9.4 %collective-permute-start.2 = (f32[128,128]{1,0:T(8,128)S(1)}, f32[128,128]{1,0:T(8,128)S(1)}, u32[]{:S(2)}, u32[]{:S(2)}) collective-permute-start(f32[128,128]{1,0:T(8,128)S(1)} %get-tuple-element.33.refs_2_.refs_4_), channel_id=1, source_target_pairs={{1,0},{3,2},{5,4},{7,6},{9,8},{11,10},{13,12},{15,14},{17,16},{19,... | collective-permute-start | bytes 196616 | tf_op jit(solution)/shard_map/ppermute | solution.py:530
  48.8 17.9 %copy-start.2 = (f32[1,4,64,512]{3,2,1,0:T(8,128)S(1)}, f32[1,4,64,512]{3,2,1,0:T(8,128)}, u32[]{:S(2)}) copy-start(f32[1,4,64,512]{3,2,1,0:T(8,128)} %face_ref.1) | copy-start | bytes 1572868
  48.8 13.8 %collective-permute-start.11 = (f32[64,256]{1,0:T(8,128)S(1)}, f32[64,256]{1,0:T(8,128)S(1)}, u32[]{:S(2)}, u32[]{:S(2)}) collective-permute-start(f32[64,256]{1,0:T(8,128)S(1)} %get-tuple-element.49), channel_id=1, source_target_pairs={{1,0},{3,2},{5,4},{7,6},{9,8},{11,10},{13,12},{15,14},{17,16},{19,... | collective-permute-start | bytes 196616 | tf_op jit(solution)/shard_map/ppermute | solution.py:530
  56.6 10.1 %collective-permute-start.5 = (f32[2,64,256]{2,1,0:T(8,128)S(1)}, f32[2,64,256]{2,1,0:T(8,128)S(1)}, u32[]{:S(2)}, u32[]{:S(2)}) collective-permute-start(f32[2,64,256]{2,1,0:T(8,128)S(1)} %shard_map.66), channel_id=1, source_target_pairs={{2,4},{4,2},{6,8},{8,6},{10,12},{12,10},{14,16},{16,14},{18,20},{2... | collective-permute-start | bytes 393224 | tf_op jit(solution)/shard_map/ppermute | solution.py:541
  62.8 5.8 %collective-permute-start.12 = (f32[2,64,256]{2,1,0:T(8,128)S(1)}, f32[2,64,256]{2,1,0:T(8,128)S(1)}, u32[]{:S(2)}, u32[]{:S(2)}) collective-permute-start(f32[2,64,256]{2,1,0:T(8,128)S(1)} %shard_map.72), channel_id=1, source_target_pairs={{0,2},{2,0},{4,6},{6,4},{8,10},{10,8},{12,14},{14,12},{16,18},{18,... | collective-permute-start | bytes 393224 | tf_op jit(solution)/shard_map/ppermute | solution.py:546

commit v5 on v4

--- a/solution.py
+++ b/solution.py
@@ -12,7 +12,7 @@
 BF16 = jnp.bfloat16
 VMEM_LIMIT = 24 * 1024 * 1024
 OTHERS = 52 * 1024 * 1024
-ALONE = 63 * 1024 * 1024
+ALONE = 53 * 1024 * 1024
 PAIR = 2
 LAST = (1, 2)
 
@@ -95,51 +95,56 @@
         finish(i, x)
 
 
-def early_kernel(ids_hbm, inv_hbm, b_hbm, out, ids_ref, inverse, b, x_ref, sems):
+def early_kernel(inv_hbm, b_hbm, out, inverse, b, sems):
     @pl.when(lax.axis_index("row") == 0)
     def _():
-        size = inverse.shape[0]
         copies = [
-            pltpu.make_async_copy(inv_hbm.at[0, 0], inverse, sems.at[0]),
-            pltpu.make_async_copy(b_hbm.at[0, pl.ds(0, size)], b, sems.at[1]),
-            pltpu.make_async_copy(ids_hbm, ids_ref, sems.at[2]),
+            pltpu.make_async_copy(b_hbm.at[0, pl.ds(0, inverse.shape[0])], b, sems.at[0]),
+            pltpu.make_async_copy(inv_hbm.at[0, 0], inverse, sems.at[1]),
         ]
         for copy in copies:
             copy.start()
+        copies[0].wait()
+        right = stacked(b[...].T)
         copies[1].wait()
-        right = stacked(b[...].T)
-        copies[0].wait()
-        x_ref[...] = three(nt, right, *split(inverse[...]))
-        copies[2].wait()
-        order = ordered(ids_ref, lax.axis_index("sub"))
-        tile = x_ref.shape[0] // len(order)
-        writes = []
-        for p, k in enumerate(order):
-            rows = pl.ds(pl.multiple_of(k * tile, tile), tile)
-            writes.append(pltpu.make_async_copy(x_ref.at[rows], out.at[pl.ds(p * tile, tile)], sems.at[3 + p]))
-            writes[-1].start()
-        wait_all(writes)
-
-
-def early_solve(ids, inverses, coupling):
+        out[...] = three(nt, right, *split(inverse[...]))
+
+
+def early_solve(inverses, coupling):
     size, cols = inverses.shape[2], coupling.shape[2]
     hbm = pl.BlockSpec(memory_space=pltpu.HBM)
     return pl.pallas_call(
         early_kernel,
-        in_specs=[hbm] * 3,
-        out_specs=hbm,
+        in_specs=[hbm] * 2,
         out_shape=jax.ShapeDtypeStruct((cols, size), F32),
         scratch_shapes=[
-            pltpu.SMEM(ids.shape, jnp.int32),
             pltpu.VMEM((size, size), F32),
             pltpu.VMEM((size, cols), F32),
-            pltpu.VMEM((cols, size), F32),
-            pltpu.SemaphoreType.DMA((3 + ids.shape[0],)),
+            pltpu.SemaphoreType.DMA((2,)),
         ],
         compiler_params=pltpu.CompilerParams(vmem_limit_bytes=ALONE),
         cost_estimate=pl.CostEstimate(flops=6 * size * size * cols, bytes_accessed=1 << 20, transcendentals=0),
         name="early",
-    )(ids, inverses, coupling)
+    )(inverses, coupling)
+
+
+def arrange_kernel(ids_ref, x_ref, out):
+    @pl.when(lax.axis_index("row") > 0)
+    def _():
+        order = ordered(ids_ref, lax.axis_index("sub"))
+        tile = x_ref.shape[0] // len(order)
+        for p, k in enumerate(order):
+            out[p * tile : (p + 1) * tile] = x_ref[pl.ds(pl.multiple_of(k * tile, tile), tile)]
+
+
+def arrange(ids, x):
+    return pl.pallas_call(
+        arrange_kernel,
+        in_specs=[pl.BlockSpec(memory_space=pltpu.SMEM), pl.BlockSpec(memory_space=pltpu.VMEM)],
+        out_shape=jax.ShapeDtypeStruct(x.shape, F32),
+        compiler_params=pltpu.CompilerParams(vmem_limit_bytes=VMEM_LIMIT),
+        name="arrange",
+    )(ids, x)
 
 
 def solve_kernel(off_ref, ids_ref, f_hbm, inv_hbm, b_hbm, top, *rest, chunks, tiles):
@@ -507,7 +512,7 @@
     far = [(s, s - 1 + 2 * (s % 2)) for s in range(subs)]
     near = [(s, s + 1 - 2 * (s % 2)) for s in range(subs)]
     far, near = ([(s, t) for s, t in pairs if 0 <= t < subs] for pairs in (far, near))
-    early = early_solve(ids, block_inverses, coupling) if rows == 2 else None
+    early = early_solve(block_inverses, coupling) if rows == 2 else None
     ys = list(solve(offsets, ids, factor_blocks, block_inverses, coupling, chunks, tile))
     gain = response(offsets, factor_blocks, block_inverses)
     xs = [early] + ys[1:] if rows == 2 else ys
@@ -516,6 +521,8 @@
         recv = []
         for x in xs:
             recv.append(lax.ppermute(x, "row", [(stage - 1, stage)]))
+        if rows == 2:
+            recv[0] = arrange(ids, recv[0])
         first = first or recv
         if rows > 2:
             xs = list(update(recv, ys, xs, gain, chunks, stage))

time: 70 us -> 69.2 us (0.989)
  waiting for transfers between devices: 33 us -> 26.6 us
  starting transfers between devices: 23.4 us -> 29.2 us
    ppermute x6, waiting for transfers between devices: 22.9 us -> 16.1 us  [shards(): recv.append(lax.ppermute(x, 'row', [(stage - 1, stage)]))]
    ppermute x6, starting transfers between devices: 10.8 us -> 16.5 us  [shards(): recv.append(lax.ppermute(x, 'row', [(stage - 1, stage)]))]
    pallas_call x1 -> x2, Pallas kernels: 2.68 us -> 2.28 us  [the longest x1 1.71 us: early_solve(): pl.pallas_call(early_kernel, in_specs=[hbm] * 2, out_shape=jax.ShapeDtype...]
  transfers between devices with their start and end apart: 13 -> 13, of which waited for: 7 -> 6; matrix products, arithmetic and copies ran while one was open for 0% -> 0% of each run, Pallas kernels for 13% -> 14%
where the time goes in v5:
time: 69.2 us; the launch traced here: 68.8 us
  starting transfers between devices  29.2 us (42%)
  waiting for transfers between devices  26.6 us (38%)
  Pallas kernels  12.6 us (18%)
    ppermute x6, starting transfers between devices, shards(): recv.append(lax.ppermute(x, 'row', [(stage - 1, stage)]))  16.5 us
    ppermute x6, waiting for transfers between devices, shards(): recv.append(lax.ppermute(x, 'row', [(stage - 1, stage)]))  16.1 us
    ppermute x5, waiting for transfers between devices, shards(): got.append(lax.ppermute(kept[0] if narrow else piece, 'row', [(1, 0)]))  6.79 us
    ppermute x5, starting transfers between devices, shards(): got.append(lax.ppermute(kept[0] if narrow else piece, 'row', [(1, 0)]))  6.56 us
    pallas_call x1, Pallas kernels, solve(): pl.pallas_call(functools.partial(solve_kernel, chunks=chunks, tiles=tiles...  6.35 us
    ppermute x1, starting transfers between devices, shards(): from_far = lax.ppermute(message, 'sub', far)  6.04 us
    ppermute x1, waiting for transfers between devices, shards(): from_far = lax.ppermute(message, 'sub', far)  3.75 us
    pallas_call x3, Pallas kernels, assemble(): pl.pallas_call(kernel, in_specs=[smem] * len(ids) + [vmem] * len(arrays),...  2.91 us
  transfers between devices with their start and end apart: 13, of which 6 were waited for; matrix products, arithmetic and copies ran while one was open for 0% of the time, Pallas kernels for 14%

profile of v5, /device:TPU:9, one launch (start us, length us, event | category | flops | bytes accessed | tf_op | source)
XLA Modules:
  0.0 68.8 jit_solution(10520425802595983448)
XLA Ops:
  0.0 1.7 %early.1 = f32[512,256]{1,0:T(8,128)S(1)} custom-call(f32[1,4,256,256]{3,2,1,0:T(8,128)} %inv_hbm.5, f32[1,1024,512]{2,1,0:T(8,128)} %b_hbm.3), custom_call_target="tpu_custom_call" | custom-call | flops 201326592 | bytes 1048576 | tf_op jit(solution)/shard_map/early/pallas_call | solution.py:116
  1.7 1.5 %collective-permute-start = (f32[512,256]{1,0:T(8,128)S(1)}, f32[512,256]{1,0:T(8,128)S(1)}, u32[]{:S(2)}, u32[]{:S(2)}) collective-permute-start(f32[512,256]{1,0:T(8,128)S(1)} %early.1), channel_id=1, source_target_pairs={{0,1},{2,3},{4,5},{6,7},{8,9},{10,11},{12,13},{14,15},{16,17},{18,... | collective-permute-start | bytes 1572872 | tf_op jit(solution)/shard_map/ppermute | solution.py:523
  3.2 0.0 copy-start.1
  3.2 0.0 copy-start.4
  3.3 6.4 %others.1 = (f32[512,256]{1,0:T(8,128)}, f32[128,768]{1,0:T(8,128)S(1)}, f32[128,768]{1,0:T(8,128)S(1)}, f32[128,768]{1,0:T(8,128)S(1)}, f32[64,768]{1,0:T(8,128)S(1)}, /*index=5*/f32[64,768]{1,0:T(8,128)S(1)}) custom-call(s32[3,1,4]{2,1,0:T(1,128)S(1)} %bitcast.7, s32[4,16]{1,0:T(4,128)S(1)} %bitcast.3, f32[1,4,3,256,256]{4,3,2,1,0:T(8,128)} %f_hbm.3, ...), custom_call_target="tpu_custom_call" | custom-call | flops 2013265920 | bytes 8388608 | tf_op jit(solution)/shard_map/others/pallas_call | solution.py:196
  9.6 1.3 %collective-permute-start.1 = (f32[128,768]{1,0:T(8,128)S(1)}, f32[128,768]{1,0:T(8,128)S(1)}, u32[]{:S(2)}, u32[]{:S(2)}) collective-permute-start(f32[128,768]{1,0:T(8,128)S(1)} %get-tuple-element.29.refs_3_), channel_id=1, source_target_pairs={{0,1},{2,3},{4,5},{6,7},{8,9},{10,11},{12,13},{14,15},{16,17},{18,... | collective-permute-start | bytes 1179656 | tf_op jit(solution)/shard_map/ppermute | solution.py:523
  10.9 1.3 %collective-permute-start.3 = (f32[128,768]{1,0:T(8,128)S(1)}, f32[128,768]{1,0:T(8,128)S(1)}, u32[]{:S(2)}, u32[]{:S(2)}) collective-permute-start(f32[128,768]{1,0:T(8,128)S(1)} %get-tuple-element.34.refs_3_), channel_id=1, source_target_pairs={{0,1},{2,3},{4,5},{6,7},{8,9},{10,11},{12,13},{14,15},{16,17},{18,... | collective-permute-start | bytes 1179656 | tf_op jit(solution)/shard_map/ppermute | solution.py:523
  12.3 1.3 %collective-permute-start.6 = (f32[128,768]{1,0:T(8,128)S(1)}, f32[128,768]{1,0:T(8,128)S(1)}, u32[]{:S(2)}, u32[]{:S(2)}) collective-permute-start(f32[128,768]{1,0:T(8,128)S(1)} %get-tuple-element.38.refs_3_), channel_id=1, source_target_pairs={{0,1},{2,3},{4,5},{6,7},{8,9},{10,11},{12,13},{14,15},{16,17},{18,... | collective-permute-start | bytes 1179656 | tf_op jit(solution)/shard_map/ppermute | solution.py:523
  13.6 0.0 copy-start
  13.6 1.4 %collective-permute-start.8 = (f32[64,768]{1,0:T(8,128)S(1)}, f32[64,768]{1,0:T(8,128)S(1)}, u32[]{:S(2)}, u32[]{:S(2)}) collective-permute-start(f32[64,768]{1,0:T(8,128)S(1)} %get-tuple-element.42.refs_3_), channel_id=1, source_target_pairs={{0,1},{2,3},{4,5},{6,7},{8,9},{10,11},{12,13},{14,15},{16,17},{18,... | collective-permute-start | bytes 589832 | tf_op jit(solution)/shard_map/ppermute | solution.py:523
  15.1 0.6 response.1
  15.7 9.7 %collective-permute-start.10 = (f32[64,768]{1,0:T(8,128)S(1)}, f32[64,768]{1,0:T(8,128)S(1)}, u32[]{:S(2)}, u32[]{:S(2)}) collective-permute-start(f32[64,768]{1,0:T(8,128)S(1)} %get-tuple-element.46.refs_3_), channel_id=1, source_target_pairs={{0,1},{2,3},{4,5},{6,7},{8,9},{10,11},{12,13},{14,15},{16,17},{18,... | collective-permute-start | bytes 589832 | tf_op jit(solution)/shard_map/ppermute | solution.py:523
  25.4 0.6 arrange.1.refs_0_
  26.0 0.2 shard_map.64
  26.2 4.4 %collective-permute-done.3.refs_1_ = f32[128,768]{1,0:T(8,128)S(1)} collective-permute-done((f32[128,768]{1,0:T(8,128)S(1)}, f32[128,768]{1,0:T(8,128)S(1)}, u32[]{:S(2)}, u32[]{:S(2)}) %collective-permute-start.3) | collective-permute-done | bytes 393248 | tf_op jit(solution)/shard_map/ppermute | solution.py:523
  30.6 8.4 %collective-permute-done.6.refs_1_ = f32[128,768]{1,0:T(8,128)S(1)} collective-permute-done((f32[128,768]{1,0:T(8,128)S(1)}, f32[128,768]{1,0:T(8,128)S(1)}, u32[]{:S(2)}, u32[]{:S(2)}) %collective-permute-start.6) | collective-permute-done | bytes 393248 | tf_op jit(solution)/shard_map/ppermute | solution.py:523
  39.1 1.3 %collective-permute-start.7 = (f32[128,384]{1,0:T(8,128)S(1)}, f32[128,384]{1,0:T(8,128)S(1)}, u32[]{:S(2)}, u32[]{:S(2)}) collective-permute-start(f32[128,384]{1,0:T(8,128)S(1)} %get-tuple-element.41.refs_6_.refs_3_), channel_id=1, source_target_pairs={{1,0},{3,2},{5,4},{7,6},{9,8},{11,10},{13,12},{15,14},{17,16},{19,... | collective-permute-start | bytes 589832 | tf_op jit(solution)/shard_map/ppermute | solution.py:537
  40.3 2.9 %collective-permute-done.8.refs_1_ = f32[64,768]{1,0:T(8,128)S(1)} collective-permute-done((f32[64,768]{1,0:T(8,128)S(1)}, f32[64,768]{1,0:T(8,128)S(1)}, u32[]{:S(2)}, u32[]{:S(2)}) %collective-permute-start.8) | collective-permute-done | bytes 196640 | tf_op jit(solution)/shard_map/ppermute | solution.py:523
  43.3 1.3 %collective-permute-start.9 = (f32[64,448]{1,0:T(8,128)S(1)}, f32[64,448]{1,0:T(8,128)S(1)}, u32[]{:S(2)}, u32[]{:S(2)}) collective-permute-start(f32[64,448]{1,0:T(8,128)S(1)} %get-tuple-element.45.refs_7_.refs_4_), channel_id=1, source_target_pairs={{1,0},{3,2},{5,4},{7,6},{9,8},{11,10},{13,12},{15,14},{17,16},{19,... | collective-permute-start | bytes 344072 | tf_op jit(solution)/shard_map/ppermute | solution.py:537
  44.6 1.3 %collective-permute-start.4 = (f32[128,256]{1,0:T(8,128)S(1)}, f32[128,256]{1,0:T(8,128)S(1)}, u32[]{:S(2)}, u32[]{:S(2)}) collective-permute-start(f32[128,256]{1,0:T(8,128)S(1)} %get-tuple-element.37.refs_3_.refs_5_), channel_id=1, source_target_pairs={{1,0},{3,2},{5,4},{7,6},{9,8},{11,10},{13,12},{15,14},{17,16},{19,... | collective-permute-start | bytes 393224 | tf_op jit(solution)/shard_map/ppermute | solution.py:537
  45.9 1.3 %collective-permute-start.2 = (f32[128,128]{1,0:T(8,128)S(1)}, f32[128,128]{1,0:T(8,128)S(1)}, u32[]{:S(2)}, u32[]{:S(2)}) collective-permute-start(f32[128,128]{1,0:T(8,128)S(1)} %get-tuple-element.33.refs_2_.refs_4_), channel_id=1, source_target_pairs={{1,0},{3,2},{5,4},{7,6},{9,8},{11,10},{13,12},{15,14},{17,16},{19,... | collective-permute-start | bytes 196616 | tf_op jit(solution)/shard_map/ppermute | solution.py:537
  47.2 0.3 collective-permute-done.10.refs_1_
  47.5 1.4 %collective-permute-start.11 = (f32[64,256]{1,0:T(8,128)S(1)}, f32[64,256]{1,0:T(8,128)S(1)}, u32[]{:S(2)}, u32[]{:S(2)}) collective-permute-start(f32[64,256]{1,0:T(8,128)S(1)} %get-tuple-element.49), channel_id=1, source_target_pairs={{1,0},{3,2},{5,4},{7,6},{9,8},{11,10},{13,12},{15,14},{17,16},{19,... | collective-permute-start | bytes 196616 | tf_op jit(solution)/shard_map/ppermute | solution.py:537
  48.9 6.8 %collective-permute-done.2.refs_0_ = f32[128,128]{1,0:T(8,128)S(1)} collective-permute-done((f32[128,128]{1,0:T(8,128)S(1)}, f32[128,128]{1,0:T(8,128)S(1)}, u32[]{:S(2)}, u32[]{:S(2)}) %collective-permute-start.2) | collective-permute-done | bytes 65568 | tf_op jit(solution)/shard_map/ppermute | solution.py:537
  55.7 0.1 shard_map.66
  55.8 6.0 %collective-permute-start.5 = (f32[2,64,256]{2,1,0:T(8,128)S(1)}, f32[2,64,256]{2,1,0:T(8,128)S(1)}, u32[]{:S(2)}, u32[]{:S(2)}) collective-permute-start(f32[2,64,256]{2,1,0:T(8,128)S(1)} %shard_map.66), channel_id=1, source_target_pairs={{2,4},{4,2},{6,8},{8,6},{10,12},{12,10},{14,16},{16,14},{18,20},{2... | collective-permute-start | bytes 393224 | tf_op jit(solution)/shard_map/ppermute | solution.py:548
  61.8 0.2 shard_map.72
  62.0 0.1 collective-permute-start.12
  62.1 3.8 %collective-permute-done.5.halo_ref = f32[2,64,256]{2,1,0:T(8,128)S(1)} collective-permute-done((f32[2,64,256]{2,1,0:T(8,128)S(1)}, f32[2,64,256]{2,1,0:T(8,128)S(1)}, u32[]{:S(2)}, u32[]{:S(2)}) %collective-permute-start.5) | collective-permute-done | bytes 131104 | tf_op jit(solution)/shard_map/ppermute | solution.py:548
  65.8 1.0 %shard_map.69.base_ref = f32[4,64,512]{2,1,0:T(8,128)S(1)} custom-call(s32[4,16]{1,0:T(4,128)S(1)} %bitcast.5, f32[1,4,64,512]{3,2,1,0:T(8,128)S(1)} %copy-done.2, f32[2,64,256]{2,1,0:T(8,128)S(1)} %collective-permute-done.5.halo_ref, f32[128,128]{1,0:T(8,128)S(1)} %collective-permute-done.2.refs_0_, f32[128,256]{1,0:T(8,128)S(1)} %collective-permute-done.4.refs_1_, ...), custom_call_target="tpu_custom_call" | custom-call | tf_op jit(solution)/shard_map/pallas_call | solution.py:489
  66.9 0.9 %shard_map.71 = (f32[4,64,512]{2,1,0:T(8,128)S(1)}, f32[2,4,8,128]{3,2,1,0:T(8,128)S(1)}) custom-call(s32[4,16]{1,0:T(4,128)S(1)} %bitcast.6, f32[4,64,512]{2,1,0:T(8,128)S(1)} %shard_map.69.base_ref, f32[64,256]{1,0:T(8,128)S(1)} %collective-permute-done.11.refs_0_.refs_2_, f32[64,512]{1,0:T(8,128)S(1)} %get-tuple-element.50.refs_1_.refs_5_), custom_call_target="tpu_custom_call" | custom-call | tf_op jit(solution)/shard_map/pallas_call | solution.py:489
  67.8 1.0 %shard_map.73 = f32[4,64,512]{2,1,0:T(8,128)} custom-call(f32[4,64,512]{2,1,0:T(8,128)S(1)} %get-tuple-element.51.base_ref, f32[2,64,256]{2,1,0:T(8,128)S(1)} %collective-permute-done.12.halo_ref, f32[2,4,8,128]{3,2,1,0:T(8,128)S(1)} %get-tuple-element.52.weight_ref), custom_call_target="tpu_custom_call" | custom-call | tf_op jit(solution)/shard_map/pallas_call | solution.py:489
  (20 shorter events, 0.0 us)
Async XLA Ops:
  0.0 3.2 %copy-start.3 = (s32[16,4]{0,1:T(4,128)S(1)}, s32[16,4]{0,1:T(4,128)}, u32[]{:S(2)}) copy-start(s32[16,4]{0,1:T(4,128)} %param.11) | copy-start | bytes 772
  0.0 3.2 %copy-start.5 = (s32[1,4,3]{1,0,2:T(1,128)S(1)}, s32[1,4,3]{1,0,2:T(1,128)}, u32[]{:S(2)}) copy-start(s32[1,4,3]{1,0,2:T(1,128)} %param.8) | copy-start | bytes 148
  1.7 14.0 %collective-permute-start = (f32[512,256]{1,0:T(8,128)S(1)}, f32[512,256]{1,0:T(8,128)S(1)}, u32[]{:S(2)}, u32[]{:S(2)}) collective-permute-start(f32[512,256]{1,0:T(8,128)S(1)} %early.1), channel_id=1, source_target_pairs={{0,1},{2,3},{4,5},{6,7},{8,9},{10,11},{12,13},{14,15},{16,17},{18,... | collective-permute-start | bytes 1572872 | tf_op jit(solution)/shard_map/ppermute | solution.py:523
  3.2 11.8 %copy-start.1 = (f32[1,4,256,256]{3,2,1,0:T(8,128)S(1)}, f32[1,4,256,256]{3,2,1,0:T(8,128)}, u32[]{:S(2)}) copy-start(f32[1,4,256,256]{3,2,1,0:T(8,128)} %inv_hbm.5) | copy-start | bytes 3145732
  3.2 11.8 %copy-start.4 = (f32[1,4,3,256,256]{4,3,2,1,0:T(8,128)S(1)}, f32[1,4,3,256,256]{4,3,2,1,0:T(8,128)}, u32[]{:S(2)}) copy-start(f32[1,4,3,256,256]{4,3,2,1,0:T(8,128)} %f_hbm.3) | copy-start | bytes 9437188
  9.6 16.4 %collective-permute-start.1 = (f32[128,768]{1,0:T(8,128)S(1)}, f32[128,768]{1,0:T(8,128)S(1)}, u32[]{:S(2)}, u32[]{:S(2)}) collective-permute-start(f32[128,768]{1,0:T(8,128)S(1)} %get-tuple-element.29.refs_3_), channel_id=1, source_target_pairs={{0,1},{2,3},{4,5},{6,7},{8,9},{10,11},{12,13},{14,15},{16,17},{18,... | collective-permute-start | bytes 1179656 | tf_op jit(solution)/shard_map/ppermute | solution.py:523
  10.9 19.7 %collective-permute-start.3 = (f32[128,768]{1,0:T(8,128)S(1)}, f32[128,768]{1,0:T(8,128)S(1)}, u32[]{:S(2)}, u32[]{:S(2)}) collective-permute-start(f32[128,768]{1,0:T(8,128)S(1)} %get-tuple-element.34.refs_3_), channel_id=1, source_target_pairs={{0,1},{2,3},{4,5},{6,7},{8,9},{10,11},{12,13},{14,15},{16,17},{18,... | collective-permute-start | bytes 1179656 | tf_op jit(solution)/shard_map/ppermute | solution.py:523
  12.3 26.8 %collective-permute-start.6 = (f32[128,768]{1,0:T(8,128)S(1)}, f32[128,768]{1,0:T(8,128)S(1)}, u32[]{:S(2)}, u32[]{:S(2)}) collective-permute-start(f32[128,768]{1,0:T(8,128)S(1)} %get-tuple-element.38.refs_3_), channel_id=1, source_target_pairs={{0,1},{2,3},{4,5},{6,7},{8,9},{10,11},{12,13},{14,15},{16,17},{18,... | collective-permute-start | bytes 1179656 | tf_op jit(solution)/shard_map/ppermute | solution.py:523
  13.6 12.4 %copy-start = (f32[512,256]{1,0:T(8,128)S(1)}, f32[512,256]{1,0:T(8,128)}, u32[]{:S(2)}) copy-start(f32[512,256]{1,0:T(8,128)} %get-tuple-element.30.refs_2_) | copy-start | bytes 1572868
  13.6 29.7 %collective-permute-start.8 = (f32[64,768]{1,0:T(8,128)S(1)}, f32[64,768]{1,0:T(8,128)S(1)}, u32[]{:S(2)}, u32[]{:S(2)}) collective-permute-start(f32[64,768]{1,0:T(8,128)S(1)} %get-tuple-element.42.refs_3_), channel_id=1, source_target_pairs={{0,1},{2,3},{4,5},{6,7},{8,9},{10,11},{12,13},{14,15},{16,17},{18,... | collective-permute-start | bytes 589832 | tf_op jit(solution)/shard_map/ppermute | solution.py:523
  15.7 31.8 %collective-permute-start.10 = (f32[64,768]{1,0:T(8,128)S(1)}, f32[64,768]{1,0:T(8,128)S(1)}, u32[]{:S(2)}, u32[]{:S(2)}) collective-permute-start(f32[64,768]{1,0:T(8,128)S(1)} %get-tuple-element.46.refs_3_), channel_id=1, source_target_pairs={{0,1},{2,3},{4,5},{6,7},{8,9},{10,11},{12,13},{14,15},{16,17},{18,... | collective-permute-start | bytes 589832 | tf_op jit(solution)/shard_map/ppermute | solution.py:523
  39.1 22.8 %collective-permute-start.7 = (f32[128,384]{1,0:T(8,128)S(1)}, f32[128,384]{1,0:T(8,128)S(1)}, u32[]{:S(2)}, u32[]{:S(2)}) collective-permute-start(f32[128,384]{1,0:T(8,128)S(1)} %get-tuple-element.41.refs_6_.refs_3_), channel_id=1, source_target_pairs={{1,0},{3,2},{5,4},{7,6},{9,8},{11,10},{13,12},{15,14},{17,16},{19,... | collective-permute-start | bytes 589832 | tf_op jit(solution)/shard_map/ppermute | solution.py:537
  43.3 18.5 %collective-permute-start.9 = (f32[64,448]{1,0:T(8,128)S(1)}, f32[64,448]{1,0:T(8,128)S(1)}, u32[]{:S(2)}, u32[]{:S(2)}) collective-permute-start(f32[64,448]{1,0:T(8,128)S(1)} %get-tuple-element.45.refs_7_.refs_4_), channel_id=1, source_target_pairs={{1,0},{3,2},{5,4},{7,6},{9,8},{11,10},{13,12},{15,14},{17,16},{19,... | collective-permute-start | bytes 344072 | tf_op jit(solution)/shard_map/ppermute | solution.py:537
  44.6 11.1 %collective-permute-start.4 = (f32[128,256]{1,0:T(8,128)S(1)}, f32[128,256]{1,0:T(8,128)S(1)}, u32[]{:S(2)}, u32[]{:S(2)}) collective-permute-start(f32[128,256]{1,0:T(8,128)S(1)} %get-tuple-element.37.refs_3_.refs_5_), channel_id=1, source_target_pairs={{1,0},{3,2},{5,4},{7,6},{9,8},{11,10},{13,12},{15,14},{17,16},{19,... | collective-permute-start | bytes 393224 | tf_op jit(solution)/shard_map/ppermute | solution.py:537
  45.9 9.8 %collective-permute-start.2 = (f32[128,128]{1,0:T(8,128)S(1)}, f32[128,128]{1,0:T(8,128)S(1)}, u32[]{:S(2)}, u32[]{:S(2)}) collective-permute-start(f32[128,128]{1,0:T(8,128)S(1)} %get-tuple-element.33.refs_2_.refs_4_), channel_id=1, source_target_pairs={{1,0},{3,2},{5,4},{7,6},{9,8},{11,10},{13,12},{15,14},{17,16},{19,... | collective-permute-start | bytes 196616 | tf_op jit(solution)/shard_map/ppermute | solution.py:537
  47.5 18.4 %copy-start.2 = (f32[1,4,64,512]{3,2,1,0:T(8,128)S(1)}, f32[1,4,64,512]{3,2,1,0:T(8,128)}, u32[]{:S(2)}) copy-start(f32[1,4,64,512]{3,2,1,0:T(8,128)} %face_ref.1) | copy-start | bytes 1572868
  47.5 14.3 %collective-permute-start.11 = (f32[64,256]{1,0:T(8,128)S(1)}, f32[64,256]{1,0:T(8,128)S(1)}, u32[]{:S(2)}, u32[]{:S(2)}) collective-permute-start(f32[64,256]{1,0:T(8,128)S(1)} %get-tuple-element.49), channel_id=1, source_target_pairs={{1,0},{3,2},{5,4},{7,6},{9,8},{11,10},{13,12},{15,14},{17,16},{19,... | collective-permute-start | bytes 196616 | tf_op jit(solution)/shard_map/ppermute | solution.py:537
  55.8 10.1 %collective-permute-start.5 = (f32[2,64,256]{2,1,0:T(8,128)S(1)}, f32[2,64,256]{2,1,0:T(8,128)S(1)}, u32[]{:S(2)}, u32[]{:S(2)}) collective-permute-start(f32[2,64,256]{2,1,0:T(8,128)S(1)} %shard_map.66), channel_id=1, source_target_pairs={{2,4},{4,2},{6,8},{8,6},{10,12},{12,10},{14,16},{16,14},{18,20},{2... | collective-permute-start | bytes 393224 | tf_op jit(solution)/shard_map/ppermute | solution.py:548
  62.0 5.8 %collective-permute-start.12 = (f32[2,64,256]{2,1,0:T(8,128)S(1)}, f32[2,64,256]{2,1,0:T(8,128)S(1)}, u32[]{:S(2)}, u32[]{:S(2)}) collective-permute-start(f32[2,64,256]{2,1,0:T(8,128)S(1)} %shard_map.72), channel_id=1, source_target_pairs={{0,2},{2,0},{4,6},{6,4},{8,10},{10,8},{12,14},{14,12},{16,18},{18,... | collective-permute-start | bytes 393224 | tf_op jit(solution)/shard_map/ppermute | solution.py:553

commit v6 on v5

--- a/solution.py
+++ b/solution.py
@@ -306,6 +306,7 @@
     piece, rest = refs[0], refs[1:]
     n = recv_ref.shape[0]
     here = slice(start, start + n)
+    at, inner = start // tile, start % tile
 
     @pl.when(lax.axis_index("row") > 0)
     def _():
@@ -317,16 +318,35 @@
         high = jnp.concatenate([recv[:n], x[:n]], axis=1)
         low = jnp.concatenate([recv[n:], x[n:]], axis=1)
         both = jnp.concatenate([high, low], axis=0)
-        if start:
+        if share and last:
+            middle = oldh_ref.shape[1] // 2
+            piece[...] = three(nn, both, oldh_ref[:, :middle], oldl_ref[:, :middle])
+            rest[0][...] = both
+            return
+        if start and share:
+            middle = oldh_ref.shape[1] // 2
+            stop = middle + at * share
+            wide = three(nn, both, oldh_ref[:, :stop], oldl_ref[:, :stop])
+            for t in range(at):
+                for part in range(2):
+                    first = part * middle + t * share
+                    left = t * tile + part * share
+                    piece[:, left : left + share] = wide[:, first : first + share]
+        elif start:
             piece[:, :start] = three(nn, both, oldh_ref[:, :start], oldl_ref[:, :start])
         piece[:, here] = three(nt, both, high, low)
-        if not last:
-            rest[0][:, here] = high.T
-            rest[1][:, here] = low.T
-        elif share:
-            rest[0][...] = jnp.concatenate(
-                [piece[:, t * tile : t * tile + share] for t in range((start + n) // tile)], axis=1
-            )
+        if last:
+            return
+        for target, value in zip(rest, (high.T, low.T)):
+            if not share:
+                target[:, here] = value
+                continue
+            middle = target.shape[1] // 2
+            for part in range(2):
+                first, stop = max(inner, part * share), min(inner + n, (part + 1) * share)
+                if first < stop:
+                    left = part * middle + at * share + first - part * share
+                    target[:, left : left + stop - first] = value[:, first - inner : stop - inner]
 
     if clear:
 
@@ -340,16 +360,18 @@
     half = recv[0].shape[1] + recv[1].shape[1]
     last = start + n == total
     inputs = [*recv, *y, *gain, *kept]
+    if last and share:
+        shapes = [jax.ShapeDtypeStruct((n, total // 2), F32), jax.ShapeDtypeStruct((2 * n, 2 * half), BF16)]
+    else:
+        shapes = [jax.ShapeDtypeStruct((n, start + n), F32)]
     if not last:
-        more = [jax.ShapeDtypeStruct((2 * half, total), BF16)] * 2
-    else:
-        more = [jax.ShapeDtypeStruct((n, total // tile * share), F32)] if share else []
+        shapes += [jax.ShapeDtypeStruct((2 * half, total), BF16)] * 2
     results = pl.pallas_call(
         functools.partial(
             gram_kernel, start=start, fused=bool(gain), clear=clear, last=last, share=share, tile=tile
         ),
         in_specs=[pl.BlockSpec(memory_space=pltpu.VMEM)] * len(inputs),
-        out_shape=[jax.ShapeDtypeStruct((n, start + n), F32)] + more,
+        out_shape=shapes,
         input_output_aliases={len(inputs) - 2 + i: 1 + i for i in range(2)} if start and not last else {},
         compiler_params=pltpu.CompilerParams(vmem_limit_bytes=VMEM_LIMIT),
         cost_estimate=pl.CostEstimate(
@@ -359,11 +381,45 @@
     return results[0], list(results[1:])
 
 
+def widen_kernel(both_ref, oldh_ref, oldl_ref, out):
+    n = out.shape[0]
+    middle = out.shape[1]
+    stop = middle - n
+
+    @pl.when(lax.axis_index("row") > 0)
+    def _():
+        both = both_ref[...]
+        columns = slice(middle, middle + stop)
+        out[:, :stop] = three(nn, both, oldh_ref[:, columns], oldl_ref[:, columns])
+        out[:, stop:] = three(nt, both, both[:n], both[n:])
+
+
+def widen(both, kept):
+    n, total = both.shape[0] // 2, kept[0].shape[1]
+    return pl.pallas_call(
+        widen_kernel,
+        out_shape=jax.ShapeDtypeStruct((n, total // 2), F32),
+        compiler_params=pltpu.CompilerParams(vmem_limit_bytes=VMEM_LIMIT),
+        cost_estimate=pl.CostEstimate(flops=6 * n * both.shape[1] * total, bytes_accessed=4 << 20, transcendentals=0),
+        name="widen",
+    )(both, *kept)
+
+
 def fill(out, chunks, part, tile, low_tile):
     share = out.shape[1]
     low, high = part * share, (part + 1) * share
     base = low_tile * tile
     for start, piece in chunks:
+        if isinstance(piece, tuple):
+            narrow, wide = piece
+            n, at = narrow.shape[0], start // tile
+            for t in range(low_tile, at + 1):
+                left, columns = t * tile - base, slice(t * share, (t + 1) * share)
+                out[at - low_tile, :, left : left + share] = narrow[:, columns]
+                out[at - low_tile, :, left + share : left + tile] = wide[:, columns]
+                if t < at:
+                    out[t - low_tile, :, start - base : start - base + n] = wide[:, columns].T
+            continue
         n = piece.shape[0]
         at, inner = start // tile, start % tile
         if piece.shape[1] < start + n:
@@ -389,7 +445,9 @@
     row = lax.axis_index("row")
     both = len(pieces) > len(starts)
     for part in range(parts):
-        mine = pieces[len(starts) :] if both and part else pieces[: len(starts)]
+        mine = list(pieces[len(starts) :] if both and part else pieces[: len(starts)])
+        if len(mine) > len(starts):
+            mine[-2:] = [tuple(mine[-2:])]
         pl.when(row == part)(functools.partial(fill, out, list(zip(starts, mine)), part, tile, low_tile))
 
 
@@ -528,26 +586,29 @@
             xs = list(update(recv, ys, xs, gain, chunks, stage))
     mine, gain_now = (ys, gain) if rows == 2 else (xs, ())
     kept, own, got = [], [], []
+    halves = share if rows == 2 and all(s % tile in (0, share) for s in starts) else 0
     for c, start in enumerate(starts):
-        narrow = share if rows == 2 and start % tile >= share else 0
+        before = kept
         piece, kept = gram(
-            (first[0], first[1 + c]), (mine[0], mine[1 + c]), gain_now, kept, start, cols, tile, narrow, rows > 2
+            (first[0], first[1 + c]), (mine[0], mine[1 + c]), gain_now, kept, start, cols, tile, halves, rows > 2
         )
-        if rows == 2:
-            got.append(lax.ppermute(kept[0] if narrow else piece, "row", [(1, 0)]))
-            own.append(piece)
-        else:
+        if rows > 2:
             got.append(lax.psum(piece, "row"))
+            continue
+        got.append(lax.ppermute(piece, "row", [(1, 0)]))
+        own.append([piece])
+    if halves:
+        own[-1].append(widen(kept[0], before))
     shape = (count, share, cols)
     last = count - PAIR
 
     def pick(low, high):
-        return got[low:high] + own[low:high]
+        return got[low:high] + [x for pieces in own[low:high] for x in pieces]
 
     message = pair(pick(0, PAIR), starts[:PAIR], rows, tile, share, 0)
     from_far = lax.ppermute(message, "sub", far)
     kernel = functools.partial(middle_kernel, starts=starts[:-1], parts=rows, tile=tile)
-    arrays = [interface_block, from_far] + got[:-1] + own[:-1]
+    arrays = [interface_block, from_far] + pick(0, -1)
     (base,) = assemble(kernel, [ids], arrays, [shape], shape)
     message = pair(pick(last, None), starts[last:], rows, tile, share, last)
     from_near = lax.ppermute(message, "sub", near)

time: 69.2 us -> 70.3 us (1.016)
  waiting for transfers between devices: 26.6 us -> 28 us
    ppermute x5, waiting for transfers between devices: 6.79 us -> 8.21 us  [shards(): got.append(lax.ppermute(piece, 'row', [(1, 0)]))]
where the time goes in v6:
time: 70.3 us; the launch traced here: 69.9 us
  starting transfers between devices  28.9 us (41%)
  waiting for transfers between devices  28 us (40%)
  Pallas kernels  12.6 us (18%)
    ppermute x6, starting transfers between devices, shards(): recv.append(lax.ppermute(x, 'row', [(stage - 1, stage)]))  16.5 us
    ppermute x6, waiting for transfers between devices, shards(): recv.append(lax.ppermute(x, 'row', [(stage - 1, stage)]))  16.1 us
    ppermute x5, waiting for transfers between devices, shards(): got.append(lax.ppermute(piece, 'row', [(1, 0)]))  8.21 us
    ppermute x5, starting transfers between devices, shards(): got.append(lax.ppermute(piece, 'row', [(1, 0)]))  6.42 us
    pallas_call x1, Pallas kernels, solve(): pl.pallas_call(functools.partial(solve_kernel, chunks=chunks, tiles=tiles...  6.35 us
    ppermute x1, starting transfers between devices, shards(): from_far = lax.ppermute(message, 'sub', far)  5.85 us
    ppermute x1, waiting for transfers between devices, shards(): from_far = lax.ppermute(message, 'sub', far)  3.75 us
    pallas_call x3, Pallas kernels, assemble(): pl.pallas_call(kernel, in_specs=[smem] * len(ids) + [vmem] * len(arrays),...  2.91 us
  transfers between devices with their start and end apart: 13, of which 6 were waited for; matrix products, arithmetic and copies ran while one was open for 0% of the time, Pallas kernels for 14%

profile of v6, /device:TPU:9, one launch (start us, length us, event | category | flops | bytes accessed | tf_op | source)
XLA Modules:
  0.0 69.9 jit_solution(17824837492143345151)
XLA Ops:
  0.0 1.7 %early.1 = f32[512,256]{1,0:T(8,128)S(1)} custom-call(f32[1,4,256,256]{3,2,1,0:T(8,128)} %inv_hbm.5, f32[1,1024,512]{2,1,0:T(8,128)} %b_hbm.3), custom_call_target="tpu_custom_call" | custom-call | flops 201326592 | bytes 1048576 | tf_op jit(solution)/shard_map/early/pallas_call | solution.py:116
  1.7 1.5 %collective-permute-start = (f32[512,256]{1,0:T(8,128)S(1)}, f32[512,256]{1,0:T(8,128)S(1)}, u32[]{:S(2)}, u32[]{:S(2)}) collective-permute-start(f32[512,256]{1,0:T(8,128)S(1)} %early.1), channel_id=1, source_target_pairs={{0,1},{2,3},{4,5},{6,7},{8,9},{10,11},{12,13},{14,15},{16,17},{18,... | collective-permute-start | bytes 1572872 | tf_op jit(solution)/shard_map/ppermute | solution.py:581
  3.2 0.0 copy-start.1
  3.2 0.0 copy-start.4
  3.3 6.4 %others.1 = (f32[512,256]{1,0:T(8,128)}, f32[128,768]{1,0:T(8,128)S(1)}, f32[128,768]{1,0:T(8,128)S(1)}, f32[128,768]{1,0:T(8,128)S(1)}, f32[64,768]{1,0:T(8,128)S(1)}, /*index=5*/f32[64,768]{1,0:T(8,128)S(1)}) custom-call(s32[3,1,4]{2,1,0:T(1,128)S(1)} %bitcast.7, s32[4,16]{1,0:T(4,128)S(1)} %bitcast.3, f32[1,4,3,256,256]{4,3,2,1,0:T(8,128)} %f_hbm.3, ...), custom_call_target="tpu_custom_call" | custom-call | flops 2013265920 | bytes 8388608 | tf_op jit(solution)/shard_map/others/pallas_call | solution.py:196
  9.6 1.3 %collective-permute-start.1 = (f32[128,768]{1,0:T(8,128)S(1)}, f32[128,768]{1,0:T(8,128)S(1)}, u32[]{:S(2)}, u32[]{:S(2)}) collective-permute-start(f32[128,768]{1,0:T(8,128)S(1)} %get-tuple-element.29.refs_3_), channel_id=1, source_target_pairs={{0,1},{2,3},{4,5},{6,7},{8,9},{10,11},{12,13},{14,15},{16,17},{18,... | collective-permute-start | bytes 1179656 | tf_op jit(solution)/shard_map/ppermute | solution.py:581
  10.9 1.3 %collective-permute-start.3 = (f32[128,768]{1,0:T(8,128)S(1)}, f32[128,768]{1,0:T(8,128)S(1)}, u32[]{:S(2)}, u32[]{:S(2)}) collective-permute-start(f32[128,768]{1,0:T(8,128)S(1)} %get-tuple-element.34.refs_3_), channel_id=1, source_target_pairs={{0,1},{2,3},{4,5},{6,7},{8,9},{10,11},{12,13},{14,15},{16,17},{18,... | collective-permute-start | bytes 1179656 | tf_op jit(solution)/shard_map/ppermute | solution.py:581
  12.3 1.3 %collective-permute-start.6 = (f32[128,768]{1,0:T(8,128)S(1)}, f32[128,768]{1,0:T(8,128)S(1)}, u32[]{:S(2)}, u32[]{:S(2)}) collective-permute-start(f32[128,768]{1,0:T(8,128)S(1)} %get-tuple-element.38.refs_3_), channel_id=1, source_target_pairs={{0,1},{2,3},{4,5},{6,7},{8,9},{10,11},{12,13},{14,15},{16,17},{18,... | collective-permute-start | bytes 1179656 | tf_op jit(solution)/shard_map/ppermute | solution.py:581
  13.6 0.0 copy-start
  13.6 1.4 %collective-permute-start.8 = (f32[64,768]{1,0:T(8,128)S(1)}, f32[64,768]{1,0:T(8,128)S(1)}, u32[]{:S(2)}, u32[]{:S(2)}) collective-permute-start(f32[64,768]{1,0:T(8,128)S(1)} %get-tuple-element.42.refs_3_), channel_id=1, source_target_pairs={{0,1},{2,3},{4,5},{6,7},{8,9},{10,11},{12,13},{14,15},{16,17},{18,... | collective-permute-start | bytes 589832 | tf_op jit(solution)/shard_map/ppermute | solution.py:581
  15.1 0.6 response.1
  15.7 9.7 %collective-permute-start.10 = (f32[64,768]{1,0:T(8,128)S(1)}, f32[64,768]{1,0:T(8,128)S(1)}, u32[]{:S(2)}, u32[]{:S(2)}) collective-permute-start(f32[64,768]{1,0:T(8,128)S(1)} %get-tuple-element.46.refs_3_), channel_id=1, source_target_pairs={{0,1},{2,3},{4,5},{6,7},{8,9},{10,11},{12,13},{14,15},{16,17},{18,... | collective-permute-start | bytes 589832 | tf_op jit(solution)/shard_map/ppermute | solution.py:581
  25.4 0.6 arrange.1.refs_0_
  26.0 0.2 shard_map.64
  26.2 4.4 %collective-permute-done.3.refs_1_ = f32[128,768]{1,0:T(8,128)S(1)} collective-permute-done((f32[128,768]{1,0:T(8,128)S(1)}, f32[128,768]{1,0:T(8,128)S(1)}, u32[]{:S(2)}, u32[]{:S(2)}) %collective-permute-start.3) | collective-permute-done | bytes 393248 | tf_op jit(solution)/shard_map/ppermute | solution.py:581
  30.6 8.4 %collective-permute-done.6.refs_1_ = f32[128,768]{1,0:T(8,128)S(1)} collective-permute-done((f32[128,768]{1,0:T(8,128)S(1)}, f32[128,768]{1,0:T(8,128)S(1)}, u32[]{:S(2)}, u32[]{:S(2)}) %collective-permute-start.6) | collective-permute-done | bytes 393248 | tf_op jit(solution)/shard_map/ppermute | solution.py:581
  39.1 1.3 %collective-permute-start.7 = (f32[128,384]{1,0:T(8,128)S(1)}, f32[128,384]{1,0:T(8,128)S(1)}, u32[]{:S(2)}, u32[]{:S(2)}) collective-permute-start(f32[128,384]{1,0:T(8,128)S(1)} %get-tuple-element.41.refs_6_.refs_3_), channel_id=1, source_target_pairs={{1,0},{3,2},{5,4},{7,6},{9,8},{11,10},{13,12},{15,14},{17,16},{19,... | collective-permute-start | bytes 589832 | tf_op jit(solution)/shard_map/ppermute | solution.py:598
  40.3 2.9 %collective-permute-done.8.refs_1_ = f32[64,768]{1,0:T(8,128)S(1)} collective-permute-done((f32[64,768]{1,0:T(8,128)S(1)}, f32[64,768]{1,0:T(8,128)S(1)}, u32[]{:S(2)}, u32[]{:S(2)}) %collective-permute-start.8) | collective-permute-done | bytes 196640 | tf_op jit(solution)/shard_map/ppermute | solution.py:581
  43.3 1.3 %collective-permute-start.9 = (f32[64,448]{1,0:T(8,128)S(1)}, f32[64,448]{1,0:T(8,128)S(1)}, u32[]{:S(2)}, u32[]{:S(2)}) collective-permute-start(f32[64,448]{1,0:T(8,128)S(1)} %get-tuple-element.45.refs_7_.refs_4_), channel_id=1, source_target_pairs={{1,0},{3,2},{5,4},{7,6},{9,8},{11,10},{13,12},{15,14},{17,16},{19,... | collective-permute-start | bytes 344072 | tf_op jit(solution)/shard_map/ppermute | solution.py:598
  44.6 1.3 %collective-permute-start.4 = (f32[128,256]{1,0:T(8,128)S(1)}, f32[128,256]{1,0:T(8,128)S(1)}, u32[]{:S(2)}, u32[]{:S(2)}) collective-permute-start(f32[128,256]{1,0:T(8,128)S(1)} %get-tuple-element.37.refs_3_.refs_5_), channel_id=1, source_target_pairs={{1,0},{3,2},{5,4},{7,6},{9,8},{11,10},{13,12},{15,14},{17,16},{19,... | collective-permute-start | bytes 393224 | tf_op jit(solution)/shard_map/ppermute | solution.py:598
  45.9 1.3 %collective-permute-start.2 = (f32[128,128]{1,0:T(8,128)S(1)}, f32[128,128]{1,0:T(8,128)S(1)}, u32[]{:S(2)}, u32[]{:S(2)}) collective-permute-start(f32[128,128]{1,0:T(8,128)S(1)} %get-tuple-element.33.refs_2_.refs_4_), channel_id=1, source_target_pairs={{1,0},{3,2},{5,4},{7,6},{9,8},{11,10},{13,12},{15,14},{17,16},{19,... | collective-permute-start | bytes 196616 | tf_op jit(solution)/shard_map/ppermute | solution.py:598
  47.2 0.3 collective-permute-done.10.refs_1_
  47.5 1.3 %collective-permute-start.11 = (f32[64,256]{1,0:T(8,128)S(1)}, f32[64,256]{1,0:T(8,128)S(1)}, u32[]{:S(2)}, u32[]{:S(2)}) collective-permute-start(f32[64,256]{1,0:T(8,128)S(1)} %get-tuple-element.49.refs_1_.refs_5_), channel_id=1, source_target_pairs={{1,0},{3,2},{5,4},{7,6},{9,8},{11,10},{13,12},{15,14},{17,16},{19,... | collective-permute-start | bytes 196616 | tf_op jit(solution)/shard_map/ppermute | solution.py:598
  48.8 8.2 %collective-permute-done.2.refs_0_ = f32[128,128]{1,0:T(8,128)S(1)} collective-permute-done((f32[128,128]{1,0:T(8,128)S(1)}, f32[128,128]{1,0:T(8,128)S(1)}, u32[]{:S(2)}, u32[]{:S(2)}) %collective-permute-start.2) | collective-permute-done | bytes 65568 | tf_op jit(solution)/shard_map/ppermute | solution.py:598
  57.0 0.1 shard_map.66
  57.1 5.8 %collective-permute-start.5 = (f32[2,64,256]{2,1,0:T(8,128)S(1)}, f32[2,64,256]{2,1,0:T(8,128)S(1)}, u32[]{:S(2)}, u32[]{:S(2)}) collective-permute-start(f32[2,64,256]{2,1,0:T(8,128)S(1)} %shard_map.66), channel_id=1, source_target_pairs={{2,4},{4,2},{6,8},{8,6},{10,12},{12,10},{14,16},{16,14},{18,20},{2... | collective-permute-start | bytes 393224 | tf_op jit(solution)/shard_map/ppermute | solution.py:609
  63.0 0.2 shard_map.72
  63.1 0.1 collective-permute-start.12
  63.2 3.8 %collective-permute-done.5.halo_ref = f32[2,64,256]{2,1,0:T(8,128)S(1)} collective-permute-done((f32[2,64,256]{2,1,0:T(8,128)S(1)}, f32[2,64,256]{2,1,0:T(8,128)S(1)}, u32[]{:S(2)}, u32[]{:S(2)}) %collective-permute-start.5) | collective-permute-done | bytes 131104 | tf_op jit(solution)/shard_map/ppermute | solution.py:609
  67.0 1.0 %shard_map.69.base_ref = f32[4,64,512]{2,1,0:T(8,128)S(1)} custom-call(s32[4,16]{1,0:T(4,128)S(1)} %bitcast.5, f32[1,4,64,512]{3,2,1,0:T(8,128)S(1)} %copy-done.2, f32[2,64,256]{2,1,0:T(8,128)S(1)} %collective-permute-done.5.halo_ref, f32[128,128]{1,0:T(8,128)S(1)} %collective-permute-done.2.refs_0_, f32[128,256]{1,0:T(8,128)S(1)} %collective-permute-done.4.refs_1_, ...), custom_call_target="tpu_custom_call" | custom-call | tf_op jit(solution)/shard_map/pallas_call | solution.py:547
  68.0 0.9 %shard_map.71 = (f32[4,64,512]{2,1,0:T(8,128)S(1)}, f32[2,4,8,128]{3,2,1,0:T(8,128)S(1)}) custom-call(s32[4,16]{1,0:T(4,128)S(1)} %bitcast.6, f32[4,64,512]{2,1,0:T(8,128)S(1)} %shard_map.69.base_ref, f32[64,256]{1,0:T(8,128)S(1)} %collective-permute-done.11.refs_0_.refs_2_, f32[64,256]{1,0:T(8,128)S(1)} %get-tuple-element.49.refs_1_.refs_5_, ...), custom_call_target="tpu_custom_call" | custom-call | tf_op jit(solution)/shard_map/pallas_call | solution.py:547
  69.0 1.0 %shard_map.73 = f32[4,64,512]{2,1,0:T(8,128)} custom-call(f32[4,64,512]{2,1,0:T(8,128)S(1)} %get-tuple-element.51.base_ref, f32[2,64,256]{2,1,0:T(8,128)S(1)} %collective-permute-done.12.halo_ref, f32[2,4,8,128]{3,2,1,0:T(8,128)S(1)} %get-tuple-element.52.weight_ref), custom_call_target="tpu_custom_call" | custom-call | tf_op jit(solution)/shard_map/pallas_call | solution.py:547
  (21 shorter events, 0.1 us)
Async XLA Ops:
  0.0 3.2 %copy-start.3 = (s32[16,4]{0,1:T(4,128)S(1)}, s32[16,4]{0,1:T(4,128)}, u32[]{:S(2)}) copy-start(s32[16,4]{0,1:T(4,128)} %param.11) | copy-start | bytes 772
  0.0 3.2 %copy-start.5 = (s32[1,4,3]{1,0,2:T(1,128)S(1)}, s32[1,4,3]{1,0,2:T(1,128)}, u32[]{:S(2)}) copy-start(s32[1,4,3]{1,0,2:T(1,128)} %param.8) | copy-start | bytes 148
  1.7 14.0 %collective-permute-start = (f32[512,256]{1,0:T(8,128)S(1)}, f32[512,256]{1,0:T(8,128)S(1)}, u32[]{:S(2)}, u32[]{:S(2)}) collective-permute-start(f32[512,256]{1,0:T(8,128)S(1)} %early.1), channel_id=1, source_target_pairs={{0,1},{2,3},{4,5},{6,7},{8,9},{10,11},{12,13},{14,15},{16,17},{18,... | collective-permute-start | bytes 1572872 | tf_op jit(solution)/shard_map/ppermute | solution.py:581
  3.2 11.8 %copy-start.1 = (f32[1,4,256,256]{3,2,1,0:T(8,128)S(1)}, f32[1,4,256,256]{3,2,1,0:T(8,128)}, u32[]{:S(2)}) copy-start(f32[1,4,256,256]{3,2,1,0:T(8,128)} %inv_hbm.5) | copy-start | bytes 3145732
  3.2 11.8 %copy-start.4 = (f32[1,4,3,256,256]{4,3,2,1,0:T(8,128)S(1)}, f32[1,4,3,256,256]{4,3,2,1,0:T(8,128)}, u32[]{:S(2)}) copy-start(f32[1,4,3,256,256]{4,3,2,1,0:T(8,128)} %f_hbm.3) | copy-start | bytes 9437188
  9.6 16.4 %collective-permute-start.1 = (f32[128,768]{1,0:T(8,128)S(1)}, f32[128,768]{1,0:T(8,128)S(1)}, u32[]{:S(2)}, u32[]{:S(2)}) collective-permute-start(f32[128,768]{1,0:T(8,128)S(1)} %get-tuple-element.29.refs_3_), channel_id=1, source_target_pairs={{0,1},{2,3},{4,5},{6,7},{8,9},{10,11},{12,13},{14,15},{16,17},{18,... | collective-permute-start | bytes 1179656 | tf_op jit(solution)/shard_map/ppermute | solution.py:581
  10.9 19.7 %collective-permute-start.3 = (f32[128,768]{1,0:T(8,128)S(1)}, f32[128,768]{1,0:T(8,128)S(1)}, u32[]{:S(2)}, u32[]{:S(2)}) collective-permute-start(f32[128,768]{1,0:T(8,128)S(1)} %get-tuple-element.34.refs_3_), channel_id=1, source_target_pairs={{0,1},{2,3},{4,5},{6,7},{8,9},{10,11},{12,13},{14,15},{16,17},{18,... | collective-permute-start | bytes 1179656 | tf_op jit(solution)/shard_map/ppermute | solution.py:581
  12.3 26.8 %collective-permute-start.6 = (f32[128,768]{1,0:T(8,128)S(1)}, f32[128,768]{1,0:T(8,128)S(1)}, u32[]{:S(2)}, u32[]{:S(2)}) collective-permute-start(f32[128,768]{1,0:T(8,128)S(1)} %get-tuple-element.38.refs_3_), channel_id=1, source_target_pairs={{0,1},{2,3},{4,5},{6,7},{8,9},{10,11},{12,13},{14,15},{16,17},{18,... | collective-permute-start | bytes 1179656 | tf_op jit(solution)/shard_map/ppermute | solution.py:581
  13.6 12.4 %copy-start = (f32[512,256]{1,0:T(8,128)S(1)}, f32[512,256]{1,0:T(8,128)}, u32[]{:S(2)}) copy-start(f32[512,256]{1,0:T(8,128)} %get-tuple-element.30.refs_2_) | copy-start | bytes 1572868
  13.6 29.7 %collective-permute-start.8 = (f32[64,768]{1,0:T(8,128)S(1)}, f32[64,768]{1,0:T(8,128)S(1)}, u32[]{:S(2)}, u32[]{:S(2)}) collective-permute-start(f32[64,768]{1,0:T(8,128)S(1)} %get-tuple-element.42.refs_3_), channel_id=1, source_target_pairs={{0,1},{2,3},{4,5},{6,7},{8,9},{10,11},{12,13},{14,15},{16,17},{18,... | collective-permute-start | bytes 589832 | tf_op jit(solution)/shard_map/ppermute | solution.py:581
  15.7 31.8 %collective-permute-start.10 = (f32[64,768]{1,0:T(8,128)S(1)}, f32[64,768]{1,0:T(8,128)S(1)}, u32[]{:S(2)}, u32[]{:S(2)}) collective-permute-start(f32[64,768]{1,0:T(8,128)S(1)} %get-tuple-element.46.refs_3_), channel_id=1, source_target_pairs={{0,1},{2,3},{4,5},{6,7},{8,9},{10,11},{12,13},{14,15},{16,17},{18,... | collective-permute-start | bytes 589832 | tf_op jit(solution)/shard_map/ppermute | solution.py:581
  39.1 23.9 %collective-permute-start.7 = (f32[128,384]{1,0:T(8,128)S(1)}, f32[128,384]{1,0:T(8,128)S(1)}, u32[]{:S(2)}, u32[]{:S(2)}) collective-permute-start(f32[128,384]{1,0:T(8,128)S(1)} %get-tuple-element.41.refs_6_.refs_3_), channel_id=1, source_target_pairs={{1,0},{3,2},{5,4},{7,6},{9,8},{11,10},{13,12},{15,14},{17,16},{19,... | collective-permute-start | bytes 589832 | tf_op jit(solution)/shard_map/ppermute | solution.py:598
  43.3 19.7 %collective-permute-start.9 = (f32[64,448]{1,0:T(8,128)S(1)}, f32[64,448]{1,0:T(8,128)S(1)}, u32[]{:S(2)}, u32[]{:S(2)}) collective-permute-start(f32[64,448]{1,0:T(8,128)S(1)} %get-tuple-element.45.refs_7_.refs_4_), channel_id=1, source_target_pairs={{1,0},{3,2},{5,4},{7,6},{9,8},{11,10},{13,12},{15,14},{17,16},{19,... | collective-permute-start | bytes 344072 | tf_op jit(solution)/shard_map/ppermute | solution.py:598
  44.6 12.4 %collective-permute-start.4 = (f32[128,256]{1,0:T(8,128)S(1)}, f32[128,256]{1,0:T(8,128)S(1)}, u32[]{:S(2)}, u32[]{:S(2)}) collective-permute-start(f32[128,256]{1,0:T(8,128)S(1)} %get-tuple-element.37.refs_3_.refs_5_), channel_id=1, source_target_pairs={{1,0},{3,2},{5,4},{7,6},{9,8},{11,10},{13,12},{15,14},{17,16},{19,... | collective-permute-start | bytes 393224 | tf_op jit(solution)/shard_map/ppermute | solution.py:598
  45.9 11.1 %collective-permute-start.2 = (f32[128,128]{1,0:T(8,128)S(1)}, f32[128,128]{1,0:T(8,128)S(1)}, u32[]{:S(2)}, u32[]{:S(2)}) collective-permute-start(f32[128,128]{1,0:T(8,128)S(1)} %get-tuple-element.33.refs_2_.refs_4_), channel_id=1, source_target_pairs={{1,0},{3,2},{5,4},{7,6},{9,8},{11,10},{13,12},{15,14},{17,16},{19,... | collective-permute-start | bytes 196616 | tf_op jit(solution)/shard_map/ppermute | solution.py:598
  47.5 15.5 %collective-permute-start.11 = (f32[64,256]{1,0:T(8,128)S(1)}, f32[64,256]{1,0:T(8,128)S(1)}, u32[]{:S(2)}, u32[]{:S(2)}) collective-permute-start(f32[64,256]{1,0:T(8,128)S(1)} %get-tuple-element.49.refs_1_.refs_5_), channel_id=1, source_target_pairs={{1,0},{3,2},{5,4},{7,6},{9,8},{11,10},{13,12},{15,14},{17,16},{19,... | collective-permute-start | bytes 196616 | tf_op jit(solution)/shard_map/ppermute | solution.py:598
  48.8 18.2 %copy-start.2 = (f32[1,4,64,512]{3,2,1,0:T(8,128)S(1)}, f32[1,4,64,512]{3,2,1,0:T(8,128)}, u32[]{:S(2)}) copy-start(f32[1,4,64,512]{3,2,1,0:T(8,128)} %face_ref.1) | copy-start | bytes 1572868
  57.1 9.9 %collective-permute-start.5 = (f32[2,64,256]{2,1,0:T(8,128)S(1)}, f32[2,64,256]{2,1,0:T(8,128)S(1)}, u32[]{:S(2)}, u32[]{:S(2)}) collective-permute-start(f32[2,64,256]{2,1,0:T(8,128)S(1)} %shard_map.66), channel_id=1, source_target_pairs={{2,4},{4,2},{6,8},{8,6},{10,12},{12,10},{14,16},{16,14},{18,20},{2... | collective-permute-start | bytes 393224 | tf_op jit(solution)/shard_map/ppermute | solution.py:609
  63.1 5.8 %collective-permute-start.12 = (f32[2,64,256]{2,1,0:T(8,128)S(1)}, f32[2,64,256]{2,1,0:T(8,128)S(1)}, u32[]{:S(2)}, u32[]{:S(2)}) collective-permute-start(f32[2,64,256]{2,1,0:T(8,128)S(1)} %shard_map.72), channel_id=1, source_target_pairs={{0,2},{2,0},{4,6},{6,4},{8,10},{10,8},{12,14},{14,12},{16,18},{18,... | collective-permute-start | bytes 393224 | tf_op jit(solution)/shard_map/ppermute | solution.py:614

commit v7 on v5

--- a/solution.py
+++ b/solution.py
@@ -294,6 +294,11 @@
     )(*gain, *recv, *y, *cur)
 
 
+def slot_of(tile, count):
+    swapped = {count - 2: count - 1, count - 1: count - 2} if count % 2 == 0 else {}
+    return swapped.get(tile, tile)
+
+
 def gram_kernel(*refs, start, fused, clear, last, share, tile):
     recv0_ref, recv_ref, y0_ref, y_ref = refs[:4]
     refs = refs[4:]
@@ -302,7 +307,7 @@
         refs = refs[2:]
     if start:
         oldh_ref, oldl_ref = refs[:2]
-        refs = refs[2:]
+        refs = refs[2 if last or not share else 4 :]
     piece, rest = refs[0], refs[1:]
     n = recv_ref.shape[0]
     here = slice(start, start + n)
@@ -317,16 +322,21 @@
         high = jnp.concatenate([recv[:n], x[:n]], axis=1)
         low = jnp.concatenate([recv[n:], x[n:]], axis=1)
         both = jnp.concatenate([high, low], axis=0)
+        if share and last:
+            piece[...] = three(nn, both, oldh_ref[...], oldl_ref[...])
+            rest[0][...] = both
+            return
         if start:
             piece[:, :start] = three(nn, both, oldh_ref[:, :start], oldl_ref[:, :start])
         piece[:, here] = three(nt, both, high, low)
-        if not last:
-            rest[0][:, here] = high.T
-            rest[1][:, here] = low.T
-        elif share:
-            rest[0][...] = jnp.concatenate(
-                [piece[:, t * tile : t * tile + share] for t in range((start + n) // tile)], axis=1
-            )
+        if last:
+            return
+        turned = high.T, low.T
+        rest[0][:, here], rest[1][:, here] = turned
+        if share:
+            left = slot_of(start // tile, rest[0].shape[1] // tile) * share
+            columns = slice(left, left + share)
+            rest[2][:, columns], rest[3][:, columns] = turned[0][:, :share], turned[1][:, :share]
 
     if clear:
 
@@ -339,24 +349,52 @@
     n = recv[1].shape[0]
     half = recv[0].shape[1] + recv[1].shape[1]
     last = start + n == total
+    slim = total // tile * share
+    if last and share:
+        kept = kept[2:]
+        shapes = [jax.ShapeDtypeStruct((n, slim), F32), jax.ShapeDtypeStruct((2 * n, 2 * half), BF16)]
+    else:
+        shapes = [jax.ShapeDtypeStruct((n, start + n), F32)]
+    if not last:
+        shapes += [jax.ShapeDtypeStruct((2 * half, total), BF16)] * 2
+        shapes += [jax.ShapeDtypeStruct((2 * half, slim), BF16)] * 2 if share else []
     inputs = [*recv, *y, *gain, *kept]
-    if not last:
-        more = [jax.ShapeDtypeStruct((2 * half, total), BF16)] * 2
-    else:
-        more = [jax.ShapeDtypeStruct((n, total // tile * share), F32)] if share else []
+    first = len(inputs) - len(kept)
     results = pl.pallas_call(
         functools.partial(
             gram_kernel, start=start, fused=bool(gain), clear=clear, last=last, share=share, tile=tile
         ),
         in_specs=[pl.BlockSpec(memory_space=pltpu.VMEM)] * len(inputs),
-        out_shape=[jax.ShapeDtypeStruct((n, start + n), F32)] + more,
-        input_output_aliases={len(inputs) - 2 + i: 1 + i for i in range(2)} if start and not last else {},
+        out_shape=shapes,
+        input_output_aliases={} if last else {first + i: 1 + i for i in range(len(kept))},
         compiler_params=pltpu.CompilerParams(vmem_limit_bytes=VMEM_LIMIT),
         cost_estimate=pl.CostEstimate(
             flops=6 * n * half * (half + 2 * (start + n)), bytes_accessed=4 << 20, transcendentals=0
         ),
     )(*inputs)
     return results[0], list(results[1:])
+
+
+def widen_kernel(both_ref, oldh_ref, oldl_ref, out):
+    n, total = out.shape
+    start = total - n
+
+    @pl.when(lax.axis_index("row") > 0)
+    def _():
+        both = both_ref[...]
+        out[:, :start] = three(nn, both, oldh_ref[:, :start], oldl_ref[:, :start])
+        out[:, start:] = three(nt, both, both[:n], both[n:])
+
+
+def widen(both, kept):
+    n, total = both.shape[0] // 2, kept[0].shape[1]
+    return pl.pallas_call(
+        widen_kernel,
+        out_shape=jax.ShapeDtypeStruct((n, total), F32),
+        compiler_params=pltpu.CompilerParams(vmem_limit_bytes=VMEM_LIMIT),
+        cost_estimate=pl.CostEstimate(flops=6 * n * both.shape[1] * total, bytes_accessed=4 << 20, transcendentals=0),
+        name="widen",
+    )(both, *kept)
 
 
 def fill(out, chunks, part, tile, low_tile):
@@ -367,9 +405,9 @@
         n = piece.shape[0]
         at, inner = start // tile, start % tile
         if piece.shape[1] < start + n:
-            turned = piece[:, low_tile * share :].T
+            turned = piece[...].T
             for t in range(low_tile, at + 1):
-                first = (t - low_tile) * share
+                first = slot_of(t, at + 1) * share
                 out[t - low_tile, :, start - base : start - base + n] = turned[first : first + share]
             continue
         first, stop = max(inner, low), min(inner + n, high)
@@ -528,16 +566,19 @@
             xs = list(update(recv, ys, xs, gain, chunks, stage))
     mine, gain_now = (ys, gain) if rows == 2 else (xs, ())
     kept, own, got = [], [], []
+    slim = share if rows == 2 and all(s % tile in (0, share) for s in starts) else 0
     for c, start in enumerate(starts):
-        narrow = share if rows == 2 and start % tile >= share else 0
+        before = kept
         piece, kept = gram(
-            (first[0], first[1 + c]), (mine[0], mine[1 + c]), gain_now, kept, start, cols, tile, narrow, rows > 2
+            (first[0], first[1 + c]), (mine[0], mine[1 + c]), gain_now, kept, start, cols, tile, slim, rows > 2
         )
-        if rows == 2:
-            got.append(lax.ppermute(kept[0] if narrow else piece, "row", [(1, 0)]))
-            own.append(piece)
-        else:
+        if rows > 2:
             got.append(lax.psum(piece, "row"))
+            continue
+        got.append(lax.ppermute(piece, "row", [(1, 0)]))
+        own.append(piece)
+    if slim:
+        own[-1] = widen(kept[0], before[:2])
     shape = (count, share, cols)
     last = count - PAIR
 

time: 69.2 us -> 69.2 us (level)
  transfers between devices with their start and end apart: 13 -> 13, of which waited for: 6 -> 6; matrix products, arithmetic and copies ran while one was open for 0% -> 0% of each run, Pallas kernels for 14% -> 15%
where the time goes in v7:
time: 69.2 us; the launch traced here: 68.8 us
  starting transfers between devices  29.1 us (42%)
  waiting for transfers between devices  26.7 us (39%)
  Pallas kernels  12.6 us (18%)
    ppermute x6, starting transfers between devices, shards(): recv.append(lax.ppermute(x, 'row', [(stage - 1, stage)]))  16.5 us
    ppermute x6, waiting for transfers between devices, shards(): recv.append(lax.ppermute(x, 'row', [(stage - 1, stage)]))  16.1 us
    ppermute x5, waiting for transfers between devices, shards(): got.append(lax.ppermute(piece, 'row', [(1, 0)]))  6.89 us
    ppermute x5, starting transfers between devices, shards(): got.append(lax.ppermute(piece, 'row', [(1, 0)]))  6.42 us
    pallas_call x1, Pallas kernels, solve(): pl.pallas_call(functools.partial(solve_kernel, chunks=chunks, tiles=tiles...  6.35 us
    ppermute x1, starting transfers between devices, shards(): from_far = lax.ppermute(message, 'sub', far)  6.04 us
    ppermute x1, waiting for transfers between devices, shards(): from_far = lax.ppermute(message, 'sub', far)  3.75 us
    pallas_call x3, Pallas kernels, assemble(): pl.pallas_call(kernel, in_specs=[smem] * len(ids) + [vmem] * len(arrays),...  2.91 us
  transfers between devices with their start and end apart: 13, of which 6 were waited for; matrix products, arithmetic and copies ran while one was open for 0% of the time, Pallas kernels for 15%

profile of v7, /device:TPU:9, one launch (start us, length us, event | category | flops | bytes accessed | tf_op | source)
XLA Modules:
  0.0 68.8 jit_solution(6389344328959119586)
XLA Ops:
  0.0 1.7 %early.1 = f32[512,256]{1,0:T(8,128)S(1)} custom-call(f32[1,4,256,256]{3,2,1,0:T(8,128)} %inv_hbm.5, f32[1,1024,512]{2,1,0:T(8,128)} %b_hbm.3), custom_call_target="tpu_custom_call" | custom-call | flops 201326592 | bytes 1048576 | tf_op jit(solution)/shard_map/early/pallas_call | solution.py:116
  1.7 1.5 %collective-permute-start = (f32[512,256]{1,0:T(8,128)S(1)}, f32[512,256]{1,0:T(8,128)S(1)}, u32[]{:S(2)}, u32[]{:S(2)}) collective-permute-start(f32[512,256]{1,0:T(8,128)S(1)} %early.1), channel_id=1, source_target_pairs={{0,1},{2,3},{4,5},{6,7},{8,9},{10,11},{12,13},{14,15},{16,17},{18,... | collective-permute-start | bytes 1572872 | tf_op jit(solution)/shard_map/ppermute | solution.py:561
  3.2 0.0 copy-start.1
  3.2 0.0 copy-start.4
  3.3 6.4 %others.1 = (f32[512,256]{1,0:T(8,128)}, f32[128,768]{1,0:T(8,128)S(1)}, f32[128,768]{1,0:T(8,128)S(1)}, f32[128,768]{1,0:T(8,128)S(1)}, f32[64,768]{1,0:T(8,128)S(1)}, /*index=5*/f32[64,768]{1,0:T(8,128)S(1)}) custom-call(s32[3,1,4]{2,1,0:T(1,128)S(1)} %bitcast.7, s32[4,16]{1,0:T(4,128)S(1)} %bitcast.3, f32[1,4,3,256,256]{4,3,2,1,0:T(8,128)} %f_hbm.3, ...), custom_call_target="tpu_custom_call" | custom-call | flops 2013265920 | bytes 8388608 | tf_op jit(solution)/shard_map/others/pallas_call | solution.py:196
  9.6 1.3 %collective-permute-start.1 = (f32[128,768]{1,0:T(8,128)S(1)}, f32[128,768]{1,0:T(8,128)S(1)}, u32[]{:S(2)}, u32[]{:S(2)}) collective-permute-start(f32[128,768]{1,0:T(8,128)S(1)} %get-tuple-element.37.refs_3_), channel_id=1, source_target_pairs={{0,1},{2,3},{4,5},{6,7},{8,9},{10,11},{12,13},{14,15},{16,17},{18,... | collective-permute-start | bytes 1179656 | tf_op jit(solution)/shard_map/ppermute | solution.py:561
  10.9 1.3 %collective-permute-start.3 = (f32[128,768]{1,0:T(8,128)S(1)}, f32[128,768]{1,0:T(8,128)S(1)}, u32[]{:S(2)}, u32[]{:S(2)}) collective-permute-start(f32[128,768]{1,0:T(8,128)S(1)} %get-tuple-element.42.refs_3_), channel_id=1, source_target_pairs={{0,1},{2,3},{4,5},{6,7},{8,9},{10,11},{12,13},{14,15},{16,17},{18,... | collective-permute-start | bytes 1179656 | tf_op jit(solution)/shard_map/ppermute | solution.py:561
  12.3 1.3 %collective-permute-start.6 = (f32[128,768]{1,0:T(8,128)S(1)}, f32[128,768]{1,0:T(8,128)S(1)}, u32[]{:S(2)}, u32[]{:S(2)}) collective-permute-start(f32[128,768]{1,0:T(8,128)S(1)} %get-tuple-element.48.refs_3_), channel_id=1, source_target_pairs={{0,1},{2,3},{4,5},{6,7},{8,9},{10,11},{12,13},{14,15},{16,17},{18,... | collective-permute-start | bytes 1179656 | tf_op jit(solution)/shard_map/ppermute | solution.py:561
  13.6 0.0 copy-start
  13.6 1.4 %collective-permute-start.8 = (f32[64,768]{1,0:T(8,128)S(1)}, f32[64,768]{1,0:T(8,128)S(1)}, u32[]{:S(2)}, u32[]{:S(2)}) collective-permute-start(f32[64,768]{1,0:T(8,128)S(1)} %get-tuple-element.54.refs_3_), channel_id=1, source_target_pairs={{0,1},{2,3},{4,5},{6,7},{8,9},{10,11},{12,13},{14,15},{16,17},{18,... | collective-permute-start | bytes 589832 | tf_op jit(solution)/shard_map/ppermute | solution.py:561
  15.1 0.6 response.1
  15.7 9.7 %collective-permute-start.10 = (f32[64,768]{1,0:T(8,128)S(1)}, f32[64,768]{1,0:T(8,128)S(1)}, u32[]{:S(2)}, u32[]{:S(2)}) collective-permute-start(f32[64,768]{1,0:T(8,128)S(1)} %get-tuple-element.60.refs_3_), channel_id=1, source_target_pairs={{0,1},{2,3},{4,5},{6,7},{8,9},{10,11},{12,13},{14,15},{16,17},{18,... | collective-permute-start | bytes 589832 | tf_op jit(solution)/shard_map/ppermute | solution.py:561
  25.4 0.6 arrange.1.refs_0_
  26.0 0.2 shard_map.64
  26.2 4.4 %collective-permute-done.3.refs_1_ = f32[128,768]{1,0:T(8,128)S(1)} collective-permute-done((f32[128,768]{1,0:T(8,128)S(1)}, f32[128,768]{1,0:T(8,128)S(1)}, u32[]{:S(2)}, u32[]{:S(2)}) %collective-permute-start.3) | collective-permute-done | bytes 393248 | tf_op jit(solution)/shard_map/ppermute | solution.py:561
  30.6 8.4 %collective-permute-done.6.refs_1_ = f32[128,768]{1,0:T(8,128)S(1)} collective-permute-done((f32[128,768]{1,0:T(8,128)S(1)}, f32[128,768]{1,0:T(8,128)S(1)}, u32[]{:S(2)}, u32[]{:S(2)}) %collective-permute-start.6) | collective-permute-done | bytes 393248 | tf_op jit(solution)/shard_map/ppermute | solution.py:561
  39.1 1.3 %collective-permute-start.7 = (f32[128,384]{1,0:T(8,128)S(1)}, f32[128,384]{1,0:T(8,128)S(1)}, u32[]{:S(2)}, u32[]{:S(2)}) collective-permute-start(f32[128,384]{1,0:T(8,128)S(1)} %get-tuple-element.53.refs_6_.refs_3_), channel_id=1, source_target_pairs={{1,0},{3,2},{5,4},{7,6},{9,8},{11,10},{13,12},{15,14},{17,16},{19,... | collective-permute-start | bytes 589832 | tf_op jit(solution)/shard_map/ppermute | solution.py:578
  40.3 2.9 %collective-permute-done.8.refs_1_ = f32[64,768]{1,0:T(8,128)S(1)} collective-permute-done((f32[64,768]{1,0:T(8,128)S(1)}, f32[64,768]{1,0:T(8,128)S(1)}, u32[]{:S(2)}, u32[]{:S(2)}) %collective-permute-start.8) | collective-permute-done | bytes 196640 | tf_op jit(solution)/shard_map/ppermute | solution.py:561
  43.3 1.3 %collective-permute-start.9 = (f32[64,448]{1,0:T(8,128)S(1)}, f32[64,448]{1,0:T(8,128)S(1)}, u32[]{:S(2)}, u32[]{:S(2)}) collective-permute-start(f32[64,448]{1,0:T(8,128)S(1)} %get-tuple-element.59.refs_7_.refs_4_), channel_id=1, source_target_pairs={{1,0},{3,2},{5,4},{7,6},{9,8},{11,10},{13,12},{15,14},{17,16},{19,... | collective-permute-start | bytes 344072 | tf_op jit(solution)/shard_map/ppermute | solution.py:578
  44.6 1.3 %collective-permute-start.4 = (f32[128,256]{1,0:T(8,128)S(1)}, f32[128,256]{1,0:T(8,128)S(1)}, u32[]{:S(2)}, u32[]{:S(2)}) collective-permute-start(f32[128,256]{1,0:T(8,128)S(1)} %get-tuple-element.47.refs_3_.refs_5_), channel_id=1, source_target_pairs={{1,0},{3,2},{5,4},{7,6},{9,8},{11,10},{13,12},{15,14},{17,16},{19,... | collective-permute-start | bytes 393224 | tf_op jit(solution)/shard_map/ppermute | solution.py:578
  45.9 1.3 %collective-permute-start.2 = (f32[128,128]{1,0:T(8,128)S(1)}, f32[128,128]{1,0:T(8,128)S(1)}, u32[]{:S(2)}, u32[]{:S(2)}) collective-permute-start(f32[128,128]{1,0:T(8,128)S(1)} %get-tuple-element.41.refs_2_.refs_4_), channel_id=1, source_target_pairs={{1,0},{3,2},{5,4},{7,6},{9,8},{11,10},{13,12},{15,14},{17,16},{19,... | collective-permute-start | bytes 196616 | tf_op jit(solution)/shard_map/ppermute | solution.py:578
  47.2 0.3 collective-permute-done.10.refs_1_
  47.5 1.3 %collective-permute-start.11 = (f32[64,256]{1,0:T(8,128)S(1)}, f32[64,256]{1,0:T(8,128)S(1)}, u32[]{:S(2)}, u32[]{:S(2)}) collective-permute-start(f32[64,256]{1,0:T(8,128)S(1)} %get-tuple-element.63), channel_id=1, source_target_pairs={{1,0},{3,2},{5,4},{7,6},{9,8},{11,10},{13,12},{15,14},{17,16},{19,... | collective-permute-start | bytes 196616 | tf_op jit(solution)/shard_map/ppermute | solution.py:578
  48.8 6.9 %collective-permute-done.2.refs_0_ = f32[128,128]{1,0:T(8,128)S(1)} collective-permute-done((f32[128,128]{1,0:T(8,128)S(1)}, f32[128,128]{1,0:T(8,128)S(1)}, u32[]{:S(2)}, u32[]{:S(2)}) %collective-permute-start.2) | collective-permute-done | bytes 65568 | tf_op jit(solution)/shard_map/ppermute | solution.py:578
  55.7 0.1 shard_map.66
  55.8 6.0 %collective-permute-start.5 = (f32[2,64,256]{2,1,0:T(8,128)S(1)}, f32[2,64,256]{2,1,0:T(8,128)S(1)}, u32[]{:S(2)}, u32[]{:S(2)}) collective-permute-start(f32[2,64,256]{2,1,0:T(8,128)S(1)} %shard_map.66), channel_id=1, source_target_pairs={{2,4},{4,2},{6,8},{8,6},{10,12},{12,10},{14,16},{16,14},{18,20},{2... | collective-permute-start | bytes 393224 | tf_op jit(solution)/shard_map/ppermute | solution.py:589
  61.8 0.2 shard_map.72
  62.0 0.1 collective-permute-start.12
  62.1 3.8 %collective-permute-done.5.halo_ref = f32[2,64,256]{2,1,0:T(8,128)S(1)} collective-permute-done((f32[2,64,256]{2,1,0:T(8,128)S(1)}, f32[2,64,256]{2,1,0:T(8,128)S(1)}, u32[]{:S(2)}, u32[]{:S(2)}) %collective-permute-start.5) | collective-permute-done | bytes 131104 | tf_op jit(solution)/shard_map/ppermute | solution.py:589
  65.8 1.0 %shard_map.69.base_ref = f32[4,64,512]{2,1,0:T(8,128)S(1)} custom-call(s32[4,16]{1,0:T(4,128)S(1)} %bitcast.5, f32[1,4,64,512]{3,2,1,0:T(8,128)S(1)} %copy-done.2, f32[2,64,256]{2,1,0:T(8,128)S(1)} %collective-permute-done.5.halo_ref, f32[128,128]{1,0:T(8,128)S(1)} %collective-permute-done.2.refs_0_, f32[128,256]{1,0:T(8,128)S(1)} %collective-permute-done.4.refs_1_, ...), custom_call_target="tpu_custom_call" | custom-call | tf_op jit(solution)/shard_map/pallas_call | solution.py:527
  66.9 0.9 %shard_map.71 = (f32[4,64,512]{2,1,0:T(8,128)S(1)}, f32[2,4,8,128]{3,2,1,0:T(8,128)S(1)}) custom-call(s32[4,16]{1,0:T(4,128)S(1)} %bitcast.6, f32[4,64,512]{2,1,0:T(8,128)S(1)} %shard_map.69.base_ref, f32[64,256]{1,0:T(8,128)S(1)} %collective-permute-done.11.refs_0_.refs_2_, f32[64,512]{1,0:T(8,128)S(1)} %widen.1.refs_1_.refs_5_), custom_call_target="tpu_custom_call" | custom-call | tf_op jit(solution)/shard_map/pallas_call | solution.py:527
  67.8 1.0 %shard_map.73 = f32[4,64,512]{2,1,0:T(8,128)} custom-call(f32[4,64,512]{2,1,0:T(8,128)S(1)} %get-tuple-element.67.base_ref, f32[2,64,256]{2,1,0:T(8,128)S(1)} %collective-permute-done.12.halo_ref, f32[2,4,8,128]{3,2,1,0:T(8,128)S(1)} %get-tuple-element.68.weight_ref), custom_call_target="tpu_custom_call" | custom-call | tf_op jit(solution)/shard_map/pallas_call | solution.py:527
  (21 shorter events, 0.1 us)
Async XLA Ops:
  0.0 3.2 %copy-start.3 = (s32[16,4]{0,1:T(4,128)S(1)}, s32[16,4]{0,1:T(4,128)}, u32[]{:S(2)}) copy-start(s32[16,4]{0,1:T(4,128)} %param.11) | copy-start | bytes 772
  0.0 3.2 %copy-start.5 = (s32[1,4,3]{1,0,2:T(1,128)S(1)}, s32[1,4,3]{1,0,2:T(1,128)}, u32[]{:S(2)}) copy-start(s32[1,4,3]{1,0,2:T(1,128)} %param.8) | copy-start | bytes 148
  1.7 14.0 %collective-permute-start = (f32[512,256]{1,0:T(8,128)S(1)}, f32[512,256]{1,0:T(8,128)S(1)}, u32[]{:S(2)}, u32[]{:S(2)}) collective-permute-start(f32[512,256]{1,0:T(8,128)S(1)} %early.1), channel_id=1, source_target_pairs={{0,1},{2,3},{4,5},{6,7},{8,9},{10,11},{12,13},{14,15},{16,17},{18,... | collective-permute-start | bytes 1572872 | tf_op jit(solution)/shard_map/ppermute | solution.py:561
  3.2 11.8 %copy-start.1 = (f32[1,4,256,256]{3,2,1,0:T(8,128)S(1)}, f32[1,4,256,256]{3,2,1,0:T(8,128)}, u32[]{:S(2)}) copy-start(f32[1,4,256,256]{3,2,1,0:T(8,128)} %inv_hbm.5) | copy-start | bytes 3145732
  3.2 11.8 %copy-start.4 = (f32[1,4,3,256,256]{4,3,2,1,0:T(8,128)S(1)}, f32[1,4,3,256,256]{4,3,2,1,0:T(8,128)}, u32[]{:S(2)}) copy-start(f32[1,4,3,256,256]{4,3,2,1,0:T(8,128)} %f_hbm.3) | copy-start | bytes 9437188
  9.6 16.4 %collective-permute-start.1 = (f32[128,768]{1,0:T(8,128)S(1)}, f32[128,768]{1,0:T(8,128)S(1)}, u32[]{:S(2)}, u32[]{:S(2)}) collective-permute-start(f32[128,768]{1,0:T(8,128)S(1)} %get-tuple-element.37.refs_3_), channel_id=1, source_target_pairs={{0,1},{2,3},{4,5},{6,7},{8,9},{10,11},{12,13},{14,15},{16,17},{18,... | collective-permute-start | bytes 1179656 | tf_op jit(solution)/shard_map/ppermute | solution.py:561
  10.9 19.7 %collective-permute-start.3 = (f32[128,768]{1,0:T(8,128)S(1)}, f32[128,768]{1,0:T(8,128)S(1)}, u32[]{:S(2)}, u32[]{:S(2)}) collective-permute-start(f32[128,768]{1,0:T(8,128)S(1)} %get-tuple-element.42.refs_3_), channel_id=1, source_target_pairs={{0,1},{2,3},{4,5},{6,7},{8,9},{10,11},{12,13},{14,15},{16,17},{18,... | collective-permute-start | bytes 1179656 | tf_op jit(solution)/shard_map/ppermute | solution.py:561
  12.3 26.8 %collective-permute-start.6 = (f32[128,768]{1,0:T(8,128)S(1)}, f32[128,768]{1,0:T(8,128)S(1)}, u32[]{:S(2)}, u32[]{:S(2)}) collective-permute-start(f32[128,768]{1,0:T(8,128)S(1)} %get-tuple-element.48.refs_3_), channel_id=1, source_target_pairs={{0,1},{2,3},{4,5},{6,7},{8,9},{10,11},{12,13},{14,15},{16,17},{18,... | collective-permute-start | bytes 1179656 | tf_op jit(solution)/shard_map/ppermute | solution.py:561
  13.6 12.4 %copy-start = (f32[512,256]{1,0:T(8,128)S(1)}, f32[512,256]{1,0:T(8,128)}, u32[]{:S(2)}) copy-start(f32[512,256]{1,0:T(8,128)} %get-tuple-element.38.refs_2_) | copy-start | bytes 1572868
  13.6 29.7 %collective-permute-start.8 = (f32[64,768]{1,0:T(8,128)S(1)}, f32[64,768]{1,0:T(8,128)S(1)}, u32[]{:S(2)}, u32[]{:S(2)}) collective-permute-start(f32[64,768]{1,0:T(8,128)S(1)} %get-tuple-element.54.refs_3_), channel_id=1, source_target_pairs={{0,1},{2,3},{4,5},{6,7},{8,9},{10,11},{12,13},{14,15},{16,17},{18,... | collective-permute-start | bytes 589832 | tf_op jit(solution)/shard_map/ppermute | solution.py:561
  15.7 31.8 %collective-permute-start.10 = (f32[64,768]{1,0:T(8,128)S(1)}, f32[64,768]{1,0:T(8,128)S(1)}, u32[]{:S(2)}, u32[]{:S(2)}) collective-permute-start(f32[64,768]{1,0:T(8,128)S(1)} %get-tuple-element.60.refs_3_), channel_id=1, source_target_pairs={{0,1},{2,3},{4,5},{6,7},{8,9},{10,11},{12,13},{14,15},{16,17},{18,... | collective-permute-start | bytes 589832 | tf_op jit(solution)/shard_map/ppermute | solution.py:561
  39.1 22.8 %collective-permute-start.7 = (f32[128,384]{1,0:T(8,128)S(1)}, f32[128,384]{1,0:T(8,128)S(1)}, u32[]{:S(2)}, u32[]{:S(2)}) collective-permute-start(f32[128,384]{1,0:T(8,128)S(1)} %get-tuple-element.53.refs_6_.refs_3_), channel_id=1, source_target_pairs={{1,0},{3,2},{5,4},{7,6},{9,8},{11,10},{13,12},{15,14},{17,16},{19,... | collective-permute-start | bytes 589832 | tf_op jit(solution)/shard_map/ppermute | solution.py:578
  43.3 18.5 %collective-permute-start.9 = (f32[64,448]{1,0:T(8,128)S(1)}, f32[64,448]{1,0:T(8,128)S(1)}, u32[]{:S(2)}, u32[]{:S(2)}) collective-permute-start(f32[64,448]{1,0:T(8,128)S(1)} %get-tuple-element.59.refs_7_.refs_4_), channel_id=1, source_target_pairs={{1,0},{3,2},{5,4},{7,6},{9,8},{11,10},{13,12},{15,14},{17,16},{19,... | collective-permute-start | bytes 344072 | tf_op jit(solution)/shard_map/ppermute | solution.py:578
  44.6 11.1 %collective-permute-start.4 = (f32[128,256]{1,0:T(8,128)S(1)}, f32[128,256]{1,0:T(8,128)S(1)}, u32[]{:S(2)}, u32[]{:S(2)}) collective-permute-start(f32[128,256]{1,0:T(8,128)S(1)} %get-tuple-element.47.refs_3_.refs_5_), channel_id=1, source_target_pairs={{1,0},{3,2},{5,4},{7,6},{9,8},{11,10},{13,12},{15,14},{17,16},{19,... | collective-permute-start | bytes 393224 | tf_op jit(solution)/shard_map/ppermute | solution.py:578
  45.9 9.8 %collective-permute-start.2 = (f32[128,128]{1,0:T(8,128)S(1)}, f32[128,128]{1,0:T(8,128)S(1)}, u32[]{:S(2)}, u32[]{:S(2)}) collective-permute-start(f32[128,128]{1,0:T(8,128)S(1)} %get-tuple-element.41.refs_2_.refs_4_), channel_id=1, source_target_pairs={{1,0},{3,2},{5,4},{7,6},{9,8},{11,10},{13,12},{15,14},{17,16},{19,... | collective-permute-start | bytes 196616 | tf_op jit(solution)/shard_map/ppermute | solution.py:578
  47.5 14.3 %collective-permute-start.11 = (f32[64,256]{1,0:T(8,128)S(1)}, f32[64,256]{1,0:T(8,128)S(1)}, u32[]{:S(2)}, u32[]{:S(2)}) collective-permute-start(f32[64,256]{1,0:T(8,128)S(1)} %get-tuple-element.63), channel_id=1, source_target_pairs={{1,0},{3,2},{5,4},{7,6},{9,8},{11,10},{13,12},{15,14},{17,16},{19,... | collective-permute-start | bytes 196616 | tf_op jit(solution)/shard_map/ppermute | solution.py:578
  48.8 17.1 %copy-start.2 = (f32[1,4,64,512]{3,2,1,0:T(8,128)S(1)}, f32[1,4,64,512]{3,2,1,0:T(8,128)}, u32[]{:S(2)}) copy-start(f32[1,4,64,512]{3,2,1,0:T(8,128)} %face_ref.1) | copy-start | bytes 1572868
  55.8 10.1 %collective-permute-start.5 = (f32[2,64,256]{2,1,0:T(8,128)S(1)}, f32[2,64,256]{2,1,0:T(8,128)S(1)}, u32[]{:S(2)}, u32[]{:S(2)}) collective-permute-start(f32[2,64,256]{2,1,0:T(8,128)S(1)} %shard_map.66), channel_id=1, source_target_pairs={{2,4},{4,2},{6,8},{8,6},{10,12},{12,10},{14,16},{16,14},{18,20},{2... | collective-permute-start | bytes 393224 | tf_op jit(solution)/shard_map/ppermute | solution.py:589
  62.0 5.8 %collective-permute-start.12 = (f32[2,64,256]{2,1,0:T(8,128)S(1)}, f32[2,64,256]{2,1,0:T(8,128)S(1)}, u32[]{:S(2)}, u32[]{:S(2)}) collective-permute-start(f32[2,64,256]{2,1,0:T(8,128)S(1)} %shard_map.72), channel_id=1, source_target_pairs={{0,2},{2,0},{4,6},{6,4},{8,10},{10,8},{12,14},{14,12},{16,18},{18,... | collective-permute-start | bytes 393224 | tf_op jit(solution)/shard_map/ppermute | solution.py:594
